TPU v7x, 128 devices: a whole 4x4x4 slice. The times are simulated.
128 devices in a mesh: wide: 32 (over z, x, core), head: 4 (over y).
Axes of the slice: x: 4, y: 4, z: 4, core: 2. Of those that a mesh axis runs over, the one named last changes fastest.
Arguments:
- queries: bfloat16 [16384, 8192], P(('wide', 'head')), may hold values from -6 to 6
- keys: bfloat16 [16384, 1024], P(('wide', 'head')), may hold values from -6 to 6
- values: bfloat16 [16384, 1024], P(('wide', 'head')), may hold values from -6 to 6
- out_rows: bfloat16 [16384, 8192], P(('wide', 'head')), may hold values from -3 to 3
- output_gradient: bfloat16 [16384, 8192], P(('wide', 'head')), may hold values from -3 to 3
- log_norm_rows: float32 [16384, 64], P(('wide', 'head')), may hold values from 4 to 8
- doc_lengths: int32 [16], replicated, may hold values from 1 to 1792, 16384 in all
Outputs:
- q_grad: float32 [16384, 8192], P(('wide', 'head'))
- key_gradient: float32 [16384, 1024], P(('wide', 'head'))
- value_gradient: float32 [16384, 1024], P(('wide', 'head'))
Inputs may be any that keep to these rules, and one draw needn't show every extreme that they name: `doc_lengths`: 16 document lengths in order; they sum to 16384.
All inputs are finite; a program needn't handle non-finite values.
Results may differ from a plain program's by a relative error of at most 0.0058.
Values may be sent and summed in bfloat16 or wider, within the bound.
No kernel may reach another device: no remote copies, remote signals or barrier semaphores. Data moves between devices by JAX's collectives and lax.ppermute only.
A program may use at most 128 MiB of HBM per device.

v0:
```python
import math

import jax
import jax.numpy as jnp
from jax import lax
from jax.experimental import pallas as pl
from jax.experimental.pallas import tpu as pltpu
from jax.sharding import Mesh, PartitionSpec as P


LOG2E = math.log2(math.e)
HEAD = 128
ROWS = 128
MEMBERS = 8
GROUP = MEMBERS * ROWS
FAR_BLOCKS = 14
FAR = FAR_BLOCKS * ROWS
FAR2 = FAR - GROUP
WINDOW = FAR + GROUP
HEADS = 8
CHUNKS = 2
H = HEADS // CHUNKS
WIDTH = H * HEAD
STATS = 2 * H
TQ = 256
TK = 256
NT = (((1,), (1,)), ((), ()))
TN = (((0,), (0,)), ((), ()))

SMEM = pl.BlockSpec(memory_space=pltpu.SMEM)
VMEM = pl.BlockSpec(memory_space=pltpu.VMEM)
ANY = pl.BlockSpec(memory_space=pl.ANY)
BIG = pltpu.CompilerParams(vmem_limit_bytes=56 << 20)


def kv_pack(keys, values):
    def kernel(k_ref, v_ref, out_ref):
        for b in range(MEMBERS):
            out_ref[b, :, 0:HEAD] = k_ref[:, b * HEAD : (b + 1) * HEAD]
            out_ref[b, :, HEAD : 2 * HEAD] = v_ref[:, b * HEAD : (b + 1) * HEAD]

    return pl.pallas_call(
        kernel,
        in_specs=[VMEM, VMEM],
        out_specs=VMEM,
        out_shape=jax.ShapeDtypeStruct((MEMBERS, ROWS, 2 * HEAD), jnp.bfloat16),
        name="kv_pack",
    )(keys, values)


def split_terms(value):
    high = value.astype(jnp.bfloat16)
    rest = value - high.astype(jnp.float32)
    middle = rest.astype(jnp.bfloat16)
    low = (rest - middle.astype(jnp.float32)).astype(jnp.bfloat16)
    return high, middle, low


def rows_pack(queries, grads, outs, norms, chunk):
    def kernel(q_ref, g_ref, o_ref, n_ref, out_ref, packed, forward, arrived, sent):
        def inbound(b):
            cut = pl.ds((b * CHUNKS + chunk) * WIDTH, WIDTH)
            return (
                pltpu.make_async_copy(
                    q_ref.at[:, cut], packed.at[b, pl.ds(0, ROWS), pl.ds(0, WIDTH)], arrived.at[0, b]
                ),
                pltpu.make_async_copy(
                    g_ref.at[:, cut],
                    packed.at[b, pl.ds(0, ROWS), pl.ds(WIDTH, WIDTH)],
                    arrived.at[1, b],
                ),
                pltpu.make_async_copy(o_ref.at[:, cut], forward.at[b], arrived.at[2, b]),
            )

        for b in range(MEMBERS):
            for copy in inbound(b):
                copy.start()
        lane = lax.broadcasted_iota(jnp.int32, (ROWS, 128), 1)
        for b in range(MEMBERS):
            for copy in inbound(b):
                copy.wait()
            deltas = jnp.zeros((ROWS, 128), jnp.float32)
            for h in range(H):
                cut = slice(h * HEAD, (h + 1) * HEAD)
                grad = packed[b, 0:ROWS, WIDTH + h * HEAD : WIDTH + (h + 1) * HEAD]
                product = grad.astype(jnp.float32) * forward[b, :, cut].astype(jnp.float32)
                deltas = jnp.where(lane == h, jnp.sum(product, axis=1, keepdims=True), deltas)
            first = b * HEADS + chunk * H
            stats = jnp.concatenate([n_ref[first : first + H], deltas.T[0:H]], axis=0)
            high, middle, low = split_terms(stats)
            packed[b, ROWS : ROWS + STATS, 0:ROWS] = high
            packed[b, ROWS : ROWS + STATS, ROWS : 2 * ROWS] = middle
            packed[b, ROWS : ROWS + STATS, 2 * ROWS : 3 * ROWS] = low
            packed[b, ROWS : ROWS + STATS, 3 * ROWS :] = jnp.zeros(
                (STATS, 2 * WIDTH - 3 * ROWS), jnp.bfloat16
            )
            pltpu.make_async_copy(packed.at[b], out_ref.at[b], sent.at[b]).start()
        for b in range(MEMBERS):
            pltpu.make_async_copy(packed.at[b], out_ref.at[b], sent.at[b]).wait()

    shape = (MEMBERS, ROWS + STATS, 2 * WIDTH)
    return pl.pallas_call(
        kernel,
        in_specs=[ANY, ANY, ANY, VMEM],
        out_specs=ANY,
        out_shape=jax.ShapeDtypeStruct(shape, jnp.bfloat16),
        scratch_shapes=[
            pltpu.VMEM(shape, jnp.bfloat16),
            pltpu.VMEM((MEMBERS, ROWS, WIDTH), jnp.bfloat16),
            pltpu.SemaphoreType.DMA((3, MEMBERS)),
            pltpu.SemaphoreType.DMA((MEMBERS,)),
        ],
        compiler_params=BIG,
        name="rows_pack",
    )(queries, grads, outs, norms)


def relay(block):
    def kernel(block_ref, out_ref, copied):
        copy = pltpu.make_async_copy(block_ref.at[pl.ds(GROUP - FAR2, FAR2)], out_ref, copied)
        copy.start()
        copy.wait()

    return pl.pallas_call(
        kernel,
        in_specs=[ANY],
        out_specs=ANY,
        out_shape=jax.ShapeDtypeStruct((FAR2, 2 * HEAD), jnp.bfloat16),
        scratch_shapes=[pltpu.SemaphoreType.DMA],
        name="relay",
    )(block)


def attention(doc_lengths, first_token, rows, far2, far1, near, earlier, chunk):
    scaling = 1.0 / math.sqrt(HEAD)
    docs = doc_lengths.shape[0]
    parts = TQ // ROWS
    last = chunk == CHUNKS - 1
    q_at = chunk * WIDTH if last else 0

    def kernel(lengths_ref, first_ref, rows_ref, far2_ref, far1_ref, near_ref, *rest):
        if last:
            q_earlier, sums_ref, q_out, far2_out, far1_out, near_out, window, acc, q_acc = rest
        else:
            q_out, acc, window, q_acc = rest
        window[0:FAR2] = far2_ref[...]
        window[FAR2:FAR] = far1_ref[...]
        window[FAR:WINDOW] = near_ref[...]
        if last:
            acc[...] = sums_ref[...]
            q_out[:, :, 0 : chunk * WIDTH] = q_earlier[...]
        else:
            acc[...] = jnp.zeros_like(acc)
        group_first = first_ref[0]
        window_first = group_first - FAR

        def query_tile(tile, carry):
            token = group_first + tile * TQ
            position = token + lax.broadcasted_iota(jnp.int32, (8, TQ), 1)
            start = jnp.int32(0)
            doc_first = start
            doc_start = jnp.zeros((8, TQ), jnp.int32)
            for doc in range(1, docs):
                start = start + lengths_ref[doc - 1]
                doc_first = jnp.where(start <= token, start, doc_first)
                doc_start = jnp.where(start <= position, start, doc_start)
            low = doc_start[0:1] - window_first
            reach = position[0:1] - doc_start[0:1]
            key_begin = (doc_first - window_first) // TK
            key_end = (token + TQ - 1 - window_first) // TK + 1
            block = tile * parts
            pairs = [(h, s) for h in range(H) for s in range(parts)]
            query = jnp.concatenate(
                [rows_ref[block + s, 0:ROWS, h * HEAD : (h + 1) * HEAD] for h, s in pairs], axis=0
            )
            grad = jnp.concatenate(
                [rows_ref[block + s, 0:ROWS, WIDTH + h * HEAD : WIDTH + (h + 1) * HEAD] for h, s in pairs],
                axis=0,
            )
            stats = [
                sum(
                    rows_ref[block + s, ROWS : ROWS + STATS, t * ROWS : (t + 1) * ROWS].astype(
                        jnp.float32
                    )
                    for t in (2, 1, 0)
                )
                for s in range(parts)
            ]
            norm = LOG2E * jnp.concatenate([stats[s][h : h + 1] for h, s in pairs], axis=1)
            delta = jnp.concatenate([stats[s][H + h : H + h + 1] for h, s in pairs], axis=1)
            q_acc[...] = jnp.zeros_like(q_acc)

            def key_tile(index, inner):
                row = pl.multiple_of(index * TK, TK)
                k_rows = window[pl.ds(row, TK), 0:HEAD]
                v_rows = window[pl.ds(row, TK), HEAD : 2 * HEAD]
                offset = row + lax.broadcasted_iota(jnp.int32, (TK, TQ), 0) - low
                allowed = (offset >= 0) & (offset <= reach)
                allowed = jnp.concatenate([allowed] * H, axis=1)
                scores = lax.dot_general(k_rows, query, NT, preferred_element_type=jnp.float32)
                attend = jnp.where(allowed, jnp.exp2(scores * (scaling * LOG2E) - norm), 0.0)
                prob_grad = lax.dot_general(v_rows, grad, NT, preferred_element_type=jnp.float32)
                score_low = (attend * (prob_grad - delta)).astype(jnp.bfloat16)
                attend_low = attend.astype(jnp.bfloat16)
                acc[pl.ds(row, TK), HEAD : 2 * HEAD] += jnp.dot(
                    attend_low, grad, preferred_element_type=jnp.float32
                )
                acc[pl.ds(row, TK), 0:HEAD] += jnp.dot(
                    score_low, query, preferred_element_type=jnp.float32
                )
                q_acc[...] += lax.dot_general(
                    score_low, k_rows, TN, preferred_element_type=jnp.float32
                )
                return inner

            lax.fori_loop(key_begin, key_end, key_tile, 0)
            for at_row, (h, s) in enumerate(pairs):
                part = q_acc[at_row * ROWS : (at_row + 1) * ROWS, :] * scaling
                q_out[block + s, :, q_at + h * HEAD : q_at + (h + 1) * HEAD] = part.astype(
                    jnp.bfloat16
                )
            return carry

        lax.fori_loop(0, GROUP // TQ, query_tile, 0)
        if last:
            for ref, begin, end in (
                (far2_out, 0, FAR2),
                (far1_out, FAR2, FAR),
                (near_out, FAR, WINDOW),
            ):
                ref[:, 0:HEAD] = (acc[begin:end, 0:HEAD] * scaling).astype(ref.dtype)
                ref[:, HEAD : 2 * HEAD] = acc[begin:end, HEAD : 2 * HEAD].astype(ref.dtype)

    pair = 2 * HEAD
    q_shape = jax.ShapeDtypeStruct((MEMBERS, ROWS, q_at + WIDTH), jnp.bfloat16)
    acc_shape = (WINDOW, pair)
    window_scratch = pltpu.VMEM((WINDOW, pair), jnp.bfloat16)
    q_scratch = pltpu.VMEM((H * TQ, HEAD), jnp.float32)
    if last:
        out_shape = [
            q_shape,
            jax.ShapeDtypeStruct((FAR2, pair), jnp.bfloat16),
            jax.ShapeDtypeStruct((GROUP, pair), jnp.bfloat16),
            jax.ShapeDtypeStruct((GROUP, pair), jnp.float32),
        ]
        scratch = [window_scratch, pltpu.VMEM(acc_shape, jnp.float32), q_scratch]
    else:
        out_shape = [q_shape, jax.ShapeDtypeStruct(acc_shape, jnp.float32)]
        scratch = [window_scratch, q_scratch]
    operands = [doc_lengths, first_token, rows, far2, far1, near, *earlier]
    return pl.pallas_call(
        kernel,
        in_specs=[SMEM, SMEM] + [VMEM] * (len(operands) - 2),
        out_specs=[VMEM] * len(out_shape),
        out_shape=out_shape,
        scratch_shapes=scratch,
        compiler_params=BIG,
    )(*operands)


def kv_sum(near, back1, back2):
    def kernel(near_ref, back1_ref, back2_ref, out_ref):
        for b in range(MEMBERS):
            cut = slice(b * ROWS, (b + 1) * ROWS)
            total = near_ref[cut] + back1_ref[cut].astype(jnp.float32)
            skip = (GROUP - FAR2) // ROWS
            if b >= skip:
                far = slice((b - skip) * ROWS, (b - skip + 1) * ROWS)
                total = total + back2_ref[far].astype(jnp.float32)
            out_ref[b] = total.astype(jnp.bfloat16)

    return pl.pallas_call(
        kernel,
        in_specs=[VMEM] * 3,
        out_specs=VMEM,
        out_shape=jax.ShapeDtypeStruct((MEMBERS, ROWS, 2 * HEAD), jnp.bfloat16),
        name="kv_sum",
    )(near, back1, back2)


def q_unpack(blocks):
    width = HEADS * HEAD

    def kernel(in_ref, out_ref, narrow, wide, arrived, sent):
        def inbound(b):
            return pltpu.make_async_copy(in_ref.at[b], narrow.at[b], arrived.at[b])

        def outbound(b):
            return pltpu.make_async_copy(
                wide.at[b], out_ref.at[:, pl.ds(b * width, width)], sent.at[b]
            )

        for b in range(MEMBERS):
            inbound(b).start()
        for b in range(MEMBERS):
            inbound(b).wait()
            wide[b] = narrow[b].astype(jnp.float32)
            outbound(b).start()
        for b in range(MEMBERS):
            outbound(b).wait()

    shape = (MEMBERS, ROWS, width)
    return pl.pallas_call(
        kernel,
        in_specs=[ANY],
        out_specs=ANY,
        out_shape=jax.ShapeDtypeStruct((ROWS, MEMBERS * width), jnp.float32),
        scratch_shapes=[
            pltpu.VMEM(shape, jnp.bfloat16),
            pltpu.VMEM(shape, jnp.float32),
            pltpu.SemaphoreType.DMA((MEMBERS,)),
            pltpu.SemaphoreType.DMA((MEMBERS,)),
        ],
        compiler_params=BIG,
        name="q_unpack",
    )(blocks)


def kv_unpack(both):
    def kernel(both_ref, k_ref, v_ref):
        for b in range(MEMBERS):
            k_ref[:, b * HEAD : (b + 1) * HEAD] = both_ref[b, :, 0:HEAD].astype(jnp.float32)
            v_ref[:, b * HEAD : (b + 1) * HEAD] = both_ref[b, :, HEAD:].astype(jnp.float32)

    shape = jax.ShapeDtypeStruct((ROWS, MEMBERS * HEAD), jnp.float32)
    return pl.pallas_call(
        kernel,
        in_specs=[VMEM],
        out_specs=[VMEM, VMEM],
        out_shape=[shape, shape],
        name="kv_unpack",
    )(both)


def exchange(blocks):
    return lax.all_to_all(blocks, ("core", "head"), split_axis=0, concat_axis=0, tiled=True)


def shifted(block, by):
    count = lax.axis_size("group")
    pairs = [(i, i + by) for i in range(count) if 0 <= i + by < count]
    return lax.ppermute(block, "group", pairs)


def on_device(queries, keys, values, out_rows, output_gradient, log_norm_rows, doc_lengths):
    near = exchange(kv_pack(keys, values)).reshape(GROUP, 2 * HEAD)
    norms = log_norm_rows.T
    rows = []
    for chunk in range(CHUNKS):
        packed = rows_pack(queries, output_gradient, out_rows, norms, chunk)
        rows.append(exchange(packed))
    far1 = shifted(near, 1)
    relayed = relay(far1)
    far2 = shifted(relayed, 1)
    first_token = (lax.axis_index("group") * GROUP).astype(jnp.int32).reshape(1)
    results = []
    for chunk in range(CHUNKS):
        results = attention(doc_lengths, first_token, rows[chunk], far2, far1, near, results, chunk)
    q_all, far2_sum, far1_sum, near_sum = results
    back1 = shifted(far1_sum, -1)
    back2 = shifted(far2_sum, -2)
    q_back = exchange(q_all)
    both = exchange(kv_sum(near_sum, back1, back2))
    q_grad = q_unpack(q_back)
    key_gradient, value_gradient = kv_unpack(both)
    return (q_grad, key_gradient, value_gradient)


def solution(mesh):
    wide, head = mesh.shape["wide"], mesh.shape["head"]
    cores = MEMBERS // head
    finer = Mesh(mesh.devices.reshape(wide // cores, cores, head), ("group", "core", "head"))
    split = P(("group", "core", "head"), None)
    return jax.shard_map(
        on_device,
        mesh=finer,
        in_specs=(split,) * 6 + (P(),),
        out_specs=(split, split, split),
        check_vma=False,
    )
```

profile of v0, /device:TPU:7, one launch (start us, length us, event | category | flops | bytes accessed | tf_op | source)
XLA Modules:
  0.0 236.2 jit_solution(14928725650160091495)
XLA Ops:
  0.6 1.9 kv_pack.1
  2.5 5.1 %all-to-all-start.1 = ((bf16[8,128,256]{2,1,0:T(8,128)(2,1)}), bf16[8,128,256]{2,1,0:T(8,128)(2,1)S(1)}, u32[]{:S(2)}, u32[]{:S(2)}) async-start(bf16[8,128,256]{2,1,0:T(8,128)(2,1)} %kv_pack.1), calls=%async_computation.1 | async-start | bytes 1048576 | tf_op jit(solution)/shard_map/all_to_all | solution.py:336
  7.7 4.3 %rows_pack.3 = bf16[8,136,1024]{2,1,0:T(8,128)(2,1)} custom-call(bf16[128,8192]{1,0:T(8,128)(2,1)} %q_ref.3, bf16[128,8192]{1,0:T(8,128)(2,1)} %g_ref.3, bf16[128,8192]{1,0:T(8,128)(2,1)} %o_ref.3, f32[64,128]{1,0:T(8,128)} %bitcast.6), custom_call_target="tpu_custom_call" | custom-call | tf_op jit(solution)/shard_map/rows_pack/pallas_call | solution.py:102
  12.0 5.0 %all-to-all-done.1 = bf16[8,128,256]{2,1,0:T(8,128)(2,1)S(1)} async-done(((bf16[8,128,256]{2,1,0:T(8,128)(2,1)}), bf16[8,128,256]{2,1,0:T(8,128)(2,1)S(1)}, u32[]{:S(2)}, u32[]{:S(2)}) %all-to-all-start.1) | async-done | bytes 524320 | tf_op jit(solution)/shard_map/all_to_all | solution.py:336
  17.0 3.8 %all-to-all-start.2 = ((bf16[8,136,1024]{2,1,0:T(8,128)(2,1)}), bf16[8,136,1024]{2,1,0:T(8,128)(2,1)S(1)}, u32[]{:S(2)}, u32[]{:S(2)}) async-start(bf16[8,136,1024]{2,1,0:T(8,128)(2,1)} %rows_pack.3), calls=%async_computation.2 | async-start | bytes 4456448 | tf_op jit(solution)/shard_map/all_to_all | solution.py:336
  20.9 4.3 %rows_pack.2 = bf16[8,136,1024]{2,1,0:T(8,128)(2,1)} custom-call(bf16[128,8192]{1,0:T(8,128)(2,1)} %q_ref.3, bf16[128,8192]{1,0:T(8,128)(2,1)} %g_ref.3, bf16[128,8192]{1,0:T(8,128)(2,1)} %o_ref.3, f32[64,128]{1,0:T(8,128)} %bitcast.7), custom_call_target="tpu_custom_call" | custom-call | tf_op jit(solution)/shard_map/rows_pack/pallas_call | solution.py:102
  25.2 23.3 %all-to-all-done.2.rows_ref = bf16[8,136,1024]{2,1,0:T(8,128)(2,1)S(1)} async-done(((bf16[8,136,1024]{2,1,0:T(8,128)(2,1)}), bf16[8,136,1024]{2,1,0:T(8,128)(2,1)S(1)}, u32[]{:S(2)}, u32[]{:S(2)}) %all-to-all-start.2) | async-done | bytes 2228256 | tf_op jit(solution)/shard_map/all_to_all | solution.py:336
  49.8 3.8 %all-to-all-start = ((bf16[8,136,1024]{2,1,0:T(8,128)(2,1)}), bf16[8,136,1024]{2,1,0:T(8,128)(2,1)S(1)}, u32[]{:S(2)}, u32[]{:S(2)}) async-start(bf16[8,136,1024]{2,1,0:T(8,128)(2,1)} %rows_pack.2), calls=%async_computation | async-start | bytes 4456448 | tf_op jit(solution)/shard_map/all_to_all | solution.py:336
  53.7 3.4 %collective-permute-start = (bf16[1024,256]{1,0:T(8,128)(2,1)S(1)}, bf16[1024,256]{1,0:T(8,128)(2,1)S(1)}, u32[]{:S(2)}, u32[]{:S(2)}) collective-permute-start(bf16[1024,256]{1,0:T(8,128)(2,1)S(1)} %bitcast.3), channel_id=1, source_target_pairs={{0,8},{8,16},{16,24},{24,32},{32,40},{40,48},{48,56},{56,64},{64,7... | collective-permute-start | bytes 1572872 | tf_op jit(solution)/shard_map/ppermute | solution.py:342
  57.1 11.8 %collective-permute-done.block_ref.far1_ref = bf16[1024,256]{1,0:T(8,128)(2,1)S(1)} collective-permute-done((bf16[1024,256]{1,0:T(8,128)(2,1)S(1)}, bf16[1024,256]{1,0:T(8,128)(2,1)S(1)}, u32[]{:S(2)}, u32[]{:S(2)}) %collective-permute-start) | collective-permute-done | bytes 524320 | tf_op jit(solution)/shard_map/ppermute | solution.py:342
  69.7 13.0 %relay.1 = bf16[768,256]{1,0:T(8,128)(2,1)} custom-call(bf16[1024,256]{1,0:T(8,128)(2,1)} %copy-done.3), custom_call_target="tpu_custom_call" | custom-call | tf_op jit(solution)/shard_map/relay/pallas_call | solution.py:124
  82.8 5.6 %collective-permute-start.1 = (bf16[768,256]{1,0:T(8,128)(2,1)}, bf16[768,256]{1,0:T(8,128)(2,1)S(1)}, u32[]{:S(2)}, u32[]{:S(2)}) collective-permute-start(bf16[768,256]{1,0:T(8,128)(2,1)} %relay.1), channel_id=1, source_target_pairs={{0,8},{8,16},{16,24},{24,32},{32,40},{40,48},{48,56},{56,64},{64,7... | collective-permute-start | bytes 1179656 | tf_op jit(solution)/shard_map/ppermute | solution.py:342
  88.3 7.8 %collective-permute-done.1.far2_ref = bf16[768,256]{1,0:T(8,128)(2,1)S(1)} collective-permute-done((bf16[768,256]{1,0:T(8,128)(2,1)}, bf16[768,256]{1,0:T(8,128)(2,1)S(1)}, u32[]{:S(2)}, u32[]{:S(2)}) %collective-permute-start.1) | collective-permute-done | bytes 393248 | tf_op jit(solution)/shard_map/ppermute | solution.py:342
  96.9 29.1 %shard_map.94 = (bf16[8,128,512]{2,1,0:T(8,128)(2,1)}, f32[2816,256]{1,0:T(8,128)}) custom-call(s32[16]{0:T(128)} %lengths_ref.3, s32[1]{0:T(128)} %bitcast.first_ref, bf16[8,136,1024]{2,1,0:T(8,128)(2,1)} %copy-done.1, bf16[768,256]{1,0:T(8,128)(2,1)} %copy-done.5, bf16[1024,256]{1,0:T(8,128)(2,1)} %copy-done.3, bf16[1024,256]{1,0:T(8,128)(2,1)} %bitcast.4), custom_call_target="tpu_custom_call" | custom-call | tf_op jit(solution)/shard_map/pallas_call | solution.py:251
  127.4 30.7 %shard_map.95 = (bf16[8,128,1024]{2,1,0:T(8,128)(2,1)}, bf16[768,256]{1,0:T(8,128)(2,1)}, bf16[1024,256]{1,0:T(8,128)(2,1)}, f32[1024,256]{1,0:T(8,128)}) custom-call(s32[16]{0:T(128)} %lengths_ref.3, s32[1]{0:T(128)} %bitcast.first_ref, bf16[8,136,1024]{2,1,0:T(8,128)(2,1)} %copy-done, bf16[768,256]{1,0:T(8,128)(2,1)} %copy-done.5, ...), custom_call_target="tpu_custom_call" | custom-call | tf_op jit(solution)/shard_map/pallas_call | solution.py:251
  160.0 1.9 collective-permute-start.3
  161.9 16.5 %collective-permute-done.3.back2_ref = bf16[768,256]{1,0:T(8,128)(2,1)S(1)} collective-permute-done((bf16[768,256]{1,0:T(8,128)(2,1)}, bf16[768,256]{1,0:T(8,128)(2,1)S(1)}, u32[]{:S(2)}, u32[]{:S(2)}) %collective-permute-start.3) | collective-permute-done | bytes 393248 | tf_op jit(solution)/shard_map/ppermute | solution.py:342
  178.4 3.9 %collective-permute-done.2.back1_ref = bf16[1024,256]{1,0:T(8,128)(2,1)S(1)} collective-permute-done((bf16[1024,256]{1,0:T(8,128)(2,1)}, bf16[1024,256]{1,0:T(8,128)(2,1)S(1)}, u32[]{:S(2)}, u32[]{:S(2)}) %collective-permute-start.2) | collective-permute-done | bytes 524320 | tf_op jit(solution)/shard_map/ppermute | solution.py:342
  183.1 2.4 %kv_sum.1 = bf16[8,128,256]{2,1,0:T(8,128)(2,1)} custom-call(f32[1024,256]{1,0:T(8,128)} %get-tuple-element.14.near_ref, bf16[1024,256]{1,0:T(8,128)(2,1)} %copy-done.6, bf16[768,256]{1,0:T(8,128)(2,1)} %copy-done.7), custom_call_target="tpu_custom_call" | custom-call | tf_op jit(solution)/shard_map/kv_sum/pallas_call | solution.py:272
  185.5 16.1 %all_to_all.25.both_ref = bf16[8,128,256]{2,1,0:T(8,128)(2,1)} all-to-all(bf16[8,128,256]{2,1,0:T(8,128)(2,1)} %kv_sum.1), channel_id=1, replica_groups=mesh['group'=16,'core'=2,'head'=4] {'core','head'}, dimensions={0} | all-to-all | bytes 1048576 | tf_op jit(solution)/shard_map/all_to_all | solution.py:336
  201.7 3.9 %all-to-all-start.3 = ((bf16[8,128,1024]{2,1,0:T(8,128)(2,1)}), bf16[8,128,1024]{2,1,0:T(8,128)(2,1)S(1)}, u32[]{:S(2)}, u32[]{:S(2)}) async-start(bf16[8,128,1024]{2,1,0:T(8,128)(2,1)} %get-tuple-element.13), calls=%async_computation.3 | async-start | bytes 4194304 | tf_op jit(solution)/shard_map/all_to_all | solution.py:336
  205.5 2.1 kv_unpack.1
  207.7 24.1 %all-to-all-done.3.in_ref = bf16[8,128,1024]{2,1,0:T(8,128)(2,1)S(1)} async-done(((bf16[8,128,1024]{2,1,0:T(8,128)(2,1)}), bf16[8,128,1024]{2,1,0:T(8,128)(2,1)S(1)}, u32[]{:S(2)}, u32[]{:S(2)}) %all-to-all-start.3) | async-done | bytes 2097184 | tf_op jit(solution)/shard_map/all_to_all | solution.py:336
  233.1 3.1 %q_unpack.1 = f32[128,8192]{1,0:T(8,128)} custom-call(bf16[8,128,1024]{2,1,0:T(8,128)(2,1)} %copy-done.2), custom_call_target="tpu_custom_call" | custom-call | tf_op jit(solution)/shard_map/q_unpack/pallas_call | solution.py:303
  (18 shorter events, 8.3 us)
Async XLA Ops:
  2.5 14.5 %all-to-all-start.1 = ((bf16[8,128,256]{2,1,0:T(8,128)(2,1)}), bf16[8,128,256]{2,1,0:T(8,128)(2,1)S(1)}, u32[]{:S(2)}, u32[]{:S(2)}) async-start(bf16[8,128,256]{2,1,0:T(8,128)(2,1)} %kv_pack.1), calls=%async_computation.1 | async-start | bytes 1048576 | tf_op jit(solution)/shard_map/all_to_all | solution.py:336
  17.0 36.7 %copy-start.4 = (bf16[8,128,256]{2,1,0:T(8,128)(2,1)}, bf16[8,128,256]{2,1,0:T(8,128)(2,1)S(1)}, u32[]{:S(2)}) copy-start(bf16[8,128,256]{2,1,0:T(8,128)(2,1)S(1)} %all-to-all-done.1) | copy-start | bytes 1572868
  17.0 31.4 %all-to-all-start.2 = ((bf16[8,136,1024]{2,1,0:T(8,128)(2,1)}), bf16[8,136,1024]{2,1,0:T(8,128)(2,1)S(1)}, u32[]{:S(2)}, u32[]{:S(2)}) async-start(bf16[8,136,1024]{2,1,0:T(8,128)(2,1)} %rows_pack.3), calls=%async_computation.2 | async-start | bytes 4456448 | tf_op jit(solution)/shard_map/all_to_all | solution.py:336
  48.5 1.4 copy-start.1
  49.8 76.1 %all-to-all-start = ((bf16[8,136,1024]{2,1,0:T(8,128)(2,1)}), bf16[8,136,1024]{2,1,0:T(8,128)(2,1)S(1)}, u32[]{:S(2)}, u32[]{:S(2)}) async-start(bf16[8,136,1024]{2,1,0:T(8,128)(2,1)} %rows_pack.2), calls=%async_computation | async-start | bytes 4456448 | tf_op jit(solution)/shard_map/all_to_all | solution.py:336
  53.7 15.3 %collective-permute-start = (bf16[1024,256]{1,0:T(8,128)(2,1)S(1)}, bf16[1024,256]{1,0:T(8,128)(2,1)S(1)}, u32[]{:S(2)}, u32[]{:S(2)}) collective-permute-start(bf16[1024,256]{1,0:T(8,128)(2,1)S(1)} %bitcast.3), channel_id=1, source_target_pairs={{0,8},{8,16},{16,24},{24,32},{32,40},{40,48},{48,56},{56,64},{64,7... | collective-permute-start | bytes 1572872 | tf_op jit(solution)/shard_map/ppermute | solution.py:342
  68.9 0.8 copy-start.3
  82.8 13.4 %collective-permute-start.1 = (bf16[768,256]{1,0:T(8,128)(2,1)}, bf16[768,256]{1,0:T(8,128)(2,1)S(1)}, u32[]{:S(2)}, u32[]{:S(2)}) collective-permute-start(bf16[768,256]{1,0:T(8,128)(2,1)} %relay.1), channel_id=1, source_target_pairs={{0,8},{8,16},{16,24},{24,32},{32,40},{40,48},{48,56},{56,64},{64,7... | collective-permute-start | bytes 1179656 | tf_op jit(solution)/shard_map/ppermute | solution.py:342
  96.1 0.8 copy-start.5
  126.0 1.4 copy-start
  158.0 24.3 %collective-permute-start.2 = (bf16[1024,256]{1,0:T(8,128)(2,1)}, bf16[1024,256]{1,0:T(8,128)(2,1)S(1)}, u32[]{:S(2)}, u32[]{:S(2)}) collective-permute-start(bf16[1024,256]{1,0:T(8,128)(2,1)} %get-tuple-element.15), channel_id=1, source_target_pairs={{8,0},{16,8},{24,16},{32,24},{40,32},{48,40},{56,48},{64,56},{72,6... | collective-permute-start | bytes 1572872 | tf_op jit(solution)/shard_map/ppermute | solution.py:342
  160.0 18.5 %collective-permute-start.3 = (bf16[768,256]{1,0:T(8,128)(2,1)}, bf16[768,256]{1,0:T(8,128)(2,1)S(1)}, u32[]{:S(2)}, u32[]{:S(2)}) collective-permute-start(bf16[768,256]{1,0:T(8,128)(2,1)} %get-tuple-element.16), channel_id=1, source_target_pairs={{16,0},{24,8},{32,16},{40,24},{48,32},{56,40},{64,48},{72,56},{80,... | collective-permute-start | bytes 1179656 | tf_op jit(solution)/shard_map/ppermute | solution.py:342
  178.4 3.9 %copy-start.7 = (bf16[768,256]{1,0:T(8,128)(2,1)}, bf16[768,256]{1,0:T(8,128)(2,1)S(1)}, u32[]{:S(2)}) copy-start(bf16[768,256]{1,0:T(8,128)(2,1)S(1)} %collective-permute-done.3.back2_ref) | copy-start | bytes 1179652
  182.3 0.8 copy-start.6
  201.7 30.1 %all-to-all-start.3 = ((bf16[8,128,1024]{2,1,0:T(8,128)(2,1)}), bf16[8,128,1024]{2,1,0:T(8,128)(2,1)S(1)}, u32[]{:S(2)}, u32[]{:S(2)}) async-start(bf16[8,128,1024]{2,1,0:T(8,128)(2,1)} %get-tuple-element.13), calls=%async_computation.3 | async-start | bytes 4194304 | tf_op jit(solution)/shard_map/all_to_all | solution.py:336
  231.7 1.3 copy-start.2
where the time goes:
time: 237 us; the launch traced here: 236 us
  waiting for transfers between devices  92.4 us (39%)
  Pallas kernels  91 us (38%)
  starting transfers between devices  29.5 us (12%)
  blocking collectives  16.1 us (7%)
  local copies, waits for them, and re-layouts  6.43 us (3%)
    pallas_call x2, Pallas kernels, attention(): pl.pallas_call(kernel, in_specs=[SMEM, SMEM] + [VMEM] * (len(operands) -...  59.7 us
    all_to_all x4, waiting for transfers between devices, exchange(): lax.all_to_all(blocks, ('core', 'head'), split_axis=0, concat_axis=0, til...  52.4 us
    ppermute x4, waiting for transfers between devices, shifted(): return lax.ppermute(block, 'group', pairs)  40.1 us
    all_to_all x4, starting transfers between devices, exchange(): lax.all_to_all(blocks, ('core', 'head'), split_axis=0, concat_axis=0, til...  16.7 us
    all_to_all x1, blocking collectives, exchange(): lax.all_to_all(blocks, ('core', 'head'), split_axis=0, concat_axis=0, til...  16.1 us
    pallas_call x1, Pallas kernels, relay(): pl.pallas_call(kernel, in_specs=[ANY], out_specs=ANY, out_shape=jax.Shape...  13 us
    ppermute x4, starting transfers between devices, shifted(): return lax.ppermute(block, 'group', pairs)  12.8 us
    pallas_call x2, Pallas kernels, rows_pack(): pl.pallas_call(kernel, in_specs=[ANY, ANY, ANY, VMEM], out_specs=ANY, out...  8.66 us
  transfers between devices with their start and end apart: 8, of which 7 were waited for; matrix products, arithmetic and copies ran while one was open for 0% of the time, Pallas kernels for 22%

commit v1 on v0

--- a/solution.py
+++ b/solution.py
@@ -116,17 +116,14 @@
 
 
 def relay(block):
-    def kernel(block_ref, out_ref, copied):
-        copy = pltpu.make_async_copy(block_ref.at[pl.ds(GROUP - FAR2, FAR2)], out_ref, copied)
-        copy.start()
-        copy.wait()
-
-    return pl.pallas_call(
-        kernel,
-        in_specs=[ANY],
-        out_specs=ANY,
+    def kernel(block_ref, out_ref):
+        out_ref[...] = block_ref[GROUP - FAR2 :]
+
+    return pl.pallas_call(
+        kernel,
+        in_specs=[VMEM],
+        out_specs=VMEM,
         out_shape=jax.ShapeDtypeStruct((FAR2, 2 * HEAD), jnp.bfloat16),
-        scratch_shapes=[pltpu.SemaphoreType.DMA],
         name="relay",
     )(block)
 
@@ -136,11 +133,10 @@
     docs = doc_lengths.shape[0]
     parts = TQ // ROWS
     last = chunk == CHUNKS - 1
-    q_at = chunk * WIDTH if last else 0
 
     def kernel(lengths_ref, first_ref, rows_ref, far2_ref, far1_ref, near_ref, *rest):
         if last:
-            q_earlier, sums_ref, q_out, far2_out, far1_out, near_out, window, acc, q_acc = rest
+            sums_ref, q_out, far2_out, far1_out, near_out, window, acc, q_acc = rest
         else:
             q_out, acc, window, q_acc = rest
         window[0:FAR2] = far2_ref[...]
@@ -148,7 +144,6 @@
         window[FAR:WINDOW] = near_ref[...]
         if last:
             acc[...] = sums_ref[...]
-            q_out[:, :, 0 : chunk * WIDTH] = q_earlier[...]
         else:
             acc[...] = jnp.zeros_like(acc)
         group_first = first_ref[0]
@@ -216,9 +211,7 @@
             lax.fori_loop(key_begin, key_end, key_tile, 0)
             for at_row, (h, s) in enumerate(pairs):
                 part = q_acc[at_row * ROWS : (at_row + 1) * ROWS, :] * scaling
-                q_out[block + s, :, q_at + h * HEAD : q_at + (h + 1) * HEAD] = part.astype(
-                    jnp.bfloat16
-                )
+                q_out[block + s, :, h * HEAD : (h + 1) * HEAD] = part.astype(jnp.bfloat16)
             return carry
 
         lax.fori_loop(0, GROUP // TQ, query_tile, 0)
@@ -232,7 +225,7 @@
                 ref[:, HEAD : 2 * HEAD] = acc[begin:end, HEAD : 2 * HEAD].astype(ref.dtype)
 
     pair = 2 * HEAD
-    q_shape = jax.ShapeDtypeStruct((MEMBERS, ROWS, q_at + WIDTH), jnp.bfloat16)
+    q_shape = jax.ShapeDtypeStruct((MEMBERS, ROWS, WIDTH), jnp.bfloat16)
     acc_shape = (WINDOW, pair)
     window_scratch = pltpu.VMEM((WINDOW, pair), jnp.bfloat16)
     q_scratch = pltpu.VMEM((H * TQ, HEAD), jnp.float32)
@@ -278,42 +271,46 @@
     )(near, back1, back2)
 
 
-def q_unpack(blocks):
-    width = HEADS * HEAD
-
-    def kernel(in_ref, out_ref, narrow, wide, arrived, sent):
-        def inbound(b):
-            return pltpu.make_async_copy(in_ref.at[b], narrow.at[b], arrived.at[b])
-
-        def outbound(b):
+def q_unpack(parts):
+    def kernel(*refs):
+        sources, (out_ref, narrow, wide, arrived, sent) = refs[:CHUNKS], refs[CHUNKS:]
+        pieces = [(chunk, b) for chunk in range(CHUNKS) for b in range(MEMBERS)]
+
+        def inbound(chunk, b):
             return pltpu.make_async_copy(
-                wide.at[b], out_ref.at[:, pl.ds(b * width, width)], sent.at[b]
-            )
-
-        for b in range(MEMBERS):
-            inbound(b).start()
-        for b in range(MEMBERS):
-            inbound(b).wait()
-            wide[b] = narrow[b].astype(jnp.float32)
-            outbound(b).start()
-        for b in range(MEMBERS):
-            outbound(b).wait()
-
-    shape = (MEMBERS, ROWS, width)
-    return pl.pallas_call(
-        kernel,
-        in_specs=[ANY],
+                sources[chunk].at[b], narrow.at[chunk, b], arrived.at[chunk, b]
+            )
+
+        def outbound(chunk, b):
+            cut = pl.ds((b * CHUNKS + chunk) * WIDTH, WIDTH)
+            return pltpu.make_async_copy(
+                wide.at[chunk, b], out_ref.at[:, cut], sent.at[chunk, b]
+            )
+
+        for piece in pieces:
+            inbound(*piece).start()
+        for chunk, b in pieces:
+            inbound(chunk, b).wait()
+            wide[chunk, b] = narrow[chunk, b].astype(jnp.float32)
+            outbound(chunk, b).start()
+        for piece in pieces:
+            outbound(*piece).wait()
+
+    shape = (CHUNKS, MEMBERS, ROWS, WIDTH)
+    return pl.pallas_call(
+        kernel,
+        in_specs=[ANY] * CHUNKS,
         out_specs=ANY,
-        out_shape=jax.ShapeDtypeStruct((ROWS, MEMBERS * width), jnp.float32),
+        out_shape=jax.ShapeDtypeStruct((ROWS, MEMBERS * CHUNKS * WIDTH), jnp.float32),
         scratch_shapes=[
             pltpu.VMEM(shape, jnp.bfloat16),
             pltpu.VMEM(shape, jnp.float32),
-            pltpu.SemaphoreType.DMA((MEMBERS,)),
-            pltpu.SemaphoreType.DMA((MEMBERS,)),
+            pltpu.SemaphoreType.DMA((CHUNKS, MEMBERS)),
+            pltpu.SemaphoreType.DMA((CHUNKS, MEMBERS)),
         ],
         compiler_params=BIG,
         name="q_unpack",
-    )(blocks)
+    )(*parts)
 
 
 def kv_unpack(both):
@@ -353,13 +350,15 @@
     relayed = relay(far1)
     far2 = shifted(relayed, 1)
     first_token = (lax.axis_index("group") * GROUP).astype(jnp.int32).reshape(1)
-    results = []
+    sums, q_back = [], []
     for chunk in range(CHUNKS):
-        results = attention(doc_lengths, first_token, rows[chunk], far2, far1, near, results, chunk)
-    q_all, far2_sum, far1_sum, near_sum = results
+        q_part, *sums = attention(
+            doc_lengths, first_token, rows[chunk], far2, far1, near, sums, chunk
+        )
+        q_back.append(exchange(q_part))
+    far2_sum, far1_sum, near_sum = sums
     back1 = shifted(far1_sum, -1)
     back2 = shifted(far2_sum, -2)
-    q_back = exchange(q_all)
     both = exchange(kv_sum(near_sum, back1, back2))
     q_grad = q_unpack(q_back)
     key_gradient, value_gradient = kv_unpack(both)

time: 237 us -> 204 us (0.86)
  waiting for transfers between devices: 92.4 us -> 76.3 us
  blocking collectives: 16.1 us -> 0 us
  starting transfers between devices: 29.5 us -> 42.4 us
  Pallas kernels: 91 us -> 79.1 us
    all_to_all x4 -> x6, waiting for transfers between devices: 52.4 us -> 34.4 us  [exchange(): lax.all_to_all(blocks, ('core', 'head'), split_axis=0, concat_axis=0, til...]
    all_to_all x1 -> x0, blocking collectives: 16.1 us -> none  [exchange(): lax.all_to_all(blocks, ('core', 'head'), split_axis=0, concat_axis=0, til...]
    all_to_all x4 -> x6, starting transfers between devices: 16.7 us -> 29.7 us  [exchange(): lax.all_to_all(blocks, ('core', 'head'), split_axis=0, concat_axis=0, til...]
    pallas_call x2, Pallas kernels: 16.1 us -> 5.01 us  [the longest x1 3.19 us: q_unpack(): pl.pallas_call(kernel, in_specs=[ANY] * CHUNKS, out_specs=ANY, out_shape=...]
    unnamed x16 -> x18, local copies, waits for them, and re-layouts: 6.43 us -> 4.61 us
  transfers between devices with their start and end apart: 8 -> 10, of which waited for: 7 -> 7; matrix products, arithmetic and copies ran while one was open for 0% -> 0% of each run, Pallas kernels for 22% -> 37%
where the time goes in v1:
time: 204 us; the launch traced here: 203 us
  Pallas kernels  79.1 us (39%)
  waiting for transfers between devices  76.3 us (37%)
  starting transfers between devices  42.4 us (21%)
  local copies, waits for them, and re-layouts  4.61 us (2%)
    pallas_call x2, Pallas kernels, attention(): pl.pallas_call(kernel, in_specs=[SMEM, SMEM] + [VMEM] * (len(operands) -...  59 us
    ppermute x4, waiting for transfers between devices, shifted(): return lax.ppermute(block, 'group', pairs)  41.9 us
    all_to_all x6, waiting for transfers between devices, exchange(): lax.all_to_all(blocks, ('core', 'head'), split_axis=0, concat_axis=0, til...  34.4 us
    all_to_all x6, starting transfers between devices, exchange(): lax.all_to_all(blocks, ('core', 'head'), split_axis=0, concat_axis=0, til...  29.7 us
    ppermute x4, starting transfers between devices, shifted(): return lax.ppermute(block, 'group', pairs)  12.7 us
    pallas_call x2, Pallas kernels, rows_pack(): pl.pallas_call(kernel, in_specs=[ANY, ANY, ANY, VMEM], out_specs=ANY, out...  8.66 us
    unnamed x18, local copies, waits for them, and re-layouts  4.61 us
  transfers between devices with their start and end apart: 10, of which 7 were waited for; matrix products, arithmetic and copies ran while one was open for 0% of the time, Pallas kernels for 37%

profile of v1, /device:TPU:7, one launch (start us, length us, event | category | flops | bytes accessed | tf_op | source)
XLA Modules:
  0.0 203.1 jit_solution(14216660852652131752)
XLA Ops:
  0.6 1.9 kv_pack.1
  2.5 5.1 %all-to-all-start.1 = ((bf16[8,128,256]{2,1,0:T(8,128)(2,1)}), bf16[8,128,256]{2,1,0:T(8,128)(2,1)S(1)}, u32[]{:S(2)}, u32[]{:S(2)}) async-start(bf16[8,128,256]{2,1,0:T(8,128)(2,1)} %kv_pack.1), calls=%async_computation.1 | async-start | bytes 1048576 | tf_op jit(solution)/shard_map/all_to_all | solution.py:333
  7.7 4.3 %rows_pack.2 = bf16[8,136,1024]{2,1,0:T(8,128)(2,1)} custom-call(bf16[128,8192]{1,0:T(8,128)(2,1)} %q_ref.3, bf16[128,8192]{1,0:T(8,128)(2,1)} %g_ref.3, bf16[128,8192]{1,0:T(8,128)(2,1)} %o_ref.3, f32[64,128]{1,0:T(8,128)} %bitcast.6), custom_call_target="tpu_custom_call" | custom-call | tf_op jit(solution)/shard_map/rows_pack/pallas_call | solution.py:102
  12.0 5.0 %all-to-all-done.1 = bf16[8,128,256]{2,1,0:T(8,128)(2,1)S(1)} async-done(((bf16[8,128,256]{2,1,0:T(8,128)(2,1)}), bf16[8,128,256]{2,1,0:T(8,128)(2,1)S(1)}, u32[]{:S(2)}, u32[]{:S(2)}) %all-to-all-start.1) | async-done | bytes 524320 | tf_op jit(solution)/shard_map/all_to_all | solution.py:333
  17.0 3.8 %all-to-all-start = ((bf16[8,136,1024]{2,1,0:T(8,128)(2,1)}), bf16[8,136,1024]{2,1,0:T(8,128)(2,1)S(1)}, u32[]{:S(2)}, u32[]{:S(2)}) async-start(bf16[8,136,1024]{2,1,0:T(8,128)(2,1)} %rows_pack.2), calls=%async_computation | async-start | bytes 4456448 | tf_op jit(solution)/shard_map/all_to_all | solution.py:333
  20.9 4.3 %rows_pack.3 = bf16[8,136,1024]{2,1,0:T(8,128)(2,1)} custom-call(bf16[128,8192]{1,0:T(8,128)(2,1)} %q_ref.3, bf16[128,8192]{1,0:T(8,128)(2,1)} %g_ref.3, bf16[128,8192]{1,0:T(8,128)(2,1)} %o_ref.3, f32[64,128]{1,0:T(8,128)} %bitcast.7), custom_call_target="tpu_custom_call" | custom-call | tf_op jit(solution)/shard_map/rows_pack/pallas_call | solution.py:102
  25.2 23.3 %all-to-all-done.rows_ref = bf16[8,136,1024]{2,1,0:T(8,128)(2,1)S(1)} async-done(((bf16[8,136,1024]{2,1,0:T(8,128)(2,1)}), bf16[8,136,1024]{2,1,0:T(8,128)(2,1)S(1)}, u32[]{:S(2)}, u32[]{:S(2)}) %all-to-all-start) | async-done | bytes 2228256 | tf_op jit(solution)/shard_map/all_to_all | solution.py:333
  49.9 4.6 %all-to-all-start.3 = ((bf16[8,136,1024]{2,1,0:T(8,128)(2,1)}), bf16[8,136,1024]{2,1,0:T(8,128)(2,1)}, u32[]{:S(2)}, u32[]{:S(2)}) async-start(bf16[8,136,1024]{2,1,0:T(8,128)(2,1)} %rows_pack.3), calls=%async_computation.3 | async-start | bytes 4456448 | tf_op jit(solution)/shard_map/all_to_all | solution.py:333
  54.4 3.4 %collective-permute-start = (bf16[1024,256]{1,0:T(8,128)(2,1)S(1)}, bf16[1024,256]{1,0:T(8,128)(2,1)S(1)}, u32[]{:S(2)}, u32[]{:S(2)}) collective-permute-start(bf16[1024,256]{1,0:T(8,128)(2,1)S(1)} %bitcast.3), channel_id=1, source_target_pairs={{0,8},{8,16},{16,24},{24,32},{32,40},{40,48},{48,56},{56,64},{64,7... | collective-permute-start | bytes 1572872 | tf_op jit(solution)/shard_map/ppermute | solution.py:339
  57.9 11.9 %collective-permute-done.block_ref.far1_ref = bf16[1024,256]{1,0:T(8,128)(2,1)S(1)} collective-permute-done((bf16[1024,256]{1,0:T(8,128)(2,1)S(1)}, bf16[1024,256]{1,0:T(8,128)(2,1)S(1)}, u32[]{:S(2)}, u32[]{:S(2)}) %collective-permute-start) | collective-permute-done | bytes 524320 | tf_op jit(solution)/shard_map/ppermute | solution.py:339
  72.4 5.5 %collective-permute-start.1 = (bf16[768,256]{1,0:T(8,128)(2,1)}, bf16[768,256]{1,0:T(8,128)(2,1)S(1)}, u32[]{:S(2)}, u32[]{:S(2)}) collective-permute-start(bf16[768,256]{1,0:T(8,128)(2,1)} %relay.1), channel_id=1, source_target_pairs={{0,8},{8,16},{16,24},{24,32},{32,40},{40,48},{48,56},{56,64},{64,7... | collective-permute-start | bytes 1179656 | tf_op jit(solution)/shard_map/ppermute | solution.py:339
  77.8 7.8 %collective-permute-done.1.far2_ref = bf16[768,256]{1,0:T(8,128)(2,1)S(1)} collective-permute-done((bf16[768,256]{1,0:T(8,128)(2,1)}, bf16[768,256]{1,0:T(8,128)(2,1)S(1)}, u32[]{:S(2)}, u32[]{:S(2)}) %collective-permute-start.1) | collective-permute-done | bytes 393248 | tf_op jit(solution)/shard_map/ppermute | solution.py:339
  86.4 29.1 %shard_map.94 = (bf16[8,128,512]{2,1,0:T(8,128)(2,1)}, f32[2816,256]{1,0:T(8,128)}) custom-call(s32[16]{0:T(128)} %lengths_ref.3, s32[1]{0:T(128)} %bitcast.first_ref, bf16[8,136,1024]{2,1,0:T(8,128)(2,1)} %copy-done, bf16[768,256]{1,0:T(8,128)(2,1)} %copy-done.6, bf16[1024,256]{1,0:T(8,128)(2,1)} %copy-done.1, bf16[1024,256]{1,0:T(8,128)(2,1)} %bitcast.4), custom_call_target="tpu_custom_call" | custom-call | tf_op jit(solution)/shard_map/pallas_call | solution.py:244
  115.5 6.0 %all-to-all-start.2 = ((bf16[8,128,512]{2,1,0:T(8,128)(2,1)}), bf16[8,128,512]{2,1,0:T(8,128)(2,1)S(1)}, u32[]{:S(2)}, u32[]{:S(2)}) async-start(bf16[8,128,512]{2,1,0:T(8,128)(2,1)} %get-tuple-element.11), calls=%async_computation.2 | async-start | bytes 2097152 | tf_op jit(solution)/shard_map/all_to_all | solution.py:333
  121.5 29.9 %shard_map.95 = (bf16[8,128,512]{2,1,0:T(8,128)(2,1)}, bf16[768,256]{1,0:T(8,128)(2,1)}, bf16[1024,256]{1,0:T(8,128)(2,1)}, f32[1024,256]{1,0:T(8,128)}) custom-call(s32[16]{0:T(128)} %lengths_ref.3, s32[1]{0:T(128)} %bitcast.first_ref, bf16[8,136,1024]{2,1,0:T(8,128)(2,1)} %all-to-all-done.3.rows_ref, bf16[768,256]{1,0:T(8,128)(2,1)} %copy-done.6, ...), custom_call_target="tpu_custom_call" | custom-call | tf_op jit(solution)/shard_map/pallas_call | solution.py:244
  151.4 4.8 %all-to-all-start.4 = ((bf16[8,128,512]{2,1,0:T(8,128)(2,1)}), bf16[8,128,512]{2,1,0:T(8,128)(2,1)S(1)}, u32[]{:S(2)}, u32[]{:S(2)}) async-start(bf16[8,128,512]{2,1,0:T(8,128)(2,1)} %get-tuple-element.13), calls=%async_computation.4 | async-start | bytes 2097152 | tf_op jit(solution)/shard_map/all_to_all | solution.py:333
  158.2 1.9 collective-permute-start.3
  160.1 18.3 %collective-permute-done.3.back2_ref = bf16[768,256]{1,0:T(8,128)(2,1)S(1)} collective-permute-done((bf16[768,256]{1,0:T(8,128)(2,1)}, bf16[768,256]{1,0:T(8,128)(2,1)S(1)}, u32[]{:S(2)}, u32[]{:S(2)}) %collective-permute-start.3) | collective-permute-done | bytes 393248 | tf_op jit(solution)/shard_map/ppermute | solution.py:339
  178.5 3.9 %collective-permute-done.2.back1_ref = bf16[1024,256]{1,0:T(8,128)(2,1)S(1)} collective-permute-done((bf16[1024,256]{1,0:T(8,128)(2,1)}, bf16[1024,256]{1,0:T(8,128)(2,1)S(1)}, u32[]{:S(2)}, u32[]{:S(2)}) %collective-permute-start.2) | collective-permute-done | bytes 524320 | tf_op jit(solution)/shard_map/ppermute | solution.py:339
  183.2 2.4 %kv_sum.1 = bf16[8,128,256]{2,1,0:T(8,128)(2,1)} custom-call(f32[1024,256]{1,0:T(8,128)} %get-tuple-element.14.near_ref, bf16[1024,256]{1,0:T(8,128)(2,1)} %copy-done.7, bf16[768,256]{1,0:T(8,128)(2,1)} %copy-done.8), custom_call_target="tpu_custom_call" | custom-call | tf_op jit(solution)/shard_map/kv_sum/pallas_call | solution.py:265
  185.6 5.3 %all-to-all-start.5 = ((bf16[8,128,256]{2,1,0:T(8,128)(2,1)}), bf16[8,128,256]{2,1,0:T(8,128)(2,1)S(1)}, u32[]{:S(2)}, u32[]{:S(2)}) async-start(bf16[8,128,256]{2,1,0:T(8,128)(2,1)} %kv_sum.1), calls=%async_computation.5 | async-start | bytes 1048576 | tf_op jit(solution)/shard_map/all_to_all | solution.py:333
  190.9 3.2 %q_unpack.1 = f32[128,8192]{1,0:T(8,128)} custom-call(bf16[8,128,512]{2,1,0:T(8,128)(2,1)} %copy-done.3, bf16[8,128,512]{2,1,0:T(8,128)(2,1)} %copy-done.4), custom_call_target="tpu_custom_call" | custom-call | tf_op jit(solution)/shard_map/q_unpack/pallas_call | solution.py:300
  194.1 6.1 %all-to-all-done.5.both_ref = bf16[8,128,256]{2,1,0:T(8,128)(2,1)S(1)} async-done(((bf16[8,128,256]{2,1,0:T(8,128)(2,1)}), bf16[8,128,256]{2,1,0:T(8,128)(2,1)S(1)}, u32[]{:S(2)}, u32[]{:S(2)}) %all-to-all-start.5) | async-done | bytes 524320 | tf_op jit(solution)/shard_map/all_to_all | solution.py:333
  201.0 2.1 %kv_unpack.1 = (f32[128,1024]{1,0:T(8,128)}, f32[128,1024]{1,0:T(8,128)}) custom-call(bf16[8,128,256]{2,1,0:T(8,128)(2,1)} %copy-done.5), custom_call_target="tpu_custom_call" | custom-call | tf_op jit(solution)/shard_map/kv_unpack/pallas_call | solution.py:323
  (23 shorter events, 8.3 us)
Async XLA Ops:
  2.5 14.5 %all-to-all-start.1 = ((bf16[8,128,256]{2,1,0:T(8,128)(2,1)}), bf16[8,128,256]{2,1,0:T(8,128)(2,1)S(1)}, u32[]{:S(2)}, u32[]{:S(2)}) async-start(bf16[8,128,256]{2,1,0:T(8,128)(2,1)} %kv_pack.1), calls=%async_computation.1 | async-start | bytes 1048576 | tf_op jit(solution)/shard_map/all_to_all | solution.py:333
  17.0 37.4 %copy-start.2 = (bf16[8,128,256]{2,1,0:T(8,128)(2,1)}, bf16[8,128,256]{2,1,0:T(8,128)(2,1)S(1)}, u32[]{:S(2)}) copy-start(bf16[8,128,256]{2,1,0:T(8,128)(2,1)S(1)} %all-to-all-done.1) | copy-start | bytes 1572868
  17.0 31.4 %all-to-all-start = ((bf16[8,136,1024]{2,1,0:T(8,128)(2,1)}), bf16[8,136,1024]{2,1,0:T(8,128)(2,1)S(1)}, u32[]{:S(2)}, u32[]{:S(2)}) async-start(bf16[8,136,1024]{2,1,0:T(8,128)(2,1)} %rows_pack.2), calls=%async_computation | async-start | bytes 4456448 | tf_op jit(solution)/shard_map/all_to_all | solution.py:333
  48.5 1.4 copy-start
  49.9 65.6 %all-to-all-start.3 = ((bf16[8,136,1024]{2,1,0:T(8,128)(2,1)}), bf16[8,136,1024]{2,1,0:T(8,128)(2,1)}, u32[]{:S(2)}, u32[]{:S(2)}) async-start(bf16[8,136,1024]{2,1,0:T(8,128)(2,1)} %rows_pack.3), calls=%async_computation.3 | async-start | bytes 4456448 | tf_op jit(solution)/shard_map/all_to_all | solution.py:333
  54.4 15.3 %collective-permute-start = (bf16[1024,256]{1,0:T(8,128)(2,1)S(1)}, bf16[1024,256]{1,0:T(8,128)(2,1)S(1)}, u32[]{:S(2)}, u32[]{:S(2)}) collective-permute-start(bf16[1024,256]{1,0:T(8,128)(2,1)S(1)} %bitcast.3), channel_id=1, source_target_pairs={{0,8},{8,16},{16,24},{24,32},{32,40},{40,48},{48,56},{56,64},{64,7... | collective-permute-start | bytes 1572872 | tf_op jit(solution)/shard_map/ppermute | solution.py:339
  69.8 0.8 copy-start.1
  72.4 13.2 %collective-permute-start.1 = (bf16[768,256]{1,0:T(8,128)(2,1)}, bf16[768,256]{1,0:T(8,128)(2,1)S(1)}, u32[]{:S(2)}, u32[]{:S(2)}) collective-permute-start(bf16[768,256]{1,0:T(8,128)(2,1)} %relay.1), channel_id=1, source_target_pairs={{0,8},{8,16},{16,24},{24,32},{32,40},{40,48},{48,56},{56,64},{64,7... | collective-permute-start | bytes 1179656 | tf_op jit(solution)/shard_map/ppermute | solution.py:339
  85.6 0.8 copy-start.6
  115.5 35.9 %all-to-all-start.2 = ((bf16[8,128,512]{2,1,0:T(8,128)(2,1)}), bf16[8,128,512]{2,1,0:T(8,128)(2,1)S(1)}, u32[]{:S(2)}, u32[]{:S(2)}) async-start(bf16[8,128,512]{2,1,0:T(8,128)(2,1)} %get-tuple-element.11), calls=%async_computation.2 | async-start | bytes 2097152 | tf_op jit(solution)/shard_map/all_to_all | solution.py:333
  151.4 34.1 %copy-start.3 = (bf16[8,128,512]{2,1,0:T(8,128)(2,1)}, bf16[8,128,512]{2,1,0:T(8,128)(2,1)S(1)}, u32[]{:S(2)}) copy-start(bf16[8,128,512]{2,1,0:T(8,128)(2,1)S(1)} %all-to-all-done.2.refs_0_) | copy-start | bytes 3145732
  151.4 34.1 %all-to-all-start.4 = ((bf16[8,128,512]{2,1,0:T(8,128)(2,1)}), bf16[8,128,512]{2,1,0:T(8,128)(2,1)S(1)}, u32[]{:S(2)}, u32[]{:S(2)}) async-start(bf16[8,128,512]{2,1,0:T(8,128)(2,1)} %get-tuple-element.13), calls=%async_computation.4 | async-start | bytes 2097152 | tf_op jit(solution)/shard_map/all_to_all | solution.py:333
  156.3 26.1 %collective-permute-start.2 = (bf16[1024,256]{1,0:T(8,128)(2,1)}, bf16[1024,256]{1,0:T(8,128)(2,1)S(1)}, u32[]{:S(2)}, u32[]{:S(2)}) collective-permute-start(bf16[1024,256]{1,0:T(8,128)(2,1)} %get-tuple-element.15), channel_id=1, source_target_pairs={{8,0},{16,8},{24,16},{32,24},{40,32},{48,40},{56,48},{64,56},{72,6... | collective-permute-start | bytes 1572872 | tf_op jit(solution)/shard_map/ppermute | solution.py:339
  158.2 20.3 %collective-permute-start.3 = (bf16[768,256]{1,0:T(8,128)(2,1)}, bf16[768,256]{1,0:T(8,128)(2,1)S(1)}, u32[]{:S(2)}, u32[]{:S(2)}) collective-permute-start(bf16[768,256]{1,0:T(8,128)(2,1)} %get-tuple-element.16), channel_id=1, source_target_pairs={{16,0},{24,8},{32,16},{40,24},{48,32},{56,40},{64,48},{72,56},{80,... | collective-permute-start | bytes 1179656 | tf_op jit(solution)/shard_map/ppermute | solution.py:339
  178.5 3.9 %copy-start.8 = (bf16[768,256]{1,0:T(8,128)(2,1)}, bf16[768,256]{1,0:T(8,128)(2,1)S(1)}, u32[]{:S(2)}) copy-start(bf16[768,256]{1,0:T(8,128)(2,1)S(1)} %collective-permute-done.3.back2_ref) | copy-start | bytes 1179652
  182.4 0.8 copy-start.7
  185.6 5.3 %copy-start.4 = (bf16[8,128,512]{2,1,0:T(8,128)(2,1)}, bf16[8,128,512]{2,1,0:T(8,128)(2,1)S(1)}, u32[]{:S(2)}) copy-start(bf16[8,128,512]{2,1,0:T(8,128)(2,1)S(1)} %all-to-all-done.4.refs_1_) | copy-start | bytes 3145732
  185.6 14.6 %all-to-all-start.5 = ((bf16[8,128,256]{2,1,0:T(8,128)(2,1)}), bf16[8,128,256]{2,1,0:T(8,128)(2,1)S(1)}, u32[]{:S(2)}, u32[]{:S(2)}) async-start(bf16[8,128,256]{2,1,0:T(8,128)(2,1)} %kv_sum.1), calls=%async_computation.5 | async-start | bytes 1048576 | tf_op jit(solution)/shard_map/all_to_all | solution.py:333
  200.2 0.8 copy-start.5

commit v2 on v1

--- a/solution.py
+++ b/solution.py
@@ -9,6 +9,7 @@
 
 
 LOG2E = math.log2(math.e)
+MASKED = -1e30
 HEAD = 128
 ROWS = 128
 MEMBERS = 8
@@ -134,18 +135,38 @@
     parts = TQ // ROWS
     last = chunk == CHUNKS - 1
 
-    def kernel(lengths_ref, first_ref, rows_ref, far2_ref, far1_ref, near_ref, *rest):
+    def kernel(lengths_ref, first_ref, rows_hbm, far2_ref, far1_ref, near_ref, *rest):
         if last:
-            sums_ref, q_out, far2_out, far1_out, near_out, window, acc, q_acc = rest
+            sums_ref, q_hbm, far2_out, far1_out, near_out, *scratch = rest
+            rows_ref, q_ref, window, acc, q_acc, row_sem, key_sem, q_sem, sums, sums_sem = scratch
+            sums_copy = pltpu.make_async_copy(sums_ref, sums, sums_sem)
         else:
-            q_out, acc, window, q_acc = rest
-        window[0:FAR2] = far2_ref[...]
-        window[FAR2:FAR] = far1_ref[...]
-        window[FAR:WINDOW] = near_ref[...]
+            q_hbm, sums_out, *scratch = rest
+            rows_ref, q_ref, window, acc, q_acc, row_sem, key_sem, q_sem = scratch
+
+        def rows_copy(tile):
+            cut = pl.ds(tile * parts, parts)
+            return pltpu.make_async_copy(rows_hbm.at[cut], rows_ref.at[cut], row_sem.at[tile])
+
+        def q_copy(tile):
+            cut = pl.ds(tile * parts, parts)
+            return pltpu.make_async_copy(q_ref.at[cut], q_hbm.at[cut], q_sem.at[tile])
+
+        key_copies = [
+            pltpu.make_async_copy(ref, window.at[pl.ds(begin, size)], key_sem.at[i])
+            for i, (ref, begin, size) in enumerate(
+                ((far2_ref, 0, FAR2), (far1_ref, FAR2, GROUP), (near_ref, FAR, GROUP))
+            )
+        ]
+        for copy in key_copies:
+            copy.start()
+        for tile in range(GROUP // TQ):
+            rows_copy(tile).start()
         if last:
-            acc[...] = sums_ref[...]
-        else:
-            acc[...] = jnp.zeros_like(acc)
+            sums_copy.start()
+        acc[...] = jnp.zeros_like(acc)
+        for copy in key_copies:
+            copy.wait()
         group_first = first_ref[0]
         window_first = group_first - FAR
 
@@ -164,6 +185,7 @@
             key_begin = (doc_first - window_first) // TK
             key_end = (token + TQ - 1 - window_first) // TK + 1
             block = tile * parts
+            rows_copy(tile).wait()
             pairs = [(h, s) for h in range(H) for s in range(parts)]
             query = jnp.concatenate(
                 [rows_ref[block + s, 0:ROWS, h * HEAD : (h + 1) * HEAD] for h, s in pairs], axis=0
@@ -191,9 +213,9 @@
                 v_rows = window[pl.ds(row, TK), HEAD : 2 * HEAD]
                 offset = row + lax.broadcasted_iota(jnp.int32, (TK, TQ), 0) - low
                 allowed = (offset >= 0) & (offset <= reach)
-                allowed = jnp.concatenate([allowed] * H, axis=1)
+                bias = jnp.concatenate([jnp.where(allowed, 0.0, MASKED)] * H, axis=1)
                 scores = lax.dot_general(k_rows, query, NT, preferred_element_type=jnp.float32)
-                attend = jnp.where(allowed, jnp.exp2(scores * (scaling * LOG2E) - norm), 0.0)
+                attend = jnp.exp2(scores * (scaling * LOG2E) - norm + bias)
                 prob_grad = lax.dot_general(v_rows, grad, NT, preferred_element_type=jnp.float32)
                 score_low = (attend * (prob_grad - delta)).astype(jnp.bfloat16)
                 attend_low = attend.astype(jnp.bfloat16)
@@ -211,24 +233,40 @@
             lax.fori_loop(key_begin, key_end, key_tile, 0)
             for at_row, (h, s) in enumerate(pairs):
                 part = q_acc[at_row * ROWS : (at_row + 1) * ROWS, :] * scaling
-                q_out[block + s, :, h * HEAD : (h + 1) * HEAD] = part.astype(jnp.bfloat16)
+                q_ref[block + s, :, h * HEAD : (h + 1) * HEAD] = part.astype(jnp.bfloat16)
+            q_copy(tile).start()
             return carry
 
         lax.fori_loop(0, GROUP // TQ, query_tile, 0)
         if last:
+            sums_copy.wait()
             for ref, begin, end in (
                 (far2_out, 0, FAR2),
                 (far1_out, FAR2, FAR),
                 (near_out, FAR, WINDOW),
             ):
-                ref[:, 0:HEAD] = (acc[begin:end, 0:HEAD] * scaling).astype(ref.dtype)
-                ref[:, HEAD : 2 * HEAD] = acc[begin:end, HEAD : 2 * HEAD].astype(ref.dtype)
+                total = acc[begin:end] + sums[begin:end]
+                ref[:, 0:HEAD] = (total[:, 0:HEAD] * scaling).astype(ref.dtype)
+                ref[:, HEAD : 2 * HEAD] = total[:, HEAD : 2 * HEAD].astype(ref.dtype)
+        else:
+            pltpu.sync_copy(acc, sums_out)
+        for tile in range(GROUP // TQ):
+            q_copy(tile).wait()
 
     pair = 2 * HEAD
     q_shape = jax.ShapeDtypeStruct((MEMBERS, ROWS, WIDTH), jnp.bfloat16)
     acc_shape = (WINDOW, pair)
-    window_scratch = pltpu.VMEM((WINDOW, pair), jnp.bfloat16)
-    q_scratch = pltpu.VMEM((H * TQ, HEAD), jnp.float32)
+    tiles = GROUP // TQ
+    scratch = [
+        pltpu.VMEM((MEMBERS, ROWS + STATS, 2 * WIDTH), jnp.bfloat16),
+        pltpu.VMEM(q_shape.shape, q_shape.dtype),
+        pltpu.VMEM((WINDOW, pair), jnp.bfloat16),
+        pltpu.VMEM(acc_shape, jnp.float32),
+        pltpu.VMEM((H * TQ, HEAD), jnp.float32),
+        pltpu.SemaphoreType.DMA((tiles,)),
+        pltpu.SemaphoreType.DMA((3,)),
+        pltpu.SemaphoreType.DMA((tiles,)),
+    ]
     if last:
         out_shape = [
             q_shape,
@@ -236,15 +274,16 @@
             jax.ShapeDtypeStruct((GROUP, pair), jnp.bfloat16),
             jax.ShapeDtypeStruct((GROUP, pair), jnp.float32),
         ]
-        scratch = [window_scratch, pltpu.VMEM(acc_shape, jnp.float32), q_scratch]
+        out_specs = [ANY, VMEM, VMEM, VMEM]
+        scratch += [pltpu.VMEM(acc_shape, jnp.float32), pltpu.SemaphoreType.DMA]
     else:
         out_shape = [q_shape, jax.ShapeDtypeStruct(acc_shape, jnp.float32)]
-        scratch = [window_scratch, q_scratch]
+        out_specs = [ANY, ANY]
     operands = [doc_lengths, first_token, rows, far2, far1, near, *earlier]
     return pl.pallas_call(
         kernel,
-        in_specs=[SMEM, SMEM] + [VMEM] * (len(operands) - 2),
-        out_specs=[VMEM] * len(out_shape),
+        in_specs=[SMEM, SMEM] + [ANY] * (len(operands) - 2),
+        out_specs=out_specs,
         out_shape=out_shape,
         scratch_shapes=scratch,
         compiler_params=BIG,
@@ -252,21 +291,50 @@
 
 
 def kv_sum(near, back1, back2):
-    def kernel(near_ref, back1_ref, back2_ref, out_ref):
-        for b in range(MEMBERS):
+    skip = (GROUP - FAR2) // ROWS
+
+    def kernel(near_hbm, back1_hbm, back2_hbm, out_hbm, near_ref, back1_ref, back2_ref, out_ref, sems):
+        def inbound(b):
+            cut = pl.ds(b * ROWS, ROWS)
+            copies = [
+                pltpu.make_async_copy(near_hbm.at[cut], near_ref.at[cut], sems.at[0, b]),
+                pltpu.make_async_copy(back1_hbm.at[cut], back1_ref.at[cut], sems.at[1, b]),
+            ]
+            if b >= skip:
+                far = pl.ds((b - skip) * ROWS, ROWS)
+                copies.append(
+                    pltpu.make_async_copy(back2_hbm.at[far], back2_ref.at[far], sems.at[2, b])
+                )
+            return copies
+
+        def outbound(b):
+            return pltpu.make_async_copy(out_ref.at[b], out_hbm.at[b], sems.at[3, b])
+
+        for b in range(MEMBERS):
+            for copy in inbound(b):
+                copy.start()
+        for b in range(MEMBERS):
+            for copy in inbound(b):
+                copy.wait()
             cut = slice(b * ROWS, (b + 1) * ROWS)
             total = near_ref[cut] + back1_ref[cut].astype(jnp.float32)
-            skip = (GROUP - FAR2) // ROWS
             if b >= skip:
                 far = slice((b - skip) * ROWS, (b - skip + 1) * ROWS)
                 total = total + back2_ref[far].astype(jnp.float32)
             out_ref[b] = total.astype(jnp.bfloat16)
-
-    return pl.pallas_call(
-        kernel,
-        in_specs=[VMEM] * 3,
-        out_specs=VMEM,
-        out_shape=jax.ShapeDtypeStruct((MEMBERS, ROWS, 2 * HEAD), jnp.bfloat16),
+            outbound(b).start()
+        for b in range(MEMBERS):
+            outbound(b).wait()
+
+    shape = (MEMBERS, ROWS, 2 * HEAD)
+    return pl.pallas_call(
+        kernel,
+        in_specs=[ANY] * 3,
+        out_specs=ANY,
+        out_shape=jax.ShapeDtypeStruct(shape, jnp.bfloat16),
+        scratch_shapes=[pltpu.VMEM(a.shape, a.dtype) for a in (near, back1, back2)]
+        + [pltpu.VMEM(shape, jnp.bfloat16), pltpu.SemaphoreType.DMA((4, MEMBERS))],
+        compiler_params=BIG,
         name="kv_sum",
     )(near, back1, back2)
 
@@ -314,17 +382,43 @@
 
 
 def kv_unpack(both):
-    def kernel(both_ref, k_ref, v_ref):
-        for b in range(MEMBERS):
-            k_ref[:, b * HEAD : (b + 1) * HEAD] = both_ref[b, :, 0:HEAD].astype(jnp.float32)
-            v_ref[:, b * HEAD : (b + 1) * HEAD] = both_ref[b, :, HEAD:].astype(jnp.float32)
+    def kernel(both_hbm, k_hbm, v_hbm, both_ref, k_ref, v_ref, sems):
+        def inbound(b):
+            return pltpu.make_async_copy(both_hbm.at[b], both_ref.at[b], sems.at[0, b])
+
+        def outbound(b):
+            cut = pl.ds(b * HEAD, HEAD)
+            return (
+                pltpu.make_async_copy(k_ref.at[b], k_hbm.at[:, cut], sems.at[1, b]),
+                pltpu.make_async_copy(v_ref.at[b], v_hbm.at[:, cut], sems.at[2, b]),
+            )
+
+        for b in range(MEMBERS):
+            inbound(b).start()
+        for b in range(MEMBERS):
+            inbound(b).wait()
+            k_ref[b] = both_ref[b, :, 0:HEAD].astype(jnp.float32)
+            v_ref[b] = both_ref[b, :, HEAD:].astype(jnp.float32)
+            for copy in outbound(b):
+                copy.start()
+        for b in range(MEMBERS):
+            for copy in outbound(b):
+                copy.wait()
 
     shape = jax.ShapeDtypeStruct((ROWS, MEMBERS * HEAD), jnp.float32)
-    return pl.pallas_call(
-        kernel,
-        in_specs=[VMEM],
-        out_specs=[VMEM, VMEM],
+    halves = pltpu.VMEM((MEMBERS, ROWS, HEAD), jnp.float32)
+    return pl.pallas_call(
+        kernel,
+        in_specs=[ANY],
+        out_specs=[ANY, ANY],
         out_shape=[shape, shape],
+        scratch_shapes=[
+            pltpu.VMEM((MEMBERS, ROWS, 2 * HEAD), jnp.bfloat16),
+            halves,
+            halves,
+            pltpu.SemaphoreType.DMA((3, MEMBERS)),
+        ],
+        compiler_params=BIG,
         name="kv_unpack",
     )(both)
 

time: 204 us -> 201 us (0.985)
  Pallas kernels: 79.1 us -> 76.2 us
    pallas_call x4, Pallas kernels: 63.5 us -> 60.6 us  [the longest x2 56.1 us: attention(): pl.pallas_call(kernel, in_specs=[SMEM, SMEM] + [ANY] * (len(operands) - 2...]
  transfers between devices with their start and end apart: 10 -> 10, of which waited for: 7 -> 7; matrix products, arithmetic and copies ran while one was open for 0% -> 0% of each run, Pallas kernels for 37% -> 36%
where the time goes in v2:
time: 201 us; the launch traced here: 200 us
  waiting for transfers between devices  76.3 us (38%)
  Pallas kernels  76.2 us (38%)
  starting transfers between devices  42.4 us (21%)
  local copies, waits for them, and re-layouts  4.62 us (2%)
    pallas_call x2, Pallas kernels, attention(): pl.pallas_call(kernel, in_specs=[SMEM, SMEM] + [ANY] * (len(operands) - 2...  56.1 us
    ppermute x4, waiting for transfers between devices, shifted(): return lax.ppermute(block, 'group', pairs)  41.9 us
    all_to_all x6, waiting for transfers between devices, exchange(): lax.all_to_all(blocks, ('core', 'head'), split_axis=0, concat_axis=0, til...  34.4 us
    all_to_all x6, starting transfers between devices, exchange(): lax.all_to_all(blocks, ('core', 'head'), split_axis=0, concat_axis=0, til...  29.7 us
    ppermute x4, starting transfers between devices, shifted(): return lax.ppermute(block, 'group', pairs)  12.7 us
    pallas_call x2, Pallas kernels, rows_pack(): pl.pallas_call(kernel, in_specs=[ANY, ANY, ANY, VMEM], out_specs=ANY, out...  8.66 us
    unnamed x18, local copies, waits for them, and re-layouts  4.62 us
  transfers between devices with their start and end apart: 10, of which 7 were waited for; matrix products, arithmetic and copies ran while one was open for 0% of the time, Pallas kernels for 36%

profile of v2, /device:TPU:7, one launch (start us, length us, event | category | flops | bytes accessed | tf_op | source)
XLA Modules:
  0.0 200.3 jit_solution(11023692830774600859)
XLA Ops:
  0.6 1.9 kv_pack.1
  2.5 5.1 %all-to-all-start.1 = ((bf16[8,128,256]{2,1,0:T(8,128)(2,1)}), bf16[8,128,256]{2,1,0:T(8,128)(2,1)S(1)}, u32[]{:S(2)}, u32[]{:S(2)}) async-start(bf16[8,128,256]{2,1,0:T(8,128)(2,1)} %kv_pack.1), calls=%async_computation.1 | async-start | bytes 1048576 | tf_op jit(solution)/shard_map/all_to_all | solution.py:427
  7.7 4.3 %rows_pack.2 = bf16[8,136,1024]{2,1,0:T(8,128)(2,1)} custom-call(bf16[128,8192]{1,0:T(8,128)(2,1)} %q_ref.3, bf16[128,8192]{1,0:T(8,128)(2,1)} %g_ref.3, bf16[128,8192]{1,0:T(8,128)(2,1)} %o_ref.3, f32[64,128]{1,0:T(8,128)} %bitcast.6), custom_call_target="tpu_custom_call" | custom-call | tf_op jit(solution)/shard_map/rows_pack/pallas_call | solution.py:103
  12.0 5.0 %all-to-all-done.1 = bf16[8,128,256]{2,1,0:T(8,128)(2,1)S(1)} async-done(((bf16[8,128,256]{2,1,0:T(8,128)(2,1)}), bf16[8,128,256]{2,1,0:T(8,128)(2,1)S(1)}, u32[]{:S(2)}, u32[]{:S(2)}) %all-to-all-start.1) | async-done | bytes 524320 | tf_op jit(solution)/shard_map/all_to_all | solution.py:427
  17.0 3.8 %all-to-all-start = ((bf16[8,136,1024]{2,1,0:T(8,128)(2,1)}), bf16[8,136,1024]{2,1,0:T(8,128)(2,1)S(1)}, u32[]{:S(2)}, u32[]{:S(2)}) async-start(bf16[8,136,1024]{2,1,0:T(8,128)(2,1)} %rows_pack.2), calls=%async_computation | async-start | bytes 4456448 | tf_op jit(solution)/shard_map/all_to_all | solution.py:427
  20.9 4.3 %rows_pack.3 = bf16[8,136,1024]{2,1,0:T(8,128)(2,1)} custom-call(bf16[128,8192]{1,0:T(8,128)(2,1)} %q_ref.3, bf16[128,8192]{1,0:T(8,128)(2,1)} %g_ref.3, bf16[128,8192]{1,0:T(8,128)(2,1)} %o_ref.3, f32[64,128]{1,0:T(8,128)} %bitcast.7), custom_call_target="tpu_custom_call" | custom-call | tf_op jit(solution)/shard_map/rows_pack/pallas_call | solution.py:103
  25.2 23.3 %all-to-all-done.rows_hbm = bf16[8,136,1024]{2,1,0:T(8,128)(2,1)S(1)} async-done(((bf16[8,136,1024]{2,1,0:T(8,128)(2,1)}), bf16[8,136,1024]{2,1,0:T(8,128)(2,1)S(1)}, u32[]{:S(2)}, u32[]{:S(2)}) %all-to-all-start) | async-done | bytes 2228256 | tf_op jit(solution)/shard_map/all_to_all | solution.py:427
  49.9 4.6 %all-to-all-start.3 = ((bf16[8,136,1024]{2,1,0:T(8,128)(2,1)}), bf16[8,136,1024]{2,1,0:T(8,128)(2,1)}, u32[]{:S(2)}, u32[]{:S(2)}) async-start(bf16[8,136,1024]{2,1,0:T(8,128)(2,1)} %rows_pack.3), calls=%async_computation.3 | async-start | bytes 4456448 | tf_op jit(solution)/shard_map/all_to_all | solution.py:427
  54.4 3.4 %collective-permute-start = (bf16[1024,256]{1,0:T(8,128)(2,1)S(1)}, bf16[1024,256]{1,0:T(8,128)(2,1)S(1)}, u32[]{:S(2)}, u32[]{:S(2)}) collective-permute-start(bf16[1024,256]{1,0:T(8,128)(2,1)S(1)} %bitcast.3), channel_id=1, source_target_pairs={{0,8},{8,16},{16,24},{24,32},{32,40},{40,48},{48,56},{56,64},{64,7... | collective-permute-start | bytes 1572872 | tf_op jit(solution)/shard_map/ppermute | solution.py:433
  57.9 11.9 %collective-permute-done.block_ref.far1_ref = bf16[1024,256]{1,0:T(8,128)(2,1)S(1)} collective-permute-done((bf16[1024,256]{1,0:T(8,128)(2,1)S(1)}, bf16[1024,256]{1,0:T(8,128)(2,1)S(1)}, u32[]{:S(2)}, u32[]{:S(2)}) %collective-permute-start) | collective-permute-done | bytes 524320 | tf_op jit(solution)/shard_map/ppermute | solution.py:433
  72.4 5.5 %collective-permute-start.1 = (bf16[768,256]{1,0:T(8,128)(2,1)}, bf16[768,256]{1,0:T(8,128)(2,1)S(1)}, u32[]{:S(2)}, u32[]{:S(2)}) collective-permute-start(bf16[768,256]{1,0:T(8,128)(2,1)} %relay.1), channel_id=1, source_target_pairs={{0,8},{8,16},{16,24},{24,32},{32,40},{40,48},{48,56},{56,64},{64,7... | collective-permute-start | bytes 1179656 | tf_op jit(solution)/shard_map/ppermute | solution.py:433
  77.8 7.8 %collective-permute-done.1.far2_ref = bf16[768,256]{1,0:T(8,128)(2,1)S(1)} collective-permute-done((bf16[768,256]{1,0:T(8,128)(2,1)}, bf16[768,256]{1,0:T(8,128)(2,1)S(1)}, u32[]{:S(2)}, u32[]{:S(2)}) %collective-permute-start.1) | collective-permute-done | bytes 393248 | tf_op jit(solution)/shard_map/ppermute | solution.py:433
  86.4 27.9 %shard_map.94 = (bf16[8,128,512]{2,1,0:T(8,128)(2,1)}, f32[2816,256]{1,0:T(8,128)}) custom-call(s32[16]{0:T(128)} %lengths_ref.3, s32[1]{0:T(128)} %bitcast.first_ref, bf16[8,136,1024]{2,1,0:T(8,128)(2,1)} %copy-done, bf16[768,256]{1,0:T(8,128)(2,1)} %copy-done.6, bf16[1024,256]{1,0:T(8,128)(2,1)} %copy-done.1, bf16[1024,256]{1,0:T(8,128)(2,1)} %bitcast.4), custom_call_target="tpu_custom_call" | custom-call | tf_op jit(solution)/shard_map/pallas_call | solution.py:283
  114.3 6.0 %all-to-all-start.2 = ((bf16[8,128,512]{2,1,0:T(8,128)(2,1)}), bf16[8,128,512]{2,1,0:T(8,128)(2,1)S(1)}, u32[]{:S(2)}, u32[]{:S(2)}) async-start(bf16[8,128,512]{2,1,0:T(8,128)(2,1)} %get-tuple-element.11), calls=%async_computation.2 | async-start | bytes 2097152 | tf_op jit(solution)/shard_map/all_to_all | solution.py:427
  120.4 28.2 %shard_map.95 = (bf16[8,128,512]{2,1,0:T(8,128)(2,1)}, bf16[768,256]{1,0:T(8,128)(2,1)}, bf16[1024,256]{1,0:T(8,128)(2,1)}, f32[1024,256]{1,0:T(8,128)}) custom-call(s32[16]{0:T(128)} %lengths_ref.3, s32[1]{0:T(128)} %bitcast.first_ref, bf16[8,136,1024]{2,1,0:T(8,128)(2,1)} %all-to-all-done.3.rows_hbm, bf16[768,256]{1,0:T(8,128)(2,1)} %copy-done.6, ...), custom_call_target="tpu_custom_call" | custom-call | tf_op jit(solution)/shard_map/pallas_call | solution.py:283
  148.6 4.8 %all-to-all-start.4 = ((bf16[8,128,512]{2,1,0:T(8,128)(2,1)}), bf16[8,128,512]{2,1,0:T(8,128)(2,1)S(1)}, u32[]{:S(2)}, u32[]{:S(2)}) async-start(bf16[8,128,512]{2,1,0:T(8,128)(2,1)} %get-tuple-element.13), calls=%async_computation.4 | async-start | bytes 2097152 | tf_op jit(solution)/shard_map/all_to_all | solution.py:427
  155.4 1.9 collective-permute-start.3
  157.3 18.3 %collective-permute-done.3.back2_hbm = bf16[768,256]{1,0:T(8,128)(2,1)S(1)} collective-permute-done((bf16[768,256]{1,0:T(8,128)(2,1)}, bf16[768,256]{1,0:T(8,128)(2,1)S(1)}, u32[]{:S(2)}, u32[]{:S(2)}) %collective-permute-start.3) | collective-permute-done | bytes 393248 | tf_op jit(solution)/shard_map/ppermute | solution.py:433
  175.6 3.9 %collective-permute-done.2.back1_hbm = bf16[1024,256]{1,0:T(8,128)(2,1)S(1)} collective-permute-done((bf16[1024,256]{1,0:T(8,128)(2,1)}, bf16[1024,256]{1,0:T(8,128)(2,1)S(1)}, u32[]{:S(2)}, u32[]{:S(2)}) %collective-permute-start.2) | collective-permute-done | bytes 524320 | tf_op jit(solution)/shard_map/ppermute | solution.py:433
  180.3 2.5 %kv_sum.1 = bf16[8,128,256]{2,1,0:T(8,128)(2,1)} custom-call(f32[1024,256]{1,0:T(8,128)} %get-tuple-element.14.near_hbm, bf16[1024,256]{1,0:T(8,128)(2,1)} %copy-done.7, bf16[768,256]{1,0:T(8,128)(2,1)} %copy-done.8), custom_call_target="tpu_custom_call" | custom-call | tf_op jit(solution)/shard_map/kv_sum/pallas_call | solution.py:330
  182.8 5.3 %all-to-all-start.5 = ((bf16[8,128,256]{2,1,0:T(8,128)(2,1)}), bf16[8,128,256]{2,1,0:T(8,128)(2,1)S(1)}, u32[]{:S(2)}, u32[]{:S(2)}) async-start(bf16[8,128,256]{2,1,0:T(8,128)(2,1)} %kv_sum.1), calls=%async_computation.5 | async-start | bytes 1048576 | tf_op jit(solution)/shard_map/all_to_all | solution.py:427
  188.1 3.2 %q_unpack.1 = f32[128,8192]{1,0:T(8,128)} custom-call(bf16[8,128,512]{2,1,0:T(8,128)(2,1)} %copy-done.3, bf16[8,128,512]{2,1,0:T(8,128)(2,1)} %copy-done.4), custom_call_target="tpu_custom_call" | custom-call | tf_op jit(solution)/shard_map/q_unpack/pallas_call | solution.py:368
  191.3 6.1 %all-to-all-done.5.both_hbm = bf16[8,128,256]{2,1,0:T(8,128)(2,1)S(1)} async-done(((bf16[8,128,256]{2,1,0:T(8,128)(2,1)}), bf16[8,128,256]{2,1,0:T(8,128)(2,1)S(1)}, u32[]{:S(2)}, u32[]{:S(2)}) %all-to-all-start.5) | async-done | bytes 524320 | tf_op jit(solution)/shard_map/all_to_all | solution.py:427
  198.3 2.0 kv_unpack.1
  (23 shorter events, 8.3 us)
Async XLA Ops:
  2.5 14.5 %all-to-all-start.1 = ((bf16[8,128,256]{2,1,0:T(8,128)(2,1)}), bf16[8,128,256]{2,1,0:T(8,128)(2,1)S(1)}, u32[]{:S(2)}, u32[]{:S(2)}) async-start(bf16[8,128,256]{2,1,0:T(8,128)(2,1)} %kv_pack.1), calls=%async_computation.1 | async-start | bytes 1048576 | tf_op jit(solution)/shard_map/all_to_all | solution.py:427
  17.0 37.4 %copy-start.2 = (bf16[8,128,256]{2,1,0:T(8,128)(2,1)}, bf16[8,128,256]{2,1,0:T(8,128)(2,1)S(1)}, u32[]{:S(2)}) copy-start(bf16[8,128,256]{2,1,0:T(8,128)(2,1)S(1)} %all-to-all-done.1) | copy-start | bytes 1572868
  17.0 31.4 %all-to-all-start = ((bf16[8,136,1024]{2,1,0:T(8,128)(2,1)}), bf16[8,136,1024]{2,1,0:T(8,128)(2,1)S(1)}, u32[]{:S(2)}, u32[]{:S(2)}) async-start(bf16[8,136,1024]{2,1,0:T(8,128)(2,1)} %rows_pack.2), calls=%async_computation | async-start | bytes 4456448 | tf_op jit(solution)/shard_map/all_to_all | solution.py:427
  48.5 1.4 copy-start
  49.9 64.4 %all-to-all-start.3 = ((bf16[8,136,1024]{2,1,0:T(8,128)(2,1)}), bf16[8,136,1024]{2,1,0:T(8,128)(2,1)}, u32[]{:S(2)}, u32[]{:S(2)}) async-start(bf16[8,136,1024]{2,1,0:T(8,128)(2,1)} %rows_pack.3), calls=%async_computation.3 | async-start | bytes 4456448 | tf_op jit(solution)/shard_map/all_to_all | solution.py:427
  54.4 15.3 %collective-permute-start = (bf16[1024,256]{1,0:T(8,128)(2,1)S(1)}, bf16[1024,256]{1,0:T(8,128)(2,1)S(1)}, u32[]{:S(2)}, u32[]{:S(2)}) collective-permute-start(bf16[1024,256]{1,0:T(8,128)(2,1)S(1)} %bitcast.3), channel_id=1, source_target_pairs={{0,8},{8,16},{16,24},{24,32},{32,40},{40,48},{48,56},{56,64},{64,7... | collective-permute-start | bytes 1572872 | tf_op jit(solution)/shard_map/ppermute | solution.py:433
  69.8 0.8 copy-start.1
  72.4 13.2 %collective-permute-start.1 = (bf16[768,256]{1,0:T(8,128)(2,1)}, bf16[768,256]{1,0:T(8,128)(2,1)S(1)}, u32[]{:S(2)}, u32[]{:S(2)}) collective-permute-start(bf16[768,256]{1,0:T(8,128)(2,1)} %relay.1), channel_id=1, source_target_pairs={{0,8},{8,16},{16,24},{24,32},{32,40},{40,48},{48,56},{56,64},{64,7... | collective-permute-start | bytes 1179656 | tf_op jit(solution)/shard_map/ppermute | solution.py:433
  85.6 0.8 copy-start.6
  114.3 34.3 %all-to-all-start.2 = ((bf16[8,128,512]{2,1,0:T(8,128)(2,1)}), bf16[8,128,512]{2,1,0:T(8,128)(2,1)S(1)}, u32[]{:S(2)}, u32[]{:S(2)}) async-start(bf16[8,128,512]{2,1,0:T(8,128)(2,1)} %get-tuple-element.11), calls=%async_computation.2 | async-start | bytes 2097152 | tf_op jit(solution)/shard_map/all_to_all | solution.py:427
  148.6 34.2 %copy-start.3 = (bf16[8,128,512]{2,1,0:T(8,128)(2,1)}, bf16[8,128,512]{2,1,0:T(8,128)(2,1)S(1)}, u32[]{:S(2)}) copy-start(bf16[8,128,512]{2,1,0:T(8,128)(2,1)S(1)} %all-to-all-done.2.refs_0_) | copy-start | bytes 3145732
  148.6 34.2 %all-to-all-start.4 = ((bf16[8,128,512]{2,1,0:T(8,128)(2,1)}), bf16[8,128,512]{2,1,0:T(8,128)(2,1)S(1)}, u32[]{:S(2)}, u32[]{:S(2)}) async-start(bf16[8,128,512]{2,1,0:T(8,128)(2,1)} %get-tuple-element.13), calls=%async_computation.4 | async-start | bytes 2097152 | tf_op jit(solution)/shard_map/all_to_all | solution.py:427
  153.4 26.1 %collective-permute-start.2 = (bf16[1024,256]{1,0:T(8,128)(2,1)}, bf16[1024,256]{1,0:T(8,128)(2,1)S(1)}, u32[]{:S(2)}, u32[]{:S(2)}) collective-permute-start(bf16[1024,256]{1,0:T(8,128)(2,1)} %get-tuple-element.15), channel_id=1, source_target_pairs={{8,0},{16,8},{24,16},{32,24},{40,32},{48,40},{56,48},{64,56},{72,6... | collective-permute-start | bytes 1572872 | tf_op jit(solution)/shard_map/ppermute | solution.py:433
  155.4 20.3 %collective-permute-start.3 = (bf16[768,256]{1,0:T(8,128)(2,1)}, bf16[768,256]{1,0:T(8,128)(2,1)S(1)}, u32[]{:S(2)}, u32[]{:S(2)}) collective-permute-start(bf16[768,256]{1,0:T(8,128)(2,1)} %get-tuple-element.16), channel_id=1, source_target_pairs={{16,0},{24,8},{32,16},{40,24},{48,32},{56,40},{64,48},{72,56},{80,... | collective-permute-start | bytes 1179656 | tf_op jit(solution)/shard_map/ppermute | solution.py:433
  175.6 3.9 %copy-start.8 = (bf16[768,256]{1,0:T(8,128)(2,1)}, bf16[768,256]{1,0:T(8,128)(2,1)S(1)}, u32[]{:S(2)}) copy-start(bf16[768,256]{1,0:T(8,128)(2,1)S(1)} %collective-permute-done.3.back2_hbm) | copy-start | bytes 1179652
  179.6 0.8 copy-start.7
  182.8 5.3 %copy-start.4 = (bf16[8,128,512]{2,1,0:T(8,128)(2,1)}, bf16[8,128,512]{2,1,0:T(8,128)(2,1)S(1)}, u32[]{:S(2)}) copy-start(bf16[8,128,512]{2,1,0:T(8,128)(2,1)S(1)} %all-to-all-done.4.refs_1_) | copy-start | bytes 3145732
  182.8 14.6 %all-to-all-start.5 = ((bf16[8,128,256]{2,1,0:T(8,128)(2,1)}), bf16[8,128,256]{2,1,0:T(8,128)(2,1)S(1)}, u32[]{:S(2)}, u32[]{:S(2)}) async-start(bf16[8,128,256]{2,1,0:T(8,128)(2,1)} %kv_sum.1), calls=%async_computation.5 | async-start | bytes 1048576 | tf_op jit(solution)/shard_map/all_to_all | solution.py:427
  197.5 0.8 copy-start.5

commit v3 on v1

--- a/solution.py
+++ b/solution.py
@@ -9,6 +9,7 @@
 
 
 LOG2E = math.log2(math.e)
+MASKED = -1e30
 HEAD = 128
 ROWS = 128
 MEMBERS = 8
@@ -128,24 +129,68 @@
     )(block)
 
 
-def attention(doc_lengths, first_token, rows, far2, far1, near, earlier, chunk):
+def attention(doc_lengths, first_token, rows, far2, far1, near, sums, q_far, keys):
     scaling = 1.0 / math.sqrt(HEAD)
     docs = doc_lengths.shape[0]
     parts = TQ // ROWS
-    last = chunk == CHUNKS - 1
-
-    def kernel(lengths_ref, first_ref, rows_ref, far2_ref, far1_ref, near_ref, *rest):
-        if last:
-            sums_ref, q_out, far2_out, far1_out, near_out, window, acc, q_acc = rest
-        else:
-            q_out, acc, window, q_acc = rest
-        window[0:FAR2] = far2_ref[...]
-        window[FAR2:FAR] = far1_ref[...]
-        window[FAR:WINDOW] = near_ref[...]
-        if last:
-            acc[...] = sums_ref[...]
-        else:
-            acc[...] = jnp.zeros_like(acc)
+    tiles = GROUP // TQ
+    pair = 2 * HEAD
+    low_row = FAR if keys == "near" else 0
+    high_row = FAR if keys == "far" else WINDOW
+    held = pl.ds(low_row, high_row - low_row)
+    sources = [
+        (ref, begin, size)
+        for ref, begin, size in ((far2, 0, FAR2), (far1, FAR2, GROUP), (near, FAR, GROUP))
+        if low_row <= begin < high_row
+    ]
+    operands = [doc_lengths, first_token, rows] + [ref for ref, _, _ in sources]
+    if keys != "all":
+        operands.append(sums)
+    if keys == "near":
+        operands.append(q_far)
+
+    def kernel(lengths_ref, first_ref, rows_hbm, *rest):
+        rest = list(rest)
+        source_refs = [rest.pop(0) for _ in sources]
+        if keys != "all":
+            sums_hbm = rest.pop(0)
+        if keys == "near":
+            q_far_hbm = rest.pop(0)
+        q_hbm = rest.pop(0)
+        sums_out = [rest.pop(0) for _ in (sources if keys != "all" else [0])]
+        rows_ref, q_ref, window, acc, q_acc, row_sem, key_sem, q_sem, sums_ref, sums_sem, far_sem = rest
+
+        def rows_copy(tile):
+            cut = pl.ds(tile * parts, parts)
+            return pltpu.make_async_copy(rows_hbm.at[cut], rows_ref.at[cut], row_sem.at[tile])
+
+        def q_copy(tile):
+            if keys == "far":
+                return pltpu.make_async_copy(q_acc.at[tile], q_hbm.at[tile], q_sem.at[tile])
+            cut = pl.ds(tile * parts, parts)
+            return pltpu.make_async_copy(q_ref.at[cut], q_hbm.at[cut], q_sem.at[tile])
+
+        def q_far_copy(tile):
+            return pltpu.make_async_copy(q_far_hbm.at[tile], q_acc.at[tile], far_sem.at[tile])
+
+        def sums_copy():
+            return pltpu.make_async_copy(sums_hbm.at[held], sums_ref.at[held], sums_sem)
+
+        key_copies = [
+            pltpu.make_async_copy(ref, window.at[pl.ds(begin, size)], key_sem.at[i])
+            for i, (ref, (_, begin, size)) in enumerate(zip(source_refs, sources))
+        ]
+        for copy in key_copies:
+            copy.start()
+        for tile in range(tiles):
+            rows_copy(tile).start()
+            if keys == "near":
+                q_far_copy(tile).start()
+        if keys != "all":
+            sums_copy().start()
+        acc[low_row:high_row] = jnp.zeros((high_row - low_row, pair), jnp.float32)
+        for copy in key_copies:
+            copy.wait()
         group_first = first_ref[0]
         window_first = group_first - FAR
 
@@ -163,13 +208,25 @@
             reach = position[0:1] - doc_start[0:1]
             key_begin = (doc_first - window_first) // TK
             key_end = (token + TQ - 1 - window_first) // TK + 1
+            if keys == "far":
+                key_end = jnp.minimum(key_end, FAR // TK)
+            if keys == "near":
+                key_begin = jnp.maximum(key_begin, FAR // TK)
             block = tile * parts
+            rows_copy(tile).wait()
+            if keys == "near":
+                q_far_copy(tile).wait()
+            else:
+                q_acc[tile] = jnp.zeros((H * TQ, HEAD), jnp.float32)
             pairs = [(h, s) for h in range(H) for s in range(parts)]
             query = jnp.concatenate(
                 [rows_ref[block + s, 0:ROWS, h * HEAD : (h + 1) * HEAD] for h, s in pairs], axis=0
             )
             grad = jnp.concatenate(
-                [rows_ref[block + s, 0:ROWS, WIDTH + h * HEAD : WIDTH + (h + 1) * HEAD] for h, s in pairs],
+                [
+                    rows_ref[block + s, 0:ROWS, WIDTH + h * HEAD : WIDTH + (h + 1) * HEAD]
+                    for h, s in pairs
+                ],
                 axis=0,
             )
             stats = [
@@ -183,7 +240,6 @@
             ]
             norm = LOG2E * jnp.concatenate([stats[s][h : h + 1] for h, s in pairs], axis=1)
             delta = jnp.concatenate([stats[s][H + h : H + h + 1] for h, s in pairs], axis=1)
-            q_acc[...] = jnp.zeros_like(q_acc)
 
             def key_tile(index, inner):
                 row = pl.multiple_of(index * TK, TK)
@@ -191,9 +247,9 @@
                 v_rows = window[pl.ds(row, TK), HEAD : 2 * HEAD]
                 offset = row + lax.broadcasted_iota(jnp.int32, (TK, TQ), 0) - low
                 allowed = (offset >= 0) & (offset <= reach)
-                allowed = jnp.concatenate([allowed] * H, axis=1)
+                bias = jnp.concatenate([jnp.where(allowed, 0.0, MASKED)] * H, axis=1)
                 scores = lax.dot_general(k_rows, query, NT, preferred_element_type=jnp.float32)
-                attend = jnp.where(allowed, jnp.exp2(scores * (scaling * LOG2E) - norm), 0.0)
+                attend = jnp.exp2(scores * (scaling * LOG2E) - norm + bias)
                 prob_grad = lax.dot_general(v_rows, grad, NT, preferred_element_type=jnp.float32)
                 score_low = (attend * (prob_grad - delta)).astype(jnp.bfloat16)
                 attend_low = attend.astype(jnp.bfloat16)
@@ -203,72 +259,116 @@
                 acc[pl.ds(row, TK), 0:HEAD] += jnp.dot(
                     score_low, query, preferred_element_type=jnp.float32
                 )
-                q_acc[...] += lax.dot_general(
+                q_acc[tile] += lax.dot_general(
                     score_low, k_rows, TN, preferred_element_type=jnp.float32
                 )
                 return inner
 
             lax.fori_loop(key_begin, key_end, key_tile, 0)
-            for at_row, (h, s) in enumerate(pairs):
-                part = q_acc[at_row * ROWS : (at_row + 1) * ROWS, :] * scaling
-                q_out[block + s, :, h * HEAD : (h + 1) * HEAD] = part.astype(jnp.bfloat16)
+            if keys != "far":
+                for at_row, (h, s) in enumerate(pairs):
+                    part = q_acc[tile, at_row * ROWS : (at_row + 1) * ROWS, :] * scaling
+                    q_ref[block + s, :, h * HEAD : (h + 1) * HEAD] = part.astype(jnp.bfloat16)
+            q_copy(tile).start()
             return carry
 
-        lax.fori_loop(0, GROUP // TQ, query_tile, 0)
-        if last:
-            for ref, begin, end in (
-                (far2_out, 0, FAR2),
-                (far1_out, FAR2, FAR),
-                (near_out, FAR, WINDOW),
-            ):
-                ref[:, 0:HEAD] = (acc[begin:end, 0:HEAD] * scaling).astype(ref.dtype)
-                ref[:, HEAD : 2 * HEAD] = acc[begin:end, HEAD : 2 * HEAD].astype(ref.dtype)
-
-    pair = 2 * HEAD
+        lax.fori_loop(0, tiles, query_tile, 0)
+        if keys == "all":
+            pltpu.sync_copy(acc, sums_out[0])
+        else:
+            sums_copy().wait()
+            for ref, (_, begin, size) in zip(sums_out, sources):
+                total = acc[begin : begin + size] + sums_ref[begin : begin + size]
+                ref[:, 0:HEAD] = (total[:, 0:HEAD] * scaling).astype(ref.dtype)
+                ref[:, HEAD : 2 * HEAD] = total[:, HEAD : 2 * HEAD].astype(ref.dtype)
+        for tile in range(tiles):
+            q_copy(tile).wait()
+
     q_shape = jax.ShapeDtypeStruct((MEMBERS, ROWS, WIDTH), jnp.bfloat16)
     acc_shape = (WINDOW, pair)
-    window_scratch = pltpu.VMEM((WINDOW, pair), jnp.bfloat16)
-    q_scratch = pltpu.VMEM((H * TQ, HEAD), jnp.float32)
-    if last:
-        out_shape = [
-            q_shape,
-            jax.ShapeDtypeStruct((FAR2, pair), jnp.bfloat16),
-            jax.ShapeDtypeStruct((GROUP, pair), jnp.bfloat16),
-            jax.ShapeDtypeStruct((GROUP, pair), jnp.float32),
-        ]
-        scratch = [window_scratch, pltpu.VMEM(acc_shape, jnp.float32), q_scratch]
+    q_acc_shape = (tiles, H * TQ, HEAD)
+    if keys == "all":
+        out_shape = [q_shape, jax.ShapeDtypeStruct(acc_shape, jnp.float32)]
+        out_specs = [ANY, ANY]
+    elif keys == "far":
+        out_shape = [jax.ShapeDtypeStruct(q_acc_shape, jnp.float32)]
+        out_shape += [jax.ShapeDtypeStruct((size, pair), jnp.bfloat16) for _, _, size in sources]
+        out_specs = [ANY] + [VMEM] * len(sources)
     else:
-        out_shape = [q_shape, jax.ShapeDtypeStruct(acc_shape, jnp.float32)]
-        scratch = [window_scratch, q_scratch]
-    operands = [doc_lengths, first_token, rows, far2, far1, near, *earlier]
-    return pl.pallas_call(
-        kernel,
-        in_specs=[SMEM, SMEM] + [VMEM] * (len(operands) - 2),
-        out_specs=[VMEM] * len(out_shape),
+        out_shape = [q_shape, jax.ShapeDtypeStruct((GROUP, pair), jnp.float32)]
+        out_specs = [ANY, VMEM]
+    return pl.pallas_call(
+        kernel,
+        in_specs=[SMEM, SMEM] + [ANY] * (len(operands) - 2),
+        out_specs=out_specs,
         out_shape=out_shape,
-        scratch_shapes=scratch,
+        scratch_shapes=[
+            pltpu.VMEM((MEMBERS, ROWS + STATS, 2 * WIDTH), jnp.bfloat16),
+            pltpu.VMEM(q_shape.shape, q_shape.dtype),
+            pltpu.VMEM((WINDOW, pair), jnp.bfloat16),
+            pltpu.VMEM(acc_shape, jnp.float32),
+            pltpu.VMEM(q_acc_shape, jnp.float32),
+            pltpu.SemaphoreType.DMA((tiles,)),
+            pltpu.SemaphoreType.DMA((3,)),
+            pltpu.SemaphoreType.DMA((tiles,)),
+            pltpu.VMEM(acc_shape, jnp.float32),
+            pltpu.SemaphoreType.DMA,
+            pltpu.SemaphoreType.DMA((tiles,)),
+        ],
         compiler_params=BIG,
     )(*operands)
 
 
-def kv_sum(near, back1, back2):
-    def kernel(near_ref, back1_ref, back2_ref, out_ref):
-        for b in range(MEMBERS):
-            cut = slice(b * ROWS, (b + 1) * ROWS)
-            total = near_ref[cut] + back1_ref[cut].astype(jnp.float32)
-            skip = (GROUP - FAR2) // ROWS
-            if b >= skip:
-                far = slice((b - skip) * ROWS, (b - skip + 1) * ROWS)
-                total = total + back2_ref[far].astype(jnp.float32)
-            out_ref[b] = total.astype(jnp.bfloat16)
-
-    return pl.pallas_call(
-        kernel,
-        in_specs=[VMEM] * 3,
-        out_specs=VMEM,
-        out_shape=jax.ShapeDtypeStruct((MEMBERS, ROWS, 2 * HEAD), jnp.bfloat16),
+def kv_sum(member, near, back1, back2):
+    skip = (GROUP - FAR2) // ROWS
+    wide = 2 * HEAD
+
+    def kernel(member_ref, near_hbm, back1_hbm, back2_hbm, *rest):
+        outs, (near_ref, back1_ref, back2_ref, out_ref, sems) = rest[:MEMBERS], rest[MEMBERS:]
+
+        def inbound(k):
+            b = (member_ref[0] + k) % MEMBERS
+            cut = pl.ds(pl.multiple_of(b * ROWS, ROWS), ROWS)
+            far = pl.ds(pl.multiple_of(jnp.maximum(b - skip, 0) * ROWS, ROWS), ROWS)
+            return (
+                pltpu.make_async_copy(near_hbm.at[cut], near_ref.at[k], sems.at[0, k]),
+                pltpu.make_async_copy(back1_hbm.at[cut], back1_ref.at[k], sems.at[1, k]),
+                pltpu.make_async_copy(back2_hbm.at[far], back2_ref.at[k], sems.at[2, k]),
+            )
+
+        def outbound(k):
+            return pltpu.make_async_copy(out_ref.at[k], outs[k], sems.at[3, k])
+
+        for k in range(MEMBERS):
+            for copy in inbound(k):
+                copy.start()
+        for k in range(MEMBERS):
+            for copy in inbound(k):
+                copy.wait()
+            reached = (member_ref[0] + k) % MEMBERS >= skip
+            total = near_ref[k] + back1_ref[k].astype(jnp.float32)
+            total = total + jnp.where(reached, back2_ref[k].astype(jnp.float32), 0.0)
+            out_ref[k] = total.astype(jnp.bfloat16)
+            outbound(k).start()
+        for k in range(MEMBERS):
+            outbound(k).wait()
+
+    shape = (MEMBERS, ROWS, wide)
+    return pl.pallas_call(
+        kernel,
+        in_specs=[SMEM] + [ANY] * 3,
+        out_specs=[ANY] * MEMBERS,
+        out_shape=[jax.ShapeDtypeStruct((ROWS, wide), jnp.bfloat16)] * MEMBERS,
+        scratch_shapes=[
+            pltpu.VMEM(shape, jnp.float32),
+            pltpu.VMEM(shape, jnp.bfloat16),
+            pltpu.VMEM(shape, jnp.bfloat16),
+            pltpu.VMEM(shape, jnp.bfloat16),
+            pltpu.SemaphoreType.DMA((4, MEMBERS)),
+        ],
+        compiler_params=BIG,
         name="kv_sum",
-    )(near, back1, back2)
+    )(member, near, back1, back2)
 
 
 def q_unpack(parts):
@@ -313,20 +413,49 @@
     )(*parts)
 
 
-def kv_unpack(both):
-    def kernel(both_ref, k_ref, v_ref):
-        for b in range(MEMBERS):
-            k_ref[:, b * HEAD : (b + 1) * HEAD] = both_ref[b, :, 0:HEAD].astype(jnp.float32)
-            v_ref[:, b * HEAD : (b + 1) * HEAD] = both_ref[b, :, HEAD:].astype(jnp.float32)
+def kv_unpack(member, pieces):
+    def kernel(member_ref, *rest):
+        sources, (k_hbm, v_hbm, both_ref, k_ref, v_ref, sems) = rest[:MEMBERS], rest[MEMBERS:]
+
+        def inbound(k):
+            return pltpu.make_async_copy(sources[k], both_ref.at[k], sems.at[0, k])
+
+        def outbound(k):
+            head = (member_ref[0] + MEMBERS - k) % MEMBERS
+            cut = pl.ds(pl.multiple_of(head * HEAD, HEAD), HEAD)
+            return (
+                pltpu.make_async_copy(k_ref.at[k], k_hbm.at[:, cut], sems.at[1, k]),
+                pltpu.make_async_copy(v_ref.at[k], v_hbm.at[:, cut], sems.at[2, k]),
+            )
+
+        for k in range(MEMBERS):
+            inbound(k).start()
+        for k in range(MEMBERS):
+            inbound(k).wait()
+            k_ref[k] = both_ref[k, :, 0:HEAD].astype(jnp.float32)
+            v_ref[k] = both_ref[k, :, HEAD:].astype(jnp.float32)
+            for copy in outbound(k):
+                copy.start()
+        for k in range(MEMBERS):
+            for copy in outbound(k):
+                copy.wait()
 
     shape = jax.ShapeDtypeStruct((ROWS, MEMBERS * HEAD), jnp.float32)
-    return pl.pallas_call(
-        kernel,
-        in_specs=[VMEM],
-        out_specs=[VMEM, VMEM],
+    halves = pltpu.VMEM((MEMBERS, ROWS, HEAD), jnp.float32)
+    return pl.pallas_call(
+        kernel,
+        in_specs=[SMEM] + [ANY] * MEMBERS,
+        out_specs=[ANY, ANY],
         out_shape=[shape, shape],
+        scratch_shapes=[
+            pltpu.VMEM((MEMBERS, ROWS, 2 * HEAD), jnp.bfloat16),
+            halves,
+            halves,
+            pltpu.SemaphoreType.DMA((3, MEMBERS)),
+        ],
+        compiler_params=BIG,
         name="kv_unpack",
-    )(both)
+    )(member, *pieces)
 
 
 def exchange(blocks):
@@ -350,18 +479,23 @@
     relayed = relay(far1)
     far2 = shifted(relayed, 1)
     first_token = (lax.axis_index("group") * GROUP).astype(jnp.int32).reshape(1)
-    sums, q_back = [], []
-    for chunk in range(CHUNKS):
-        q_part, *sums = attention(
-            doc_lengths, first_token, rows[chunk], far2, far1, near, sums, chunk
-        )
-        q_back.append(exchange(q_part))
-    far2_sum, far1_sum, near_sum = sums
+    member = lax.axis_index(("core", "head")).astype(jnp.int32).reshape(1)
+    fixed = (doc_lengths, first_token)
+    q_part, sums = attention(*fixed, rows[0], far2, far1, near, None, None, "all")
+    q_back = [exchange(q_part)]
+    q_far, far2_sum, far1_sum = attention(*fixed, rows[1], far2, far1, near, sums, None, "far")
     back1 = shifted(far1_sum, -1)
     back2 = shifted(far2_sum, -2)
-    both = exchange(kv_sum(near_sum, back1, back2))
+    q_part, near_sum = attention(
+        *fixed, rows[1], far2, far1, near, sums, q_far, "near"
+    )
+    q_back.append(exchange(q_part))
+    pieces = list(kv_sum(member, near_sum, back1, back2))
+    for k in range(1, MEMBERS):
+        ring = [(i, (i + k) % MEMBERS) for i in range(MEMBERS)]
+        pieces[k] = lax.ppermute(pieces[k], ("core", "head"), ring)
+    key_gradient, value_gradient = kv_unpack(member, pieces)
     q_grad = q_unpack(q_back)
-    key_gradient, value_gradient = kv_unpack(both)
     return (q_grad, key_gradient, value_gradient)
 
 

time: 204 us -> 209 us (1.025)
  starting transfers between devices: 42.4 us -> 46.1 us
    ppermute x0 -> x7, starting transfers between devices: none -> 9.66 us  [on_device(): pieces[k] = lax.ppermute(pieces[k], ('core', 'head'), ring)]
    all_to_all x6 -> x5, waiting for transfers between devices: 34.4 us -> 28.3 us  [exchange(): lax.all_to_all(blocks, ('core', 'head'), split_axis=0, concat_axis=0, til...]
    all_to_all x6 -> x5, starting transfers between devices: 29.7 us -> 23.6 us  [exchange(): lax.all_to_all(blocks, ('core', 'head'), split_axis=0, concat_axis=0, til...]
    ppermute x0 -> x7, waiting for transfers between devices: none -> 4.4 us  [on_device(): pieces[k] = lax.ppermute(pieces[k], ('core', 'head'), ring)]
    pallas_call x4 -> x5, Pallas kernels: 63.5 us -> 65.6 us  [the longest x3 61 us: attention(): pl.pallas_call(kernel, in_specs=[SMEM, SMEM] + [ANY] * (len(operands) - 2...]
    unnamed x18 -> x34, local copies, waits for them, and re-layouts: 4.61 us -> 5.34 us
  transfers between devices with their start and end apart: 10 -> 16, of which waited for: 7 -> 10; matrix products, arithmetic and copies ran while one was open for 0% -> 0% of each run, Pallas kernels for 37% -> 37%
where the time goes in v3:
time: 209 us; the launch traced here: 208 us
  Pallas kernels  81.1 us (39%)
  waiting for transfers between devices  74.3 us (36%)
  starting transfers between devices  46.1 us (22%)
  local copies, waits for them, and re-layouts  5.34 us (3%)
    pallas_call x3, Pallas kernels, attention(): pl.pallas_call(kernel, in_specs=[SMEM, SMEM] + [ANY] * (len(operands) - 2...  61 us
    ppermute x4, waiting for transfers between devices, shifted(): return lax.ppermute(block, 'group', pairs)  41.6 us
    all_to_all x5, waiting for transfers between devices, exchange(): lax.all_to_all(blocks, ('core', 'head'), split_axis=0, concat_axis=0, til...  28.3 us
    all_to_all x5, starting transfers between devices, exchange(): lax.all_to_all(blocks, ('core', 'head'), split_axis=0, concat_axis=0, til...  23.6 us
    ppermute x4, starting transfers between devices, shifted(): return lax.ppermute(block, 'group', pairs)  12.8 us
    ppermute x7, starting transfers between devices, on_device(): pieces[k] = lax.ppermute(pieces[k], ('core', 'head'), ring)  9.66 us
    pallas_call x2, Pallas kernels, rows_pack(): pl.pallas_call(kernel, in_specs=[ANY, ANY, ANY, VMEM], out_specs=ANY, out...  8.66 us
    unnamed x34, local copies, waits for them, and re-layouts  5.34 us
  transfers between devices with their start and end apart: 16, of which 10 were waited for; matrix products, arithmetic and copies ran while one was open for 0% of the time, Pallas kernels for 37%

profile of v3, /device:TPU:7, one launch (start us, length us, event | category | flops | bytes accessed | tf_op | source)
XLA Modules:
  0.0 207.8 jit_solution(3729515414561059878)
XLA Ops:
  2.5 5.1 %all-to-all-start.1 = ((bf16[8,128,256]{2,1,0:T(8,128)(2,1)}), bf16[8,128,256]{2,1,0:T(8,128)(2,1)S(1)}, u32[]{:S(2)}, u32[]{:S(2)}) async-start(bf16[8,128,256]{2,1,0:T(8,128)(2,1)} %kv_pack.1), calls=%async_computation.1 | async-start | bytes 1048576 | tf_op jit(solution)/shard_map/all_to_all | solution.py:462
  7.7 4.3 %rows_pack.2 = bf16[8,136,1024]{2,1,0:T(8,128)(2,1)} custom-call(bf16[128,8192]{1,0:T(8,128)(2,1)} %q_ref.3, bf16[128,8192]{1,0:T(8,128)(2,1)} %g_ref.3, bf16[128,8192]{1,0:T(8,128)(2,1)} %o_ref.3, f32[64,128]{1,0:T(8,128)} %bitcast.7), custom_call_target="tpu_custom_call" | custom-call | tf_op jit(solution)/shard_map/rows_pack/pallas_call | solution.py:103
  12.0 5.0 %all-to-all-done.1 = bf16[8,128,256]{2,1,0:T(8,128)(2,1)S(1)} async-done(((bf16[8,128,256]{2,1,0:T(8,128)(2,1)}), bf16[8,128,256]{2,1,0:T(8,128)(2,1)S(1)}, u32[]{:S(2)}, u32[]{:S(2)}) %all-to-all-start.1) | async-done | bytes 524320 | tf_op jit(solution)/shard_map/all_to_all | solution.py:462
  17.0 3.8 %all-to-all-start = ((bf16[8,136,1024]{2,1,0:T(8,128)(2,1)}), bf16[8,136,1024]{2,1,0:T(8,128)(2,1)S(1)}, u32[]{:S(2)}, u32[]{:S(2)}) async-start(bf16[8,136,1024]{2,1,0:T(8,128)(2,1)} %rows_pack.2), calls=%async_computation | async-start | bytes 4456448 | tf_op jit(solution)/shard_map/all_to_all | solution.py:462
  20.9 4.3 %rows_pack.3 = bf16[8,136,1024]{2,1,0:T(8,128)(2,1)} custom-call(bf16[128,8192]{1,0:T(8,128)(2,1)} %q_ref.3, bf16[128,8192]{1,0:T(8,128)(2,1)} %g_ref.3, bf16[128,8192]{1,0:T(8,128)(2,1)} %o_ref.3, f32[64,128]{1,0:T(8,128)} %bitcast.8), custom_call_target="tpu_custom_call" | custom-call | tf_op jit(solution)/shard_map/rows_pack/pallas_call | solution.py:103
  25.2 23.3 %all-to-all-done.rows_hbm = bf16[8,136,1024]{2,1,0:T(8,128)(2,1)S(1)} async-done(((bf16[8,136,1024]{2,1,0:T(8,128)(2,1)}), bf16[8,136,1024]{2,1,0:T(8,128)(2,1)S(1)}, u32[]{:S(2)}, u32[]{:S(2)}) %all-to-all-start) | async-done | bytes 2228256 | tf_op jit(solution)/shard_map/all_to_all | solution.py:462
  49.9 3.8 %all-to-all-start.3 = ((bf16[8,136,1024]{2,1,0:T(8,128)(2,1)}), bf16[8,136,1024]{2,1,0:T(8,128)(2,1)S(1)}, u32[]{:S(2)}, u32[]{:S(2)}) async-start(bf16[8,136,1024]{2,1,0:T(8,128)(2,1)} %rows_pack.3), calls=%async_computation.3 | async-start | bytes 4456448 | tf_op jit(solution)/shard_map/all_to_all | solution.py:462
  53.7 3.4 %collective-permute-start = (bf16[1024,256]{1,0:T(8,128)(2,1)S(1)}, bf16[1024,256]{1,0:T(8,128)(2,1)S(1)}, u32[]{:S(2)}, u32[]{:S(2)}) collective-permute-start(bf16[1024,256]{1,0:T(8,128)(2,1)S(1)} %bitcast.4), channel_id=1, source_target_pairs={{0,8},{8,16},{16,24},{24,32},{32,40},{40,48},{48,56},{56,64},{64,7... | collective-permute-start | bytes 1572872 | tf_op jit(solution)/shard_map/ppermute | solution.py:468
  57.2 11.8 %collective-permute-done.block_ref.rest_1_ = bf16[1024,256]{1,0:T(8,128)(2,1)S(1)} collective-permute-done((bf16[1024,256]{1,0:T(8,128)(2,1)S(1)}, bf16[1024,256]{1,0:T(8,128)(2,1)S(1)}, u32[]{:S(2)}, u32[]{:S(2)}) %collective-permute-start) | collective-permute-done | bytes 524320 | tf_op jit(solution)/shard_map/ppermute | solution.py:468
  71.6 5.6 %collective-permute-start.1 = (bf16[768,256]{1,0:T(8,128)(2,1)}, bf16[768,256]{1,0:T(8,128)(2,1)S(1)}, u32[]{:S(2)}, u32[]{:S(2)}) collective-permute-start(bf16[768,256]{1,0:T(8,128)(2,1)} %relay.1), channel_id=1, source_target_pairs={{0,8},{8,16},{16,24},{24,32},{32,40},{40,48},{48,56},{56,64},{64,7... | collective-permute-start | bytes 1179656 | tf_op jit(solution)/shard_map/ppermute | solution.py:468
  77.1 7.8 %collective-permute-done.1.rest_0_ = bf16[768,256]{1,0:T(8,128)(2,1)S(1)} collective-permute-done((bf16[768,256]{1,0:T(8,128)(2,1)}, bf16[768,256]{1,0:T(8,128)(2,1)S(1)}, u32[]{:S(2)}, u32[]{:S(2)}) %collective-permute-start.1) | collective-permute-done | bytes 393248 | tf_op jit(solution)/shard_map/ppermute | solution.py:468
  85.7 27.9 %shard_map.94 = (bf16[8,128,512]{2,1,0:T(8,128)(2,1)}, f32[2816,256]{1,0:T(8,128)}) custom-call(s32[16]{0:T(128)} %lengths_ref.5, s32[1]{0:T(128)} %bitcast.first_ref, bf16[8,136,1024]{2,1,0:T(8,128)(2,1)} %copy-done.1, bf16[768,256]{1,0:T(8,128)(2,1)} %copy-done.6, bf16[1024,256]{1,0:T(8,128)(2,1)} %copy-done.2, bf16[1024,256]{1,0:T(8,128)(2,1)} %bitcast.5), custom_call_target="tpu_custom_call" | custom-call | tf_op jit(solution)/shard_map/pallas_call | solution.py:300
  113.7 6.0 %all-to-all-start.2 = ((bf16[8,128,512]{2,1,0:T(8,128)(2,1)}), bf16[8,128,512]{2,1,0:T(8,128)(2,1)S(1)}, u32[]{:S(2)}, u32[]{:S(2)}) async-start(bf16[8,128,512]{2,1,0:T(8,128)(2,1)} %get-tuple-element.20), calls=%async_computation.2 | async-start | bytes 2097152 | tf_op jit(solution)/shard_map/all_to_all | solution.py:462
  119.7 18.9 %shard_map.95 = (f32[4,1024,128]{2,1,0:T(8,128)}, bf16[768,256]{1,0:T(8,128)(2,1)}, bf16[1024,256]{1,0:T(8,128)(2,1)}) custom-call(s32[16]{0:T(128)} %lengths_ref.5, s32[1]{0:T(128)} %bitcast.first_ref, bf16[8,136,1024]{2,1,0:T(8,128)(2,1)} %copy-done, bf16[768,256]{1,0:T(8,128)(2,1)} %copy-done.6, bf16[1024,256]{1,0:T(8,128)(2,1)} %copy-done.2, ...), custom_call_target="tpu_custom_call" | custom-call | tf_op jit(solution)/shard_map/pallas_call | solution.py:300
  138.6 14.2 %shard_map.96 = (bf16[8,128,512]{2,1,0:T(8,128)(2,1)}, f32[1024,256]{1,0:T(8,128)}) custom-call(s32[16]{0:T(128)} %lengths_ref.5, s32[1]{0:T(128)} %bitcast.first_ref, bf16[8,136,1024]{2,1,0:T(8,128)(2,1)} %copy-done, bf16[1024,256]{1,0:T(8,128)(2,1)} %bitcast.6, f32[2816,256]{1,0:T(8,128)} %get-tuple-element.21.rest_2_.rest_1_, ...), custom_call_target="tpu_custom_call" | custom-call | tf_op jit(solution)/shard_map/pallas_call | solution.py:300
  152.7 4.8 %all-to-all-start.4 = ((bf16[8,128,512]{2,1,0:T(8,128)(2,1)}), bf16[8,128,512]{2,1,0:T(8,128)(2,1)S(1)}, u32[]{:S(2)}, u32[]{:S(2)}) async-start(bf16[8,128,512]{2,1,0:T(8,128)(2,1)} %get-tuple-element.23), calls=%async_computation.4 | async-start | bytes 2097152 | tf_op jit(solution)/shard_map/all_to_all | solution.py:462
  159.5 1.9 collective-permute-start.3
  161.4 18.1 %collective-permute-done.3.back2_hbm = bf16[768,256]{1,0:T(8,128)(2,1)S(1)} collective-permute-done((bf16[768,256]{1,0:T(8,128)(2,1)}, bf16[768,256]{1,0:T(8,128)(2,1)S(1)}, u32[]{:S(2)}, u32[]{:S(2)}) %collective-permute-start.3) | collective-permute-done | bytes 393248 | tf_op jit(solution)/shard_map/ppermute | solution.py:468
  179.5 3.9 %collective-permute-done.2.back1_hbm = bf16[1024,256]{1,0:T(8,128)(2,1)S(1)} collective-permute-done((bf16[1024,256]{1,0:T(8,128)(2,1)S(1)}, bf16[1024,256]{1,0:T(8,128)(2,1)S(1)}, u32[]{:S(2)}, u32[]{:S(2)}) %collective-permute-start.2) | collective-permute-done | bytes 524320 | tf_op jit(solution)/shard_map/ppermute | solution.py:468
  184.2 2.6 %kv_sum.1 = (bf16[128,256]{1,0:T(8,128)(2,1)}, bf16[128,256]{1,0:T(8,128)(2,1)}, bf16[128,256]{1,0:T(8,128)(2,1)}, bf16[128,256]{1,0:T(8,128)(2,1)}, bf16[128,25...) custom-call(s32[1]{0:T(128)} %bitcast.3.member_ref, ...), custom_call_target="tpu_custom_call" | custom-call | tf_op jit(solution)/shard_map/kv_sum/pallas_call | solution.py:357
  187.9 2.3 %collective-permute-start.5 = (bf16[128,256]{1,0:T(8,128)(2,1)}, bf16[128,256]{1,0:T(8,128)(2,1)S(1)}, u32[]{:S(2)}, u32[]{:S(2)}) collective-permute-start(bf16[128,256]{1,0:T(8,128)(2,1)} %get-tuple-element.29), channel_id=1, source_target_pairs={{0,2},{1,3},{2,4},{3,5},{4,6},{5,7},{6,0},{7,1},{8,10},{9,11},{10,... | collective-permute-start | bytes 196616 | tf_op jit(solution)/shard_map/ppermute | solution.py:496
  190.2 2.7 %collective-permute-start.6 = (bf16[128,256]{1,0:T(8,128)(2,1)}, bf16[128,256]{1,0:T(8,128)(2,1)S(1)}, u32[]{:S(2)}, u32[]{:S(2)}) collective-permute-start(bf16[128,256]{1,0:T(8,128)(2,1)} %get-tuple-element.30), channel_id=1, source_target_pairs={{0,3},{1,4},{2,5},{3,6},{4,7},{5,0},{6,1},{7,2},{8,11},{9,12},{10,... | collective-permute-start | bytes 196616 | tf_op jit(solution)/shard_map/ppermute | solution.py:496
  201.5 2.0 kv_unpack.1
  204.6 3.2 %q_unpack.1 = f32[128,8192]{1,0:T(8,128)} custom-call(bf16[8,128,512]{2,1,0:T(8,128)(2,1)} %copy-done.4, bf16[8,128,512]{2,1,0:T(8,128)(2,1)} %copy-done.5), custom_call_target="tpu_custom_call" | custom-call | tf_op jit(solution)/shard_map/q_unpack/pallas_call | solution.py:400
  (52 shorter events, 20.0 us)
Async XLA Ops:
  2.5 14.5 %all-to-all-start.1 = ((bf16[8,128,256]{2,1,0:T(8,128)(2,1)}), bf16[8,128,256]{2,1,0:T(8,128)(2,1)S(1)}, u32[]{:S(2)}, u32[]{:S(2)}) async-start(bf16[8,128,256]{2,1,0:T(8,128)(2,1)} %kv_pack.1), calls=%async_computation.1 | async-start | bytes 1048576 | tf_op jit(solution)/shard_map/all_to_all | solution.py:462
  17.0 36.7 %copy-start.3 = (bf16[8,128,256]{2,1,0:T(8,128)(2,1)}, bf16[8,128,256]{2,1,0:T(8,128)(2,1)S(1)}, u32[]{:S(2)}) copy-start(bf16[8,128,256]{2,1,0:T(8,128)(2,1)S(1)} %all-to-all-done.1) | copy-start | bytes 1572868
  17.0 31.4 %all-to-all-start = ((bf16[8,136,1024]{2,1,0:T(8,128)(2,1)}), bf16[8,136,1024]{2,1,0:T(8,128)(2,1)S(1)}, u32[]{:S(2)}, u32[]{:S(2)}) async-start(bf16[8,136,1024]{2,1,0:T(8,128)(2,1)} %rows_pack.2), calls=%async_computation | async-start | bytes 4456448 | tf_op jit(solution)/shard_map/all_to_all | solution.py:462
  49.9 63.8 %all-to-all-start.3 = ((bf16[8,136,1024]{2,1,0:T(8,128)(2,1)}), bf16[8,136,1024]{2,1,0:T(8,128)(2,1)S(1)}, u32[]{:S(2)}, u32[]{:S(2)}) async-start(bf16[8,136,1024]{2,1,0:T(8,128)(2,1)} %rows_pack.3), calls=%async_computation.3 | async-start | bytes 4456448 | tf_op jit(solution)/shard_map/all_to_all | solution.py:462
  53.7 15.3 %collective-permute-start = (bf16[1024,256]{1,0:T(8,128)(2,1)S(1)}, bf16[1024,256]{1,0:T(8,128)(2,1)S(1)}, u32[]{:S(2)}, u32[]{:S(2)}) collective-permute-start(bf16[1024,256]{1,0:T(8,128)(2,1)S(1)} %bitcast.4), channel_id=1, source_target_pairs={{0,8},{8,16},{16,24},{24,32},{32,40},{40,48},{48,56},{56,64},{64,7... | collective-permute-start | bytes 1572872 | tf_op jit(solution)/shard_map/ppermute | solution.py:468
  71.6 13.4 %collective-permute-start.1 = (bf16[768,256]{1,0:T(8,128)(2,1)}, bf16[768,256]{1,0:T(8,128)(2,1)S(1)}, u32[]{:S(2)}, u32[]{:S(2)}) collective-permute-start(bf16[768,256]{1,0:T(8,128)(2,1)} %relay.1), channel_id=1, source_target_pairs={{0,8},{8,16},{16,24},{24,32},{32,40},{40,48},{48,56},{56,64},{64,7... | collective-permute-start | bytes 1179656 | tf_op jit(solution)/shard_map/ppermute | solution.py:468
  113.6 6.0 %copy-start = (bf16[8,136,1024]{2,1,0:T(8,128)(2,1)}, bf16[8,136,1024]{2,1,0:T(8,128)(2,1)S(1)}, u32[]{:S(2)}) copy-start(bf16[8,136,1024]{2,1,0:T(8,128)(2,1)S(1)} %all-to-all-done.3.rows_hbm) | copy-start | bytes 6684676
  113.7 39.1 %all-to-all-start.2 = ((bf16[8,128,512]{2,1,0:T(8,128)(2,1)}), bf16[8,128,512]{2,1,0:T(8,128)(2,1)S(1)}, u32[]{:S(2)}, u32[]{:S(2)}) async-start(bf16[8,128,512]{2,1,0:T(8,128)(2,1)} %get-tuple-element.20), calls=%async_computation.2 | async-start | bytes 2097152 | tf_op jit(solution)/shard_map/all_to_all | solution.py:462
  138.5 19.0 %copy-start.16 = (bf16[1024,256]{1,0:T(8,128)(2,1)S(1)}, bf16[1024,256]{1,0:T(8,128)(2,1)}, u32[]{:S(2)}) copy-start(bf16[1024,256]{1,0:T(8,128)(2,1)} %get-tuple-element.25) | copy-start | bytes 1572868
  152.7 50.8 %copy-start.4 = (bf16[8,128,512]{2,1,0:T(8,128)(2,1)}, bf16[8,128,512]{2,1,0:T(8,128)(2,1)S(1)}, u32[]{:S(2)}) copy-start(bf16[8,128,512]{2,1,0:T(8,128)(2,1)S(1)} %all-to-all-done.2.refs_0_) | copy-start | bytes 3145732
  152.7 50.8 %all-to-all-start.4 = ((bf16[8,128,512]{2,1,0:T(8,128)(2,1)}), bf16[8,128,512]{2,1,0:T(8,128)(2,1)S(1)}, u32[]{:S(2)}, u32[]{:S(2)}) async-start(bf16[8,128,512]{2,1,0:T(8,128)(2,1)} %get-tuple-element.23), calls=%async_computation.4 | async-start | bytes 2097152 | tf_op jit(solution)/shard_map/all_to_all | solution.py:462
  157.5 25.9 %collective-permute-start.2 = (bf16[1024,256]{1,0:T(8,128)(2,1)S(1)}, bf16[1024,256]{1,0:T(8,128)(2,1)S(1)}, u32[]{:S(2)}, u32[]{:S(2)}) collective-permute-start(bf16[1024,256]{1,0:T(8,128)(2,1)S(1)} %copy-done.16), channel_id=1, source_target_pairs={{8,0},{16,8},{24,16},{32,24},{40,32},{48,40},{56,48},{64,56},{72,6... | collective-permute-start | bytes 1572872 | tf_op jit(solution)/shard_map/ppermute | solution.py:468
  159.5 20.1 %collective-permute-start.3 = (bf16[768,256]{1,0:T(8,128)(2,1)}, bf16[768,256]{1,0:T(8,128)(2,1)S(1)}, u32[]{:S(2)}, u32[]{:S(2)}) collective-permute-start(bf16[768,256]{1,0:T(8,128)(2,1)} %get-tuple-element.26), channel_id=1, source_target_pairs={{16,0},{24,8},{32,16},{40,24},{48,32},{56,40},{64,48},{72,56},{80,... | collective-permute-start | bytes 1179656 | tf_op jit(solution)/shard_map/ppermute | solution.py:468
  186.8 7.1 %collective-permute-start.4 = (bf16[128,256]{1,0:T(8,128)(2,1)}, bf16[128,256]{1,0:T(8,128)(2,1)S(1)}, u32[]{:S(2)}, u32[]{:S(2)}) collective-permute-start(bf16[128,256]{1,0:T(8,128)(2,1)} %get-tuple-element.28), channel_id=1, source_target_pairs={{0,1},{1,2},{2,3},{3,4},{4,5},{5,6},{6,7},{7,0},{8,9},{9,10},{10,1... | collective-permute-start | bytes 196616 | tf_op jit(solution)/shard_map/ppermute | solution.py:496
  187.9 7.4 %collective-permute-start.5 = (bf16[128,256]{1,0:T(8,128)(2,1)}, bf16[128,256]{1,0:T(8,128)(2,1)S(1)}, u32[]{:S(2)}, u32[]{:S(2)}) collective-permute-start(bf16[128,256]{1,0:T(8,128)(2,1)} %get-tuple-element.29), channel_id=1, source_target_pairs={{0,2},{1,3},{2,4},{3,5},{4,6},{5,7},{6,0},{7,1},{8,10},{9,11},{10,... | collective-permute-start | bytes 196616 | tf_op jit(solution)/shard_map/ppermute | solution.py:496
  190.2 6.4 %collective-permute-start.6 = (bf16[128,256]{1,0:T(8,128)(2,1)}, bf16[128,256]{1,0:T(8,128)(2,1)S(1)}, u32[]{:S(2)}, u32[]{:S(2)}) collective-permute-start(bf16[128,256]{1,0:T(8,128)(2,1)} %get-tuple-element.30), channel_id=1, source_target_pairs={{0,3},{1,4},{2,5},{3,6},{4,7},{5,0},{6,1},{7,2},{8,11},{9,12},{10,... | collective-permute-start | bytes 196616 | tf_op jit(solution)/shard_map/ppermute | solution.py:496
  192.9 3.7 %collective-permute-start.7 = (bf16[128,256]{1,0:T(8,128)(2,1)}, bf16[128,256]{1,0:T(8,128)(2,1)S(1)}, u32[]{:S(2)}, u32[]{:S(2)}) collective-permute-start(bf16[128,256]{1,0:T(8,128)(2,1)} %get-tuple-element.31), channel_id=1, source_target_pairs={{0,4},{1,5},{2,6},{3,7},{4,0},{5,1},{6,2},{7,3},{8,12},{9,13},{10,... | collective-permute-start | bytes 196616 | tf_op jit(solution)/shard_map/ppermute | solution.py:496
  192.9 4.5 %collective-permute-start.8 = (bf16[128,256]{1,0:T(8,128)(2,1)}, bf16[128,256]{1,0:T(8,128)(2,1)S(1)}, u32[]{:S(2)}, u32[]{:S(2)}) collective-permute-start(bf16[128,256]{1,0:T(8,128)(2,1)} %get-tuple-element.32), channel_id=1, source_target_pairs={{0,5},{1,6},{2,7},{3,0},{4,1},{5,2},{6,3},{7,4},{8,13},{9,14},{10,... | collective-permute-start | bytes 196616 | tf_op jit(solution)/shard_map/ppermute | solution.py:496
  193.9 7.0 %copy-start.9 = (bf16[128,256]{1,0:T(8,128)(2,1)}, bf16[128,256]{1,0:T(8,128)(2,1)S(1)}, u32[]{:S(2)}) copy-start(bf16[128,256]{1,0:T(8,128)(2,1)S(1)} %collective-permute-done.4.rest_1_) | copy-start | bytes 196612
  193.9 5.4 %collective-permute-start.9 = (bf16[128,256]{1,0:T(8,128)(2,1)}, bf16[128,256]{1,0:T(8,128)(2,1)S(1)}, u32[]{:S(2)}, u32[]{:S(2)}) collective-permute-start(bf16[128,256]{1,0:T(8,128)(2,1)} %get-tuple-element.33), channel_id=1, source_target_pairs={{0,6},{1,7},{2,0},{3,1},{4,2},{5,3},{6,4},{7,5},{8,14},{9,15},{10,... | collective-permute-start | bytes 196616 | tf_op jit(solution)/shard_map/ppermute | solution.py:496
  195.3 5.6 %copy-start.10 = (bf16[128,256]{1,0:T(8,128)(2,1)}, bf16[128,256]{1,0:T(8,128)(2,1)S(1)}, u32[]{:S(2)}) copy-start(bf16[128,256]{1,0:T(8,128)(2,1)S(1)} %collective-permute-done.5.rest_2_) | copy-start | bytes 196612
  195.3 5.6 %collective-permute-start.10 = (bf16[128,256]{1,0:T(8,128)(2,1)}, bf16[128,256]{1,0:T(8,128)(2,1)S(1)}, u32[]{:S(2)}, u32[]{:S(2)}) collective-permute-start(bf16[128,256]{1,0:T(8,128)(2,1)} %get-tuple-element.34), channel_id=1, source_target_pairs={{0,7},{1,0},{2,1},{3,2},{4,3},{5,4},{6,5},{7,6},{8,15},{9,8},{10,9... | collective-permute-start | bytes 196616 | tf_op jit(solution)/shard_map/ppermute | solution.py:496
  196.6 4.3 %copy-start.11 = (bf16[128,256]{1,0:T(8,128)(2,1)}, bf16[128,256]{1,0:T(8,128)(2,1)S(1)}, u32[]{:S(2)}) copy-start(bf16[128,256]{1,0:T(8,128)(2,1)S(1)} %collective-permute-done.6.rest_3_) | copy-start | bytes 196612
  196.7 4.3 %copy-start.12 = (bf16[128,256]{1,0:T(8,128)(2,1)}, bf16[128,256]{1,0:T(8,128)(2,1)S(1)}, u32[]{:S(2)}) copy-start(bf16[128,256]{1,0:T(8,128)(2,1)S(1)} %collective-permute-done.7.rest_4_) | copy-start | bytes 196612
  (9 other events, 14.5 us)

commit v4 on v3

--- a/solution.py
+++ b/solution.py
@@ -116,19 +116,6 @@
     )(queries, grads, outs, norms)
 
 
-def relay(block):
-    def kernel(block_ref, out_ref):
-        out_ref[...] = block_ref[GROUP - FAR2 :]
-
-    return pl.pallas_call(
-        kernel,
-        in_specs=[VMEM],
-        out_specs=VMEM,
-        out_shape=jax.ShapeDtypeStruct((FAR2, 2 * HEAD), jnp.bfloat16),
-        name="relay",
-    )(block)
-
-
 def attention(doc_lengths, first_token, rows, far2, far1, near, sums, q_far, keys):
     scaling = 1.0 / math.sqrt(HEAD)
     docs = doc_lengths.shape[0]
@@ -139,10 +126,13 @@
     high_row = FAR if keys == "far" else WINDOW
     held = pl.ds(low_row, high_row - low_row)
     sources = [
-        (ref, begin, size)
-        for ref, begin, size in ((far2, 0, FAR2), (far1, FAR2, GROUP), (near, FAR, GROUP))
+        (ref, begin, ref.shape[0])
+        for ref, begin in zip(
+            (far2, *far1, near), (0, FAR2, FAR2 + far1[0].shape[0], FAR)
+        )
         if low_row <= begin < high_row
     ]
+    targets = {"all": [(0, WINDOW)], "far": [(0, FAR2), (FAR2, GROUP)], "near": [(FAR, GROUP)]}[keys]
     operands = [doc_lengths, first_token, rows] + [ref for ref, _, _ in sources]
     if keys != "all":
         operands.append(sums)
@@ -157,7 +147,7 @@
         if keys == "near":
             q_far_hbm = rest.pop(0)
         q_hbm = rest.pop(0)
-        sums_out = [rest.pop(0) for _ in (sources if keys != "all" else [0])]
+        sums_out = [rest.pop(0) for _ in targets]
         rows_ref, q_ref, window, acc, q_acc, row_sem, key_sem, q_sem, sums_ref, sums_sem, far_sem = rest
 
         def rows_copy(tile):
@@ -264,7 +254,13 @@
                 )
                 return inner
 
-            lax.fori_loop(key_begin, key_end, key_tile, 0)
+            def two_tiles(index, inner):
+                key_tile(key_begin + 2 * index, inner)
+                return key_tile(key_begin + 2 * index + 1, inner)
+
+            twos = jnp.maximum(key_end - key_begin, 0) // 2
+            lax.fori_loop(0, twos, two_tiles, 0)
+            lax.fori_loop(key_begin + 2 * twos, key_end, key_tile, 0)
             if keys != "far":
                 for at_row, (h, s) in enumerate(pairs):
                     part = q_acc[tile, at_row * ROWS : (at_row + 1) * ROWS, :] * scaling
@@ -277,7 +273,7 @@
             pltpu.sync_copy(acc, sums_out[0])
         else:
             sums_copy().wait()
-            for ref, (_, begin, size) in zip(sums_out, sources):
+            for ref, (begin, size) in zip(sums_out, targets):
                 total = acc[begin : begin + size] + sums_ref[begin : begin + size]
                 ref[:, 0:HEAD] = (total[:, 0:HEAD] * scaling).astype(ref.dtype)
                 ref[:, HEAD : 2 * HEAD] = total[:, HEAD : 2 * HEAD].astype(ref.dtype)
@@ -292,8 +288,8 @@
         out_specs = [ANY, ANY]
     elif keys == "far":
         out_shape = [jax.ShapeDtypeStruct(q_acc_shape, jnp.float32)]
-        out_shape += [jax.ShapeDtypeStruct((size, pair), jnp.bfloat16) for _, _, size in sources]
-        out_specs = [ANY] + [VMEM] * len(sources)
+        out_shape += [jax.ShapeDtypeStruct((size, pair), jnp.bfloat16) for _, size in targets]
+        out_specs = [ANY] + [VMEM] * len(targets)
     else:
         out_shape = [q_shape, jax.ShapeDtypeStruct((GROUP, pair), jnp.float32)]
         out_specs = [ANY, VMEM]
@@ -309,7 +305,7 @@
             pltpu.VMEM(acc_shape, jnp.float32),
             pltpu.VMEM(q_acc_shape, jnp.float32),
             pltpu.SemaphoreType.DMA((tiles,)),
-            pltpu.SemaphoreType.DMA((3,)),
+            pltpu.SemaphoreType.DMA((4,)),
             pltpu.SemaphoreType.DMA((tiles,)),
             pltpu.VMEM(acc_shape, jnp.float32),
             pltpu.SemaphoreType.DMA,
@@ -475,9 +471,9 @@
     for chunk in range(CHUNKS):
         packed = rows_pack(queries, output_gradient, out_rows, norms, chunk)
         rows.append(exchange(packed))
-    far1 = shifted(near, 1)
-    relayed = relay(far1)
-    far2 = shifted(relayed, 1)
+    forwarded = shifted(near[GROUP - FAR2 :], 1)
+    far1 = (shifted(near[: GROUP - FAR2], 1), forwarded)
+    far2 = shifted(forwarded, 1)
     first_token = (lax.axis_index("group") * GROUP).astype(jnp.int32).reshape(1)
     member = lax.axis_index(("core", "head")).astype(jnp.int32).reshape(1)
     fixed = (doc_lengths, first_token)

time: 209 us -> 202 us (0.967)
  Pallas kernels: 81.1 us -> 75.9 us
  waiting for transfers between devices: 74.3 us -> 72.1 us
    pallas_call x3, Pallas kernels: 61 us -> 57.5 us  [attention(): pl.pallas_call(kernel, in_specs=[SMEM, SMEM] + [ANY] * (len(operands) - 2...]
    ppermute x4 -> x5, waiting for transfers between devices: 41.6 us -> 39.4 us  [shifted(): return lax.ppermute(block, 'group', pairs)]
    ppermute x4 -> x5, starting transfers between devices: 12.8 us -> 14.8 us  [shifted(): return lax.ppermute(block, 'group', pairs)]
  transfers between devices with their start and end apart: 16 -> 17, of which waited for: 10 -> 10; matrix products, arithmetic and copies ran while one was open for 0% -> 0% of each run, Pallas kernels for 37% -> 35%
where the time goes in v4:
time: 202 us; the launch traced here: 201 us
  Pallas kernels  75.9 us (38%)
  waiting for transfers between devices  72.1 us (36%)
  starting transfers between devices  48 us (24%)
  local copies, waits for them, and re-layouts  4.46 us (2%)
    pallas_call x3, Pallas kernels, attention(): pl.pallas_call(kernel, in_specs=[SMEM, SMEM] + [ANY] * (len(operands) - 2...  57.5 us
    ppermute x5, waiting for transfers between devices, shifted(): return lax.ppermute(block, 'group', pairs)  39.4 us
    all_to_all x5, waiting for transfers between devices, exchange(): lax.all_to_all(blocks, ('core', 'head'), split_axis=0, concat_axis=0, til...  28.3 us
    all_to_all x5, starting transfers between devices, exchange(): lax.all_to_all(blocks, ('core', 'head'), split_axis=0, concat_axis=0, til...  23.6 us
    ppermute x5, starting transfers between devices, shifted(): return lax.ppermute(block, 'group', pairs)  14.8 us
    ppermute x7, starting transfers between devices, on_device(): pieces[k] = lax.ppermute(pieces[k], ('core', 'head'), ring)  9.66 us
    pallas_call x2, Pallas kernels, rows_pack(): pl.pallas_call(kernel, in_specs=[ANY, ANY, ANY, VMEM], out_specs=ANY, out...  8.66 us
    unnamed x34, local copies, waits for them, and re-layouts  4.43 us
  transfers between devices with their start and end apart: 17, of which 10 were waited for; matrix products, arithmetic and copies ran while one was open for 0% of the time, Pallas kernels for 35%

profile of v4, /device:TPU:7, one launch (start us, length us, event | category | flops | bytes accessed | tf_op | source)
XLA Modules:
  0.0 201.5 jit_solution(7637407148609630742)
XLA Ops:
  2.5 5.1 %all-to-all-start.1 = ((bf16[8,128,256]{2,1,0:T(8,128)(2,1)}), bf16[8,128,256]{2,1,0:T(8,128)(2,1)S(1)}, u32[]{:S(2)}, u32[]{:S(2)}) async-start(bf16[8,128,256]{2,1,0:T(8,128)(2,1)} %kv_pack.1), calls=%async_computation.1 | async-start | bytes 1048576 | tf_op jit(solution)/shard_map/all_to_all | solution.py:458
  7.7 4.3 %rows_pack.2 = bf16[8,136,1024]{2,1,0:T(8,128)(2,1)} custom-call(bf16[128,8192]{1,0:T(8,128)(2,1)} %q_ref.3, bf16[128,8192]{1,0:T(8,128)(2,1)} %g_ref.3, bf16[128,8192]{1,0:T(8,128)(2,1)} %o_ref.3, f32[64,128]{1,0:T(8,128)} %bitcast.9), custom_call_target="tpu_custom_call" | custom-call | tf_op jit(solution)/shard_map/rows_pack/pallas_call | solution.py:103
  12.0 5.0 %all-to-all-done.1 = bf16[8,128,256]{2,1,0:T(8,128)(2,1)S(1)} async-done(((bf16[8,128,256]{2,1,0:T(8,128)(2,1)}), bf16[8,128,256]{2,1,0:T(8,128)(2,1)S(1)}, u32[]{:S(2)}, u32[]{:S(2)}) %all-to-all-start.1) | async-done | bytes 524320 | tf_op jit(solution)/shard_map/all_to_all | solution.py:458
  17.0 3.8 %all-to-all-start = ((bf16[8,136,1024]{2,1,0:T(8,128)(2,1)}), bf16[8,136,1024]{2,1,0:T(8,128)(2,1)S(1)}, u32[]{:S(2)}, u32[]{:S(2)}) async-start(bf16[8,136,1024]{2,1,0:T(8,128)(2,1)} %rows_pack.2), calls=%async_computation | async-start | bytes 4456448 | tf_op jit(solution)/shard_map/all_to_all | solution.py:458
  20.9 4.3 %rows_pack.3 = bf16[8,136,1024]{2,1,0:T(8,128)(2,1)} custom-call(bf16[128,8192]{1,0:T(8,128)(2,1)} %q_ref.3, bf16[128,8192]{1,0:T(8,128)(2,1)} %g_ref.3, bf16[128,8192]{1,0:T(8,128)(2,1)} %o_ref.3, f32[64,128]{1,0:T(8,128)} %bitcast.10), custom_call_target="tpu_custom_call" | custom-call | tf_op jit(solution)/shard_map/rows_pack/pallas_call | solution.py:103
  25.2 23.3 %all-to-all-done.rows_hbm = bf16[8,136,1024]{2,1,0:T(8,128)(2,1)S(1)} async-done(((bf16[8,136,1024]{2,1,0:T(8,128)(2,1)}), bf16[8,136,1024]{2,1,0:T(8,128)(2,1)S(1)}, u32[]{:S(2)}, u32[]{:S(2)}) %all-to-all-start) | async-done | bytes 2228256 | tf_op jit(solution)/shard_map/all_to_all | solution.py:458
  49.9 3.8 %all-to-all-start.3 = ((bf16[8,136,1024]{2,1,0:T(8,128)(2,1)}), bf16[8,136,1024]{2,1,0:T(8,128)(2,1)S(1)}, u32[]{:S(2)}, u32[]{:S(2)}) async-start(bf16[8,136,1024]{2,1,0:T(8,128)(2,1)} %rows_pack.3), calls=%async_computation.3 | async-start | bytes 4456448 | tf_op jit(solution)/shard_map/all_to_all | solution.py:458
  53.7 3.5 %collective-permute-start = (bf16[768,256]{1,0:T(8,128)(2,1)S(1)}, bf16[768,256]{1,0:T(8,128)(2,1)S(1)}, u32[]{:S(2)}, u32[]{:S(2)}) collective-permute-start(bf16[768,256]{1,0:T(8,128)(2,1)S(1)} %bitcast.8), channel_id=1, source_target_pairs={{0,8},{8,16},{16,24},{24,32},{32,40},{40,48},{48,56},{56,64},{64,7... | collective-permute-start | bytes 1179656 | tf_op jit(solution)/shard_map/ppermute | solution.py:464
  57.2 9.0 %collective-permute-done.rest_2_ = bf16[768,256]{1,0:T(8,128)(2,1)S(1)} collective-permute-done((bf16[768,256]{1,0:T(8,128)(2,1)S(1)}, bf16[768,256]{1,0:T(8,128)(2,1)S(1)}, u32[]{:S(2)}, u32[]{:S(2)}) %collective-permute-start) | collective-permute-done | bytes 393248 | tf_op jit(solution)/shard_map/ppermute | solution.py:464
  66.2 5.6 %collective-permute-start.1 = (bf16[768,256]{1,0:T(8,128)(2,1)S(1)}, bf16[768,256]{1,0:T(8,128)(2,1)}, u32[]{:S(2)}, u32[]{:S(2)}) collective-permute-start(bf16[768,256]{1,0:T(8,128)(2,1)S(1)} %collective-permute-done.rest_2_), channel_id=1, source_target_pairs={{0,8},{8,16},{16,24},{24,32},{32,40},{40,48},{48,56},{56,64},{64,7... | collective-permute-start | bytes 1179656 | tf_op jit(solution)/shard_map/ppermute | solution.py:464
  71.8 1.9 collective-permute-start.2
  73.7 8.3 %collective-permute-done.2.rest_1_ = bf16[256,256]{1,0:T(8,128)(2,1)S(1)} collective-permute-done((bf16[256,256]{1,0:T(8,128)(2,1)S(1)}, bf16[256,256]{1,0:T(8,128)(2,1)S(1)}, u32[]{:S(2)}, u32[]{:S(2)}) %collective-permute-start.2) | collective-permute-done | bytes 131104 | tf_op jit(solution)/shard_map/ppermute | solution.py:464
  82.7 26.3 %shard_map.94 = (bf16[8,128,512]{2,1,0:T(8,128)(2,1)}, f32[2816,256]{1,0:T(8,128)}) custom-call(s32[16]{0:T(128)} %lengths_ref.5, s32[1]{0:T(128)} %bitcast.first_ref, bf16[8,136,1024]{2,1,0:T(8,128)(2,1)} %copy-done.1, bf16[768,256]{1,0:T(8,128)(2,1)} %collective-permute-done.1.rest_0_, bf16[256,256]{1,0:T(8,128)(2,1)} %copy-done.7, ...), custom_call_target="tpu_custom_call" | custom-call | tf_op jit(solution)/shard_map/pallas_call | solution.py:296
  109.0 6.0 %all-to-all-start.2 = ((bf16[8,128,512]{2,1,0:T(8,128)(2,1)}), bf16[8,128,512]{2,1,0:T(8,128)(2,1)S(1)}, u32[]{:S(2)}, u32[]{:S(2)}) async-start(bf16[8,128,512]{2,1,0:T(8,128)(2,1)} %get-tuple-element.20), calls=%async_computation.2 | async-start | bytes 2097152 | tf_op jit(solution)/shard_map/all_to_all | solution.py:458
  115.0 17.7 %shard_map.95 = (f32[4,1024,128]{2,1,0:T(8,128)}, bf16[768,256]{1,0:T(8,128)(2,1)}, bf16[1024,256]{1,0:T(8,128)(2,1)}) custom-call(s32[16]{0:T(128)} %lengths_ref.5, s32[1]{0:T(128)} %bitcast.first_ref, bf16[8,136,1024]{2,1,0:T(8,128)(2,1)} %copy-done, bf16[768,256]{1,0:T(8,128)(2,1)} %collective-permute-done.1.rest_0_, bf16[256,256]{1,0:T(8,128)(2,1)} %copy-done.7, ...), custom_call_target="tpu_custom_call" | custom-call | tf_op jit(solution)/shard_map/pallas_call | solution.py:296
  132.7 13.6 %shard_map.96 = (bf16[8,128,512]{2,1,0:T(8,128)(2,1)}, f32[1024,256]{1,0:T(8,128)}) custom-call(s32[16]{0:T(128)} %lengths_ref.5, s32[1]{0:T(128)} %bitcast.first_ref, bf16[8,136,1024]{2,1,0:T(8,128)(2,1)} %copy-done, bf16[1024,256]{1,0:T(8,128)(2,1)} %bitcast.7, f32[2816,256]{1,0:T(8,128)} %get-tuple-element.21.rest_3_.rest_1_, ...), custom_call_target="tpu_custom_call" | custom-call | tf_op jit(solution)/shard_map/pallas_call | solution.py:296
  146.3 4.8 %all-to-all-start.4 = ((bf16[8,128,512]{2,1,0:T(8,128)(2,1)}), bf16[8,128,512]{2,1,0:T(8,128)(2,1)S(1)}, u32[]{:S(2)}, u32[]{:S(2)}) async-start(bf16[8,128,512]{2,1,0:T(8,128)(2,1)} %get-tuple-element.23), calls=%async_computation.4 | async-start | bytes 2097152 | tf_op jit(solution)/shard_map/all_to_all | solution.py:458
  155.0 18.1 %collective-permute-done.4.back2_hbm = bf16[768,256]{1,0:T(8,128)(2,1)S(1)} collective-permute-done((bf16[768,256]{1,0:T(8,128)(2,1)}, bf16[768,256]{1,0:T(8,128)(2,1)S(1)}, u32[]{:S(2)}, u32[]{:S(2)}) %collective-permute-start.4) | collective-permute-done | bytes 393248 | tf_op jit(solution)/shard_map/ppermute | solution.py:464
  173.1 3.9 %collective-permute-done.3.back1_hbm = bf16[1024,256]{1,0:T(8,128)(2,1)S(1)} collective-permute-done((bf16[1024,256]{1,0:T(8,128)(2,1)S(1)}, bf16[1024,256]{1,0:T(8,128)(2,1)S(1)}, u32[]{:S(2)}, u32[]{:S(2)}) %collective-permute-start.3) | collective-permute-done | bytes 524320 | tf_op jit(solution)/shard_map/ppermute | solution.py:464
  177.8 2.6 %kv_sum.1 = (bf16[128,256]{1,0:T(8,128)(2,1)}, bf16[128,256]{1,0:T(8,128)(2,1)}, bf16[128,256]{1,0:T(8,128)(2,1)}, bf16[128,256]{1,0:T(8,128)(2,1)}, bf16[128,25...) custom-call(s32[1]{0:T(128)} %bitcast.5.member_ref, ...), custom_call_target="tpu_custom_call" | custom-call | tf_op jit(solution)/shard_map/kv_sum/pallas_call | solution.py:353
  181.5 2.3 %collective-permute-start.6 = (bf16[128,256]{1,0:T(8,128)(2,1)}, bf16[128,256]{1,0:T(8,128)(2,1)S(1)}, u32[]{:S(2)}, u32[]{:S(2)}) collective-permute-start(bf16[128,256]{1,0:T(8,128)(2,1)} %get-tuple-element.29), channel_id=1, source_target_pairs={{0,2},{1,3},{2,4},{3,5},{4,6},{5,7},{6,0},{7,1},{8,10},{9,11},{10,... | collective-permute-start | bytes 196616 | tf_op jit(solution)/shard_map/ppermute | solution.py:492
  183.8 2.7 %collective-permute-start.7 = (bf16[128,256]{1,0:T(8,128)(2,1)}, bf16[128,256]{1,0:T(8,128)(2,1)S(1)}, u32[]{:S(2)}, u32[]{:S(2)}) collective-permute-start(bf16[128,256]{1,0:T(8,128)(2,1)} %get-tuple-element.30), channel_id=1, source_target_pairs={{0,3},{1,4},{2,5},{3,6},{4,7},{5,0},{6,1},{7,2},{8,11},{9,12},{10,... | collective-permute-start | bytes 196616 | tf_op jit(solution)/shard_map/ppermute | solution.py:492
  195.1 2.0 kv_unpack.1
  198.1 3.2 %q_unpack.1 = f32[128,8192]{1,0:T(8,128)} custom-call(bf16[8,128,512]{2,1,0:T(8,128)(2,1)} %copy-done.3, bf16[8,128,512]{2,1,0:T(8,128)(2,1)} %copy-done.4), custom_call_target="tpu_custom_call" | custom-call | tf_op jit(solution)/shard_map/q_unpack/pallas_call | solution.py:396
  (55 shorter events, 19.2 us)
Async XLA Ops:
  2.5 14.5 %all-to-all-start.1 = ((bf16[8,128,256]{2,1,0:T(8,128)(2,1)}), bf16[8,128,256]{2,1,0:T(8,128)(2,1)S(1)}, u32[]{:S(2)}, u32[]{:S(2)}) async-start(bf16[8,128,256]{2,1,0:T(8,128)(2,1)} %kv_pack.1), calls=%async_computation.1 | async-start | bytes 1048576 | tf_op jit(solution)/shard_map/all_to_all | solution.py:458
  17.0 54.7 %copy-start.2 = (bf16[8,128,256]{2,1,0:T(8,128)(2,1)}, bf16[8,128,256]{2,1,0:T(8,128)(2,1)S(1)}, u32[]{:S(2)}) copy-start(bf16[8,128,256]{2,1,0:T(8,128)(2,1)S(1)} %all-to-all-done.1) | copy-start | bytes 1572868
  17.0 31.4 %all-to-all-start = ((bf16[8,136,1024]{2,1,0:T(8,128)(2,1)}), bf16[8,136,1024]{2,1,0:T(8,128)(2,1)S(1)}, u32[]{:S(2)}, u32[]{:S(2)}) async-start(bf16[8,136,1024]{2,1,0:T(8,128)(2,1)} %rows_pack.2), calls=%async_computation | async-start | bytes 4456448 | tf_op jit(solution)/shard_map/all_to_all | solution.py:458
  49.9 59.1 %all-to-all-start.3 = ((bf16[8,136,1024]{2,1,0:T(8,128)(2,1)}), bf16[8,136,1024]{2,1,0:T(8,128)(2,1)S(1)}, u32[]{:S(2)}, u32[]{:S(2)}) async-start(bf16[8,136,1024]{2,1,0:T(8,128)(2,1)} %rows_pack.3), calls=%async_computation.3 | async-start | bytes 4456448 | tf_op jit(solution)/shard_map/all_to_all | solution.py:458
  53.7 12.5 %collective-permute-start = (bf16[768,256]{1,0:T(8,128)(2,1)S(1)}, bf16[768,256]{1,0:T(8,128)(2,1)S(1)}, u32[]{:S(2)}, u32[]{:S(2)}) collective-permute-start(bf16[768,256]{1,0:T(8,128)(2,1)S(1)} %bitcast.8), channel_id=1, source_target_pairs={{0,8},{8,16},{16,24},{24,32},{32,40},{40,48},{48,56},{56,64},{64,7... | collective-permute-start | bytes 1179656 | tf_op jit(solution)/shard_map/ppermute | solution.py:464
  66.2 15.9 %copy-start.5 = (bf16[768,256]{1,0:T(8,128)(2,1)}, bf16[768,256]{1,0:T(8,128)(2,1)S(1)}, u32[]{:S(2)}) copy-start(bf16[768,256]{1,0:T(8,128)(2,1)S(1)} %collective-permute-done.rest_2_) | copy-start | bytes 1179652
  66.2 15.9 %collective-permute-start.1 = (bf16[768,256]{1,0:T(8,128)(2,1)S(1)}, bf16[768,256]{1,0:T(8,128)(2,1)}, u32[]{:S(2)}, u32[]{:S(2)}) collective-permute-start(bf16[768,256]{1,0:T(8,128)(2,1)S(1)} %collective-permute-done.rest_2_), channel_id=1, source_target_pairs={{0,8},{8,16},{16,24},{24,32},{32,40},{40,48},{48,56},{56,64},{64,7... | collective-permute-start | bytes 1179656 | tf_op jit(solution)/shard_map/ppermute | solution.py:464
  71.8 10.3 %collective-permute-start.2 = (bf16[256,256]{1,0:T(8,128)(2,1)S(1)}, bf16[256,256]{1,0:T(8,128)(2,1)S(1)}, u32[]{:S(2)}, u32[]{:S(2)}) collective-permute-start(bf16[256,256]{1,0:T(8,128)(2,1)S(1)} %bitcast.11), channel_id=1, source_target_pairs={{0,8},{8,16},{16,24},{24,32},{32,40},{40,48},{48,56},{56,64},{64,7... | collective-permute-start | bytes 393224 | tf_op jit(solution)/shard_map/ppermute | solution.py:464
  109.0 6.0 %copy-start = (bf16[8,136,1024]{2,1,0:T(8,128)(2,1)}, bf16[8,136,1024]{2,1,0:T(8,128)(2,1)S(1)}, u32[]{:S(2)}) copy-start(bf16[8,136,1024]{2,1,0:T(8,128)(2,1)S(1)} %all-to-all-done.3.rows_hbm) | copy-start | bytes 6684676
  109.0 37.3 %all-to-all-start.2 = ((bf16[8,128,512]{2,1,0:T(8,128)(2,1)}), bf16[8,128,512]{2,1,0:T(8,128)(2,1)S(1)}, u32[]{:S(2)}, u32[]{:S(2)}) async-start(bf16[8,128,512]{2,1,0:T(8,128)(2,1)} %get-tuple-element.20), calls=%async_computation.2 | async-start | bytes 2097152 | tf_op jit(solution)/shard_map/all_to_all | solution.py:458
  132.7 18.5 %copy-start.16 = (bf16[1024,256]{1,0:T(8,128)(2,1)S(1)}, bf16[1024,256]{1,0:T(8,128)(2,1)}, u32[]{:S(2)}) copy-start(bf16[1024,256]{1,0:T(8,128)(2,1)} %get-tuple-element.25) | copy-start | bytes 1572868
  146.3 50.8 %copy-start.3 = (bf16[8,128,512]{2,1,0:T(8,128)(2,1)}, bf16[8,128,512]{2,1,0:T(8,128)(2,1)S(1)}, u32[]{:S(2)}) copy-start(bf16[8,128,512]{2,1,0:T(8,128)(2,1)S(1)} %all-to-all-done.2.refs_0_) | copy-start | bytes 3145732
  146.3 50.8 %all-to-all-start.4 = ((bf16[8,128,512]{2,1,0:T(8,128)(2,1)}), bf16[8,128,512]{2,1,0:T(8,128)(2,1)S(1)}, u32[]{:S(2)}, u32[]{:S(2)}) async-start(bf16[8,128,512]{2,1,0:T(8,128)(2,1)} %get-tuple-element.23), calls=%async_computation.4 | async-start | bytes 2097152 | tf_op jit(solution)/shard_map/all_to_all | solution.py:458
  151.1 25.9 %collective-permute-start.3 = (bf16[1024,256]{1,0:T(8,128)(2,1)S(1)}, bf16[1024,256]{1,0:T(8,128)(2,1)S(1)}, u32[]{:S(2)}, u32[]{:S(2)}) collective-permute-start(bf16[1024,256]{1,0:T(8,128)(2,1)S(1)} %copy-done.16), channel_id=1, source_target_pairs={{8,0},{16,8},{24,16},{32,24},{40,32},{48,40},{56,48},{64,56},{72,6... | collective-permute-start | bytes 1572872 | tf_op jit(solution)/shard_map/ppermute | solution.py:464
  153.1 20.1 %collective-permute-start.4 = (bf16[768,256]{1,0:T(8,128)(2,1)}, bf16[768,256]{1,0:T(8,128)(2,1)S(1)}, u32[]{:S(2)}, u32[]{:S(2)}) collective-permute-start(bf16[768,256]{1,0:T(8,128)(2,1)} %get-tuple-element.26), channel_id=1, source_target_pairs={{16,0},{24,8},{32,16},{40,24},{48,32},{56,40},{64,48},{72,56},{80,... | collective-permute-start | bytes 1179656 | tf_op jit(solution)/shard_map/ppermute | solution.py:464
  180.4 7.1 %collective-permute-start.5 = (bf16[128,256]{1,0:T(8,128)(2,1)}, bf16[128,256]{1,0:T(8,128)(2,1)S(1)}, u32[]{:S(2)}, u32[]{:S(2)}) collective-permute-start(bf16[128,256]{1,0:T(8,128)(2,1)} %get-tuple-element.28), channel_id=1, source_target_pairs={{0,1},{1,2},{2,3},{3,4},{4,5},{5,6},{6,7},{7,0},{8,9},{9,10},{10,1... | collective-permute-start | bytes 196616 | tf_op jit(solution)/shard_map/ppermute | solution.py:492
  181.5 7.4 %collective-permute-start.6 = (bf16[128,256]{1,0:T(8,128)(2,1)}, bf16[128,256]{1,0:T(8,128)(2,1)S(1)}, u32[]{:S(2)}, u32[]{:S(2)}) collective-permute-start(bf16[128,256]{1,0:T(8,128)(2,1)} %get-tuple-element.29), channel_id=1, source_target_pairs={{0,2},{1,3},{2,4},{3,5},{4,6},{5,7},{6,0},{7,1},{8,10},{9,11},{10,... | collective-permute-start | bytes 196616 | tf_op jit(solution)/shard_map/ppermute | solution.py:492
  183.8 6.4 %collective-permute-start.7 = (bf16[128,256]{1,0:T(8,128)(2,1)}, bf16[128,256]{1,0:T(8,128)(2,1)S(1)}, u32[]{:S(2)}, u32[]{:S(2)}) collective-permute-start(bf16[128,256]{1,0:T(8,128)(2,1)} %get-tuple-element.30), channel_id=1, source_target_pairs={{0,3},{1,4},{2,5},{3,6},{4,7},{5,0},{6,1},{7,2},{8,11},{9,12},{10,... | collective-permute-start | bytes 196616 | tf_op jit(solution)/shard_map/ppermute | solution.py:492
  186.5 3.7 %collective-permute-start.8 = (bf16[128,256]{1,0:T(8,128)(2,1)}, bf16[128,256]{1,0:T(8,128)(2,1)S(1)}, u32[]{:S(2)}, u32[]{:S(2)}) collective-permute-start(bf16[128,256]{1,0:T(8,128)(2,1)} %get-tuple-element.31), channel_id=1, source_target_pairs={{0,4},{1,5},{2,6},{3,7},{4,0},{5,1},{6,2},{7,3},{8,12},{9,13},{10,... | collective-permute-start | bytes 196616 | tf_op jit(solution)/shard_map/ppermute | solution.py:492
  186.5 4.5 %collective-permute-start.9 = (bf16[128,256]{1,0:T(8,128)(2,1)}, bf16[128,256]{1,0:T(8,128)(2,1)S(1)}, u32[]{:S(2)}, u32[]{:S(2)}) collective-permute-start(bf16[128,256]{1,0:T(8,128)(2,1)} %get-tuple-element.32), channel_id=1, source_target_pairs={{0,5},{1,6},{2,7},{3,0},{4,1},{5,2},{6,3},{7,4},{8,13},{9,14},{10,... | collective-permute-start | bytes 196616 | tf_op jit(solution)/shard_map/ppermute | solution.py:492
  187.5 7.0 %copy-start.9 = (bf16[128,256]{1,0:T(8,128)(2,1)}, bf16[128,256]{1,0:T(8,128)(2,1)S(1)}, u32[]{:S(2)}) copy-start(bf16[128,256]{1,0:T(8,128)(2,1)S(1)} %collective-permute-done.5.rest_1_) | copy-start | bytes 196612
  187.5 5.4 %collective-permute-start.10 = (bf16[128,256]{1,0:T(8,128)(2,1)}, bf16[128,256]{1,0:T(8,128)(2,1)S(1)}, u32[]{:S(2)}, u32[]{:S(2)}) collective-permute-start(bf16[128,256]{1,0:T(8,128)(2,1)} %get-tuple-element.33), channel_id=1, source_target_pairs={{0,6},{1,7},{2,0},{3,1},{4,2},{5,3},{6,4},{7,5},{8,14},{9,15},{10,... | collective-permute-start | bytes 196616 | tf_op jit(solution)/shard_map/ppermute | solution.py:492
  188.9 5.6 %copy-start.10 = (bf16[128,256]{1,0:T(8,128)(2,1)}, bf16[128,256]{1,0:T(8,128)(2,1)S(1)}, u32[]{:S(2)}) copy-start(bf16[128,256]{1,0:T(8,128)(2,1)S(1)} %collective-permute-done.6.rest_2_) | copy-start | bytes 196612
  188.9 5.6 %collective-permute-start.11 = (bf16[128,256]{1,0:T(8,128)(2,1)}, bf16[128,256]{1,0:T(8,128)(2,1)S(1)}, u32[]{:S(2)}, u32[]{:S(2)}) collective-permute-start(bf16[128,256]{1,0:T(8,128)(2,1)} %get-tuple-element.34), channel_id=1, source_target_pairs={{0,7},{1,0},{2,1},{3,2},{4,3},{5,4},{6,5},{7,6},{8,15},{9,8},{10,9... | collective-permute-start | bytes 196616 | tf_op jit(solution)/shard_map/ppermute | solution.py:492
  (10 other events, 22.1 us)

commit v5 on v4

--- a/solution.py
+++ b/solution.py
@@ -23,6 +23,7 @@
 H = HEADS // CHUNKS
 WIDTH = H * HEAD
 STATS = 2 * H
+STEP = {"all": 2, "far": 3, "near": 2}
 TQ = 256
 TK = 256
 NT = (((1,), (1,)), ((), ()))
@@ -254,13 +255,14 @@
                 )
                 return inner
 
-            def two_tiles(index, inner):
-                key_tile(key_begin + 2 * index, inner)
-                return key_tile(key_begin + 2 * index + 1, inner)
-
-            twos = jnp.maximum(key_end - key_begin, 0) // 2
-            lax.fori_loop(0, twos, two_tiles, 0)
-            lax.fori_loop(key_begin + 2 * twos, key_end, key_tile, 0)
+            def many_tiles(index, inner):
+                for part in range(STEP[keys]):
+                    key_tile(key_begin + STEP[keys] * index + part, inner)
+                return inner
+
+            steps = jnp.maximum(key_end - key_begin, 0) // STEP[keys]
+            lax.fori_loop(0, steps, many_tiles, 0)
+            lax.fori_loop(key_begin + STEP[keys] * steps, key_end, key_tile, 0)
             if keys != "far":
                 for at_row, (h, s) in enumerate(pairs):
                     part = q_acc[tile, at_row * ROWS : (at_row + 1) * ROWS, :] * scaling

time: 202 us -> 202 us (level)
  no operation moved by 1% of the time
where the time goes in v5:
time: 202 us; the launch traced here: 201 us
  Pallas kernels  75.7 us (37%)
  waiting for transfers between devices  72.1 us (36%)
  starting transfers between devices  48 us (24%)
  local copies, waits for them, and re-layouts  4.46 us (2%)
    pallas_call x3, Pallas kernels, attention(): pl.pallas_call(kernel, in_specs=[SMEM, SMEM] + [ANY] * (len(operands) - 2...  57.3 us
    ppermute x5, waiting for transfers between devices, shifted(): return lax.ppermute(block, 'group', pairs)  39.4 us
    all_to_all x5, waiting for transfers between devices, exchange(): lax.all_to_all(blocks, ('core', 'head'), split_axis=0, concat_axis=0, til...  28.3 us
    all_to_all x5, starting transfers between devices, exchange(): lax.all_to_all(blocks, ('core', 'head'), split_axis=0, concat_axis=0, til...  23.6 us
    ppermute x5, starting transfers between devices, shifted(): return lax.ppermute(block, 'group', pairs)  14.8 us
    ppermute x7, starting transfers between devices, on_device(): pieces[k] = lax.ppermute(pieces[k], ('core', 'head'), ring)  9.66 us
    pallas_call x2, Pallas kernels, rows_pack(): pl.pallas_call(kernel, in_specs=[ANY, ANY, ANY, VMEM], out_specs=ANY, out...  8.66 us
    unnamed x34, local copies, waits for them, and re-layouts  4.43 us
  transfers between devices with their start and end apart: 17, of which 10 were waited for; matrix products, arithmetic and copies ran while one was open for 0% of the time, Pallas kernels for 35%

profile of v5, /device:TPU:7, one launch (start us, length us, event | category | flops | bytes accessed | tf_op | source)
XLA Modules:
  0.0 201.3 jit_solution(2486230726517024842)
XLA Ops:
  2.5 5.1 %all-to-all-start.1 = ((bf16[8,128,256]{2,1,0:T(8,128)(2,1)}), bf16[8,128,256]{2,1,0:T(8,128)(2,1)S(1)}, u32[]{:S(2)}, u32[]{:S(2)}) async-start(bf16[8,128,256]{2,1,0:T(8,128)(2,1)} %kv_pack.1), calls=%async_computation.1 | async-start | bytes 1048576 | tf_op jit(solution)/shard_map/all_to_all | solution.py:460
  7.7 4.3 %rows_pack.2 = bf16[8,136,1024]{2,1,0:T(8,128)(2,1)} custom-call(bf16[128,8192]{1,0:T(8,128)(2,1)} %q_ref.3, bf16[128,8192]{1,0:T(8,128)(2,1)} %g_ref.3, bf16[128,8192]{1,0:T(8,128)(2,1)} %o_ref.3, f32[64,128]{1,0:T(8,128)} %bitcast.9), custom_call_target="tpu_custom_call" | custom-call | tf_op jit(solution)/shard_map/rows_pack/pallas_call | solution.py:104
  12.0 5.0 %all-to-all-done.1 = bf16[8,128,256]{2,1,0:T(8,128)(2,1)S(1)} async-done(((bf16[8,128,256]{2,1,0:T(8,128)(2,1)}), bf16[8,128,256]{2,1,0:T(8,128)(2,1)S(1)}, u32[]{:S(2)}, u32[]{:S(2)}) %all-to-all-start.1) | async-done | bytes 524320 | tf_op jit(solution)/shard_map/all_to_all | solution.py:460
  17.0 3.8 %all-to-all-start = ((bf16[8,136,1024]{2,1,0:T(8,128)(2,1)}), bf16[8,136,1024]{2,1,0:T(8,128)(2,1)S(1)}, u32[]{:S(2)}, u32[]{:S(2)}) async-start(bf16[8,136,1024]{2,1,0:T(8,128)(2,1)} %rows_pack.2), calls=%async_computation | async-start | bytes 4456448 | tf_op jit(solution)/shard_map/all_to_all | solution.py:460
  20.9 4.3 %rows_pack.3 = bf16[8,136,1024]{2,1,0:T(8,128)(2,1)} custom-call(bf16[128,8192]{1,0:T(8,128)(2,1)} %q_ref.3, bf16[128,8192]{1,0:T(8,128)(2,1)} %g_ref.3, bf16[128,8192]{1,0:T(8,128)(2,1)} %o_ref.3, f32[64,128]{1,0:T(8,128)} %bitcast.10), custom_call_target="tpu_custom_call" | custom-call | tf_op jit(solution)/shard_map/rows_pack/pallas_call | solution.py:104
  25.2 23.3 %all-to-all-done.rows_hbm = bf16[8,136,1024]{2,1,0:T(8,128)(2,1)S(1)} async-done(((bf16[8,136,1024]{2,1,0:T(8,128)(2,1)}), bf16[8,136,1024]{2,1,0:T(8,128)(2,1)S(1)}, u32[]{:S(2)}, u32[]{:S(2)}) %all-to-all-start) | async-done | bytes 2228256 | tf_op jit(solution)/shard_map/all_to_all | solution.py:460
  49.9 3.8 %all-to-all-start.3 = ((bf16[8,136,1024]{2,1,0:T(8,128)(2,1)}), bf16[8,136,1024]{2,1,0:T(8,128)(2,1)S(1)}, u32[]{:S(2)}, u32[]{:S(2)}) async-start(bf16[8,136,1024]{2,1,0:T(8,128)(2,1)} %rows_pack.3), calls=%async_computation.3 | async-start | bytes 4456448 | tf_op jit(solution)/shard_map/all_to_all | solution.py:460
  53.7 3.5 %collective-permute-start = (bf16[768,256]{1,0:T(8,128)(2,1)S(1)}, bf16[768,256]{1,0:T(8,128)(2,1)S(1)}, u32[]{:S(2)}, u32[]{:S(2)}) collective-permute-start(bf16[768,256]{1,0:T(8,128)(2,1)S(1)} %bitcast.8), channel_id=1, source_target_pairs={{0,8},{8,16},{16,24},{24,32},{32,40},{40,48},{48,56},{56,64},{64,7... | collective-permute-start | bytes 1179656 | tf_op jit(solution)/shard_map/ppermute | solution.py:466
  57.2 9.0 %collective-permute-done.rest_2_ = bf16[768,256]{1,0:T(8,128)(2,1)S(1)} collective-permute-done((bf16[768,256]{1,0:T(8,128)(2,1)S(1)}, bf16[768,256]{1,0:T(8,128)(2,1)S(1)}, u32[]{:S(2)}, u32[]{:S(2)}) %collective-permute-start) | collective-permute-done | bytes 393248 | tf_op jit(solution)/shard_map/ppermute | solution.py:466
  66.2 5.6 %collective-permute-start.1 = (bf16[768,256]{1,0:T(8,128)(2,1)S(1)}, bf16[768,256]{1,0:T(8,128)(2,1)}, u32[]{:S(2)}, u32[]{:S(2)}) collective-permute-start(bf16[768,256]{1,0:T(8,128)(2,1)S(1)} %collective-permute-done.rest_2_), channel_id=1, source_target_pairs={{0,8},{8,16},{16,24},{24,32},{32,40},{40,48},{48,56},{56,64},{64,7... | collective-permute-start | bytes 1179656 | tf_op jit(solution)/shard_map/ppermute | solution.py:466
  71.8 1.9 collective-permute-start.2
  73.7 8.3 %collective-permute-done.2.rest_1_ = bf16[256,256]{1,0:T(8,128)(2,1)S(1)} collective-permute-done((bf16[256,256]{1,0:T(8,128)(2,1)S(1)}, bf16[256,256]{1,0:T(8,128)(2,1)S(1)}, u32[]{:S(2)}, u32[]{:S(2)}) %collective-permute-start.2) | collective-permute-done | bytes 131104 | tf_op jit(solution)/shard_map/ppermute | solution.py:466
  82.7 26.3 %shard_map.94 = (bf16[8,128,512]{2,1,0:T(8,128)(2,1)}, f32[2816,256]{1,0:T(8,128)}) custom-call(s32[16]{0:T(128)} %lengths_ref.5, s32[1]{0:T(128)} %bitcast.first_ref, bf16[8,136,1024]{2,1,0:T(8,128)(2,1)} %copy-done.1, bf16[768,256]{1,0:T(8,128)(2,1)} %collective-permute-done.1.rest_0_, bf16[256,256]{1,0:T(8,128)(2,1)} %copy-done.7, ...), custom_call_target="tpu_custom_call" | custom-call | tf_op jit(solution)/shard_map/pallas_call | solution.py:298
  109.0 6.0 %all-to-all-start.2 = ((bf16[8,128,512]{2,1,0:T(8,128)(2,1)}), bf16[8,128,512]{2,1,0:T(8,128)(2,1)S(1)}, u32[]{:S(2)}, u32[]{:S(2)}) async-start(bf16[8,128,512]{2,1,0:T(8,128)(2,1)} %get-tuple-element.20), calls=%async_computation.2 | async-start | bytes 2097152 | tf_op jit(solution)/shard_map/all_to_all | solution.py:460
  115.0 17.4 %shard_map.95 = (f32[4,1024,128]{2,1,0:T(8,128)}, bf16[768,256]{1,0:T(8,128)(2,1)}, bf16[1024,256]{1,0:T(8,128)(2,1)}) custom-call(s32[16]{0:T(128)} %lengths_ref.5, s32[1]{0:T(128)} %bitcast.first_ref, bf16[8,136,1024]{2,1,0:T(8,128)(2,1)} %copy-done, bf16[768,256]{1,0:T(8,128)(2,1)} %collective-permute-done.1.rest_0_, bf16[256,256]{1,0:T(8,128)(2,1)} %copy-done.7, ...), custom_call_target="tpu_custom_call" | custom-call | tf_op jit(solution)/shard_map/pallas_call | solution.py:298
  132.5 13.6 %shard_map.96 = (bf16[8,128,512]{2,1,0:T(8,128)(2,1)}, f32[1024,256]{1,0:T(8,128)}) custom-call(s32[16]{0:T(128)} %lengths_ref.5, s32[1]{0:T(128)} %bitcast.first_ref, bf16[8,136,1024]{2,1,0:T(8,128)(2,1)} %copy-done, bf16[1024,256]{1,0:T(8,128)(2,1)} %bitcast.7, f32[2816,256]{1,0:T(8,128)} %get-tuple-element.21.rest_3_.rest_1_, ...), custom_call_target="tpu_custom_call" | custom-call | tf_op jit(solution)/shard_map/pallas_call | solution.py:298
  146.1 4.8 %all-to-all-start.4 = ((bf16[8,128,512]{2,1,0:T(8,128)(2,1)}), bf16[8,128,512]{2,1,0:T(8,128)(2,1)S(1)}, u32[]{:S(2)}, u32[]{:S(2)}) async-start(bf16[8,128,512]{2,1,0:T(8,128)(2,1)} %get-tuple-element.23), calls=%async_computation.4 | async-start | bytes 2097152 | tf_op jit(solution)/shard_map/all_to_all | solution.py:460
  154.8 18.1 %collective-permute-done.4.back2_hbm = bf16[768,256]{1,0:T(8,128)(2,1)S(1)} collective-permute-done((bf16[768,256]{1,0:T(8,128)(2,1)}, bf16[768,256]{1,0:T(8,128)(2,1)S(1)}, u32[]{:S(2)}, u32[]{:S(2)}) %collective-permute-start.4) | collective-permute-done | bytes 393248 | tf_op jit(solution)/shard_map/ppermute | solution.py:466
  172.9 3.9 %collective-permute-done.3.back1_hbm = bf16[1024,256]{1,0:T(8,128)(2,1)S(1)} collective-permute-done((bf16[1024,256]{1,0:T(8,128)(2,1)S(1)}, bf16[1024,256]{1,0:T(8,128)(2,1)S(1)}, u32[]{:S(2)}, u32[]{:S(2)}) %collective-permute-start.3) | collective-permute-done | bytes 524320 | tf_op jit(solution)/shard_map/ppermute | solution.py:466
  177.6 2.6 %kv_sum.1 = (bf16[128,256]{1,0:T(8,128)(2,1)}, bf16[128,256]{1,0:T(8,128)(2,1)}, bf16[128,256]{1,0:T(8,128)(2,1)}, bf16[128,256]{1,0:T(8,128)(2,1)}, bf16[128,25...) custom-call(s32[1]{0:T(128)} %bitcast.5.member_ref, ...), custom_call_target="tpu_custom_call" | custom-call | tf_op jit(solution)/shard_map/kv_sum/pallas_call | solution.py:355
  181.2 2.3 %collective-permute-start.6 = (bf16[128,256]{1,0:T(8,128)(2,1)}, bf16[128,256]{1,0:T(8,128)(2,1)S(1)}, u32[]{:S(2)}, u32[]{:S(2)}) collective-permute-start(bf16[128,256]{1,0:T(8,128)(2,1)} %get-tuple-element.29), channel_id=1, source_target_pairs={{0,2},{1,3},{2,4},{3,5},{4,6},{5,7},{6,0},{7,1},{8,10},{9,11},{10,... | collective-permute-start | bytes 196616 | tf_op jit(solution)/shard_map/ppermute | solution.py:494
  183.6 2.7 %collective-permute-start.7 = (bf16[128,256]{1,0:T(8,128)(2,1)}, bf16[128,256]{1,0:T(8,128)(2,1)S(1)}, u32[]{:S(2)}, u32[]{:S(2)}) collective-permute-start(bf16[128,256]{1,0:T(8,128)(2,1)} %get-tuple-element.30), channel_id=1, source_target_pairs={{0,3},{1,4},{2,5},{3,6},{4,7},{5,0},{6,1},{7,2},{8,11},{9,12},{10,... | collective-permute-start | bytes 196616 | tf_op jit(solution)/shard_map/ppermute | solution.py:494
  194.9 2.0 kv_unpack.1
  197.9 3.2 %q_unpack.1 = f32[128,8192]{1,0:T(8,128)} custom-call(bf16[8,128,512]{2,1,0:T(8,128)(2,1)} %copy-done.3, bf16[8,128,512]{2,1,0:T(8,128)(2,1)} %copy-done.4), custom_call_target="tpu_custom_call" | custom-call | tf_op jit(solution)/shard_map/q_unpack/pallas_call | solution.py:398
  (55 shorter events, 19.2 us)
Async XLA Ops:
  2.5 14.5 %all-to-all-start.1 = ((bf16[8,128,256]{2,1,0:T(8,128)(2,1)}), bf16[8,128,256]{2,1,0:T(8,128)(2,1)S(1)}, u32[]{:S(2)}, u32[]{:S(2)}) async-start(bf16[8,128,256]{2,1,0:T(8,128)(2,1)} %kv_pack.1), calls=%async_computation.1 | async-start | bytes 1048576 | tf_op jit(solution)/shard_map/all_to_all | solution.py:460
  17.0 54.7 %copy-start.2 = (bf16[8,128,256]{2,1,0:T(8,128)(2,1)}, bf16[8,128,256]{2,1,0:T(8,128)(2,1)S(1)}, u32[]{:S(2)}) copy-start(bf16[8,128,256]{2,1,0:T(8,128)(2,1)S(1)} %all-to-all-done.1) | copy-start | bytes 1572868
  17.0 31.4 %all-to-all-start = ((bf16[8,136,1024]{2,1,0:T(8,128)(2,1)}), bf16[8,136,1024]{2,1,0:T(8,128)(2,1)S(1)}, u32[]{:S(2)}, u32[]{:S(2)}) async-start(bf16[8,136,1024]{2,1,0:T(8,128)(2,1)} %rows_pack.2), calls=%async_computation | async-start | bytes 4456448 | tf_op jit(solution)/shard_map/all_to_all | solution.py:460
  49.9 59.1 %all-to-all-start.3 = ((bf16[8,136,1024]{2,1,0:T(8,128)(2,1)}), bf16[8,136,1024]{2,1,0:T(8,128)(2,1)S(1)}, u32[]{:S(2)}, u32[]{:S(2)}) async-start(bf16[8,136,1024]{2,1,0:T(8,128)(2,1)} %rows_pack.3), calls=%async_computation.3 | async-start | bytes 4456448 | tf_op jit(solution)/shard_map/all_to_all | solution.py:460
  53.7 12.5 %collective-permute-start = (bf16[768,256]{1,0:T(8,128)(2,1)S(1)}, bf16[768,256]{1,0:T(8,128)(2,1)S(1)}, u32[]{:S(2)}, u32[]{:S(2)}) collective-permute-start(bf16[768,256]{1,0:T(8,128)(2,1)S(1)} %bitcast.8), channel_id=1, source_target_pairs={{0,8},{8,16},{16,24},{24,32},{32,40},{40,48},{48,56},{56,64},{64,7... | collective-permute-start | bytes 1179656 | tf_op jit(solution)/shard_map/ppermute | solution.py:466
  66.2 15.9 %copy-start.5 = (bf16[768,256]{1,0:T(8,128)(2,1)}, bf16[768,256]{1,0:T(8,128)(2,1)S(1)}, u32[]{:S(2)}) copy-start(bf16[768,256]{1,0:T(8,128)(2,1)S(1)} %collective-permute-done.rest_2_) | copy-start | bytes 1179652
  66.2 15.9 %collective-permute-start.1 = (bf16[768,256]{1,0:T(8,128)(2,1)S(1)}, bf16[768,256]{1,0:T(8,128)(2,1)}, u32[]{:S(2)}, u32[]{:S(2)}) collective-permute-start(bf16[768,256]{1,0:T(8,128)(2,1)S(1)} %collective-permute-done.rest_2_), channel_id=1, source_target_pairs={{0,8},{8,16},{16,24},{24,32},{32,40},{40,48},{48,56},{56,64},{64,7... | collective-permute-start | bytes 1179656 | tf_op jit(solution)/shard_map/ppermute | solution.py:466
  71.8 10.3 %collective-permute-start.2 = (bf16[256,256]{1,0:T(8,128)(2,1)S(1)}, bf16[256,256]{1,0:T(8,128)(2,1)S(1)}, u32[]{:S(2)}, u32[]{:S(2)}) collective-permute-start(bf16[256,256]{1,0:T(8,128)(2,1)S(1)} %bitcast.11), channel_id=1, source_target_pairs={{0,8},{8,16},{16,24},{24,32},{32,40},{40,48},{48,56},{56,64},{64,7... | collective-permute-start | bytes 393224 | tf_op jit(solution)/shard_map/ppermute | solution.py:466
  109.0 6.0 %copy-start = (bf16[8,136,1024]{2,1,0:T(8,128)(2,1)}, bf16[8,136,1024]{2,1,0:T(8,128)(2,1)S(1)}, u32[]{:S(2)}) copy-start(bf16[8,136,1024]{2,1,0:T(8,128)(2,1)S(1)} %all-to-all-done.3.rows_hbm) | copy-start | bytes 6684676
  109.0 37.0 %all-to-all-start.2 = ((bf16[8,128,512]{2,1,0:T(8,128)(2,1)}), bf16[8,128,512]{2,1,0:T(8,128)(2,1)S(1)}, u32[]{:S(2)}, u32[]{:S(2)}) async-start(bf16[8,128,512]{2,1,0:T(8,128)(2,1)} %get-tuple-element.20), calls=%async_computation.2 | async-start | bytes 2097152 | tf_op jit(solution)/shard_map/all_to_all | solution.py:460
  132.4 18.5 %copy-start.16 = (bf16[1024,256]{1,0:T(8,128)(2,1)S(1)}, bf16[1024,256]{1,0:T(8,128)(2,1)}, u32[]{:S(2)}) copy-start(bf16[1024,256]{1,0:T(8,128)(2,1)} %get-tuple-element.25) | copy-start | bytes 1572868
  146.1 50.8 %copy-start.3 = (bf16[8,128,512]{2,1,0:T(8,128)(2,1)}, bf16[8,128,512]{2,1,0:T(8,128)(2,1)S(1)}, u32[]{:S(2)}) copy-start(bf16[8,128,512]{2,1,0:T(8,128)(2,1)S(1)} %all-to-all-done.2.refs_0_) | copy-start | bytes 3145732
  146.1 50.8 %all-to-all-start.4 = ((bf16[8,128,512]{2,1,0:T(8,128)(2,1)}), bf16[8,128,512]{2,1,0:T(8,128)(2,1)S(1)}, u32[]{:S(2)}, u32[]{:S(2)}) async-start(bf16[8,128,512]{2,1,0:T(8,128)(2,1)} %get-tuple-element.23), calls=%async_computation.4 | async-start | bytes 2097152 | tf_op jit(solution)/shard_map/all_to_all | solution.py:460
  150.9 25.9 %collective-permute-start.3 = (bf16[1024,256]{1,0:T(8,128)(2,1)S(1)}, bf16[1024,256]{1,0:T(8,128)(2,1)S(1)}, u32[]{:S(2)}, u32[]{:S(2)}) collective-permute-start(bf16[1024,256]{1,0:T(8,128)(2,1)S(1)} %copy-done.16), channel_id=1, source_target_pairs={{8,0},{16,8},{24,16},{32,24},{40,32},{48,40},{56,48},{64,56},{72,6... | collective-permute-start | bytes 1572872 | tf_op jit(solution)/shard_map/ppermute | solution.py:466
  152.8 20.1 %collective-permute-start.4 = (bf16[768,256]{1,0:T(8,128)(2,1)}, bf16[768,256]{1,0:T(8,128)(2,1)S(1)}, u32[]{:S(2)}, u32[]{:S(2)}) collective-permute-start(bf16[768,256]{1,0:T(8,128)(2,1)} %get-tuple-element.26), channel_id=1, source_target_pairs={{16,0},{24,8},{32,16},{40,24},{48,32},{56,40},{64,48},{72,56},{80,... | collective-permute-start | bytes 1179656 | tf_op jit(solution)/shard_map/ppermute | solution.py:466
  180.2 7.1 %collective-permute-start.5 = (bf16[128,256]{1,0:T(8,128)(2,1)}, bf16[128,256]{1,0:T(8,128)(2,1)S(1)}, u32[]{:S(2)}, u32[]{:S(2)}) collective-permute-start(bf16[128,256]{1,0:T(8,128)(2,1)} %get-tuple-element.28), channel_id=1, source_target_pairs={{0,1},{1,2},{2,3},{3,4},{4,5},{5,6},{6,7},{7,0},{8,9},{9,10},{10,1... | collective-permute-start | bytes 196616 | tf_op jit(solution)/shard_map/ppermute | solution.py:494
  181.2 7.4 %collective-permute-start.6 = (bf16[128,256]{1,0:T(8,128)(2,1)}, bf16[128,256]{1,0:T(8,128)(2,1)S(1)}, u32[]{:S(2)}, u32[]{:S(2)}) collective-permute-start(bf16[128,256]{1,0:T(8,128)(2,1)} %get-tuple-element.29), channel_id=1, source_target_pairs={{0,2},{1,3},{2,4},{3,5},{4,6},{5,7},{6,0},{7,1},{8,10},{9,11},{10,... | collective-permute-start | bytes 196616 | tf_op jit(solution)/shard_map/ppermute | solution.py:494
  183.6 6.4 %collective-permute-start.7 = (bf16[128,256]{1,0:T(8,128)(2,1)}, bf16[128,256]{1,0:T(8,128)(2,1)S(1)}, u32[]{:S(2)}, u32[]{:S(2)}) collective-permute-start(bf16[128,256]{1,0:T(8,128)(2,1)} %get-tuple-element.30), channel_id=1, source_target_pairs={{0,3},{1,4},{2,5},{3,6},{4,7},{5,0},{6,1},{7,2},{8,11},{9,12},{10,... | collective-permute-start | bytes 196616 | tf_op jit(solution)/shard_map/ppermute | solution.py:494
  186.3 3.7 %collective-permute-start.8 = (bf16[128,256]{1,0:T(8,128)(2,1)}, bf16[128,256]{1,0:T(8,128)(2,1)S(1)}, u32[]{:S(2)}, u32[]{:S(2)}) collective-permute-start(bf16[128,256]{1,0:T(8,128)(2,1)} %get-tuple-element.31), channel_id=1, source_target_pairs={{0,4},{1,5},{2,6},{3,7},{4,0},{5,1},{6,2},{7,3},{8,12},{9,13},{10,... | collective-permute-start | bytes 196616 | tf_op jit(solution)/shard_map/ppermute | solution.py:494
  186.3 4.5 %collective-permute-start.9 = (bf16[128,256]{1,0:T(8,128)(2,1)}, bf16[128,256]{1,0:T(8,128)(2,1)S(1)}, u32[]{:S(2)}, u32[]{:S(2)}) collective-permute-start(bf16[128,256]{1,0:T(8,128)(2,1)} %get-tuple-element.32), channel_id=1, source_target_pairs={{0,5},{1,6},{2,7},{3,0},{4,1},{5,2},{6,3},{7,4},{8,13},{9,14},{10,... | collective-permute-start | bytes 196616 | tf_op jit(solution)/shard_map/ppermute | solution.py:494
  187.2 7.0 %copy-start.9 = (bf16[128,256]{1,0:T(8,128)(2,1)}, bf16[128,256]{1,0:T(8,128)(2,1)S(1)}, u32[]{:S(2)}) copy-start(bf16[128,256]{1,0:T(8,128)(2,1)S(1)} %collective-permute-done.5.rest_1_) | copy-start | bytes 196612
  187.2 5.4 %collective-permute-start.10 = (bf16[128,256]{1,0:T(8,128)(2,1)}, bf16[128,256]{1,0:T(8,128)(2,1)S(1)}, u32[]{:S(2)}, u32[]{:S(2)}) collective-permute-start(bf16[128,256]{1,0:T(8,128)(2,1)} %get-tuple-element.33), channel_id=1, source_target_pairs={{0,6},{1,7},{2,0},{3,1},{4,2},{5,3},{6,4},{7,5},{8,14},{9,15},{10,... | collective-permute-start | bytes 196616 | tf_op jit(solution)/shard_map/ppermute | solution.py:494
  188.7 5.6 %copy-start.10 = (bf16[128,256]{1,0:T(8,128)(2,1)}, bf16[128,256]{1,0:T(8,128)(2,1)S(1)}, u32[]{:S(2)}) copy-start(bf16[128,256]{1,0:T(8,128)(2,1)S(1)} %collective-permute-done.6.rest_2_) | copy-start | bytes 196612
  188.7 5.6 %collective-permute-start.11 = (bf16[128,256]{1,0:T(8,128)(2,1)}, bf16[128,256]{1,0:T(8,128)(2,1)S(1)}, u32[]{:S(2)}, u32[]{:S(2)}) collective-permute-start(bf16[128,256]{1,0:T(8,128)(2,1)} %get-tuple-element.34), channel_id=1, source_target_pairs={{0,7},{1,0},{2,1},{3,2},{4,3},{5,4},{6,5},{7,6},{8,15},{9,8},{10,9... | collective-permute-start | bytes 196616 | tf_op jit(solution)/shard_map/ppermute | solution.py:494
  (10 other events, 22.1 us)
